TPU v7x, 32 devices: a whole 2x2x4 slice. The times are simulated.
32 devices in a mesh: trait: 2 (over x), ppl: 16 (over z, y, core).
Axes of the slice: x: 2, y: 2, z: 4, core: 2. Of those that a mesh axis runs over, the one named last changes fastest.
Arguments:
- genotypes: bfloat16 [8192, 4096], P(('trait', 'ppl')), parts along dimension 0
- residual: float32 [64, 4096], P('trait', 'ppl'), parts along dimension 0, may hold values from -36 to 36
- noise_people: float32 [64, 4096], P('trait', 'ppl'), parts along dimension 0, may hold values from -6 to 6
- noise_coef: float32 [64, 4096], P('trait'), parts along dimension 0, may hold values from -6 to 6
- coef_all: float32 [64, 8192], P('trait'), parts along dimension 0, may hold values from -0.06 to 0.06
- block_index: int32 [2], P('trait'), parts along dimension 0, may hold values from 0 to 1
- prior_prec: float32 [64], P('trait'), parts along dimension 0, may hold values from 21 to 103
- sigma2_old: float32 [64], P('trait'), parts along dimension 0, may hold values from 0.5 to 2
- gamma_draw: float32 [64], P('trait'), parts along dimension 0, may hold values from 0.8 to 1.25
- valid_counts: int32 [32], P('trait'), parts along dimension 0, may hold values from 128 to 256, as said below
Outputs:
- coef_new: float32 [64, 8192], P('trait'), parts along dimension 0
- residual_new: float32 [64, 4096], P('trait', 'ppl'), parts along dimension 0
- sigma2_new: float32 [64], P('trait'), parts along dimension 0
There are 2 independent parts, one for each index of `trait`. A program takes and returns all parts, laid end to end along the dimension named above; each array names one. Nothing has to cross between parts.
Inputs may be any that keep to these rules, and one draw needn't show every extreme that they name: `valid_counts`: each entry counts the people present in one device's 256 slots; they fill the lowest slots, and some entry equals 256.
All inputs are finite; a program needn't handle non-finite values.
Results may differ from a plain program's by a relative error of at most 0.0049.
Values may be sent and summed in bfloat16 or wider, within the bound.
No kernel may reach another device: no remote copies, remote signals or barrier semaphores. Data moves between devices by JAX's collectives and lax.ppermute only.
A program may use at most 64 MiB of HBM per device.

v0:
```python
import jax
import jax.numpy as jnp
from jax import lax
from jax.sharding import PartitionSpec as P

ITERS = 4


PRIOR_DOF = 4.0
PRIOR_SCALE = 0.5
CONTRACT = (((1,), (1,)), ((), ()))


def per_device(
    genotypes,
    residual,
    noise_people,
    noise_coef,
    coef_all,
    block_index,
    prior_prec,
    sigma2_old,
    gamma_draw,
    valid_counts,
):
    row_count = genotypes.shape[0]
    batch_width = genotypes.shape[1]
    my_shard = lax.axis_index("ppl")
    person_mask = (jnp.arange(row_count) < valid_counts[my_shard]).astype(jnp.float32)[None, :]
    first_col = block_index[0] * batch_width
    old_coef = lax.dynamic_slice_in_dim(coef_all, first_col, batch_width, 1)
    fitted_old = lax.dot_general(
        old_coef.astype(jnp.bfloat16), genotypes, CONTRACT, preferred_element_type=jnp.float32
    )
    partial_res = person_mask * (residual + fitted_old)
    noise_var = sigma2_old[:, None]
    ridge = prior_prec[:, None]
    target = (person_mask * (partial_res + jnp.sqrt(noise_var) * noise_people)).astype(jnp.bfloat16)
    data_part = jnp.dot(target, genotypes, preferred_element_type=jnp.float32)
    fitted = jnp.zeros_like(partial_res)
    rhs = lax.psum(data_part, "ppl") / noise_var + jnp.sqrt(ridge) * noise_coef
    batch_coef = jnp.zeros_like(rhs)
    search = rhs
    direction = rhs
    norm_now = jnp.sum(search * search, axis=1)
    for number in range(ITERS):
        dir_low = direction.astype(jnp.bfloat16)
        dir_full = lax.optimization_barrier(dir_low).astype(jnp.float32)
        image = person_mask * lax.dot_general(
            dir_low, genotypes, CONTRACT, preferred_element_type=jnp.float32
        )
        local_sum = jnp.dot(
            image.astype(jnp.bfloat16), genotypes, preferred_element_type=jnp.float32
        )
        local_sum = lax.psum(local_sum, "ppl")
        applied = local_sum / noise_var + ridge * dir_full
        step_size = norm_now / jnp.sum(dir_full * applied, axis=1)
        batch_coef = batch_coef + step_size[:, None] * dir_full
        fitted = fitted + step_size[:, None] * image
        search = search - step_size[:, None] * applied
        norm_next = jnp.sum(search * search, axis=1)
        direction = search + (norm_next / norm_now)[:, None] * direction
        norm_now = norm_next
    residual_new = partial_res - fitted
    squares = lax.psum(jnp.sum(residual_new * residual_new, axis=1), "ppl")
    present = jnp.sum(valid_counts).astype(jnp.float32)
    sigma2_new = (squares + PRIOR_DOF * PRIOR_SCALE) / ((present + PRIOR_DOF) * gamma_draw)
    coef_new = lax.dynamic_update_slice_in_dim(coef_all, batch_coef, first_col, 1)
    return (coef_new, residual_new, sigma2_new)


def solution(mesh):
    return jax.shard_map(
        per_device,
        mesh=mesh,
        in_specs=(
            P(("trait", "ppl"), None),
            P("trait", "ppl"),
            P("trait", "ppl"),
            P("trait", None),
            P("trait", None),
            P("trait"),
            P("trait"),
            P("trait"),
            P("trait"),
            P("trait"),
        ),
        out_specs=(P("trait", None), P("trait", "ppl"), P("trait")),
        check_vma=False,
    )
```

profile of v0, /device:TPU:0, one launch (start us, length us, event | category | flops | bytes accessed | tf_op | source)
XLA Modules:
  0.0 537.2 jit_solution(11827598137406431919)
XLA Ops:
  7.3 1.4 copy.21
  10.6 0.7 fusion
  11.4 1.3 fusion.14
  12.8 93.5 %all-reduce.6.cloned.1.call-done = f32[32,4096]{1,0:T(8,128)} async-done(((f32[32,4096]{1,0:T(8,128)}), f32[32,4096]{1,0:T(8,128)}) %all-reduce.6.cloned.1.call-update) | async-done | bytes 524304 | tf_op jit(solution)/shard_map/psum | solution.py:41
  106.3 1.5 multiply_reduce_fusion.3
  107.8 0.7 convolution_multiply_fusion.3
  108.5 1.3 fusion.21
  109.9 91.3 %all-reduce.8.cloned.1.call-done = f32[32,4096]{1,0:T(8,128)} async-done(((f32[32,4096]{1,0:T(8,128)}), f32[32,4096]{1,0:T(8,128)}) %all-reduce.8.cloned.1.call-update) | async-done | bytes 524304 | tf_op jit(solution)/shard_map/psum | solution.py:55
  201.2 1.3 fusion.2
  202.5 1.4 multiply_reduce_fusion.2
  203.9 0.8 copy-done.1
  204.8 0.7 convolution_multiply_fusion.2
  205.6 1.3 fusion.19
  206.9 91.3 %all-reduce.10.cloned.1.call-done = f32[32,4096]{1,0:T(8,128)} async-done(((f32[32,4096]{1,0:T(8,128)}), f32[32,4096]{1,0:T(8,128)}) %all-reduce.10.cloned.1.call-update) | async-done | bytes 524304 | tf_op jit(solution)/shard_map/psum | solution.py:55
  298.2 1.3 fusion.8
  299.6 1.5 multiply_reduce_fusion.1
  301.1 2.0 fusion.26
  303.1 0.7 convolution_multiply_fusion.1
  303.9 1.3 fusion.17
  305.3 91.3 %all-reduce.12.cloned.1.call-done = f32[32,4096]{1,0:T(8,128)} async-done(((f32[32,4096]{1,0:T(8,128)}), f32[32,4096]{1,0:T(8,128)}) %all-reduce.12.cloned.1.call-update) | async-done | bytes 524304 | tf_op jit(solution)/shard_map/psum | solution.py:55
  396.5 1.4 fusion.10
  397.9 0.7 div.93
  398.6 1.4 multiply_reduce_fusion
  400.0 0.7 div.94
  400.9 0.7 copy-done.7
  401.6 0.7 convolution_multiply_fusion
  402.4 1.3 fusion.15
  405.0 90.0 %all-reduce.14.cloned.1.call-done = f32[32,4096]{1,0:T(8,128)} async-done(((f32[32,4096]{1,0:T(8,128)}), f32[32,4096]{1,0:T(8,128)}) %all-reduce.14.cloned.1.call-update) | async-done | bytes 524304 | tf_op jit(solution)/shard_map/psum | solution.py:55
  495.1 1.3 fusion.12
  496.5 1.1 fusion.6
  497.5 0.8 multiply_reduce_fusion.4
  498.3 31.9 %psum.47 = f32[32]{0:T(128)S(1)} all-reduce(f32[32]{0:T(128)S(1)} %get-tuple-element.3), channel_id=1, replica_groups=mesh['trait'=2,'ppl'=16] {'ppl'}, use_global_device_ids=true, to_apply=%region_14.0 | all-reduce | flops 32 | bytes 256 | tf_op jit(solution)/shard_map/psum | solution.py:65
  (72 shorter events, 3.2 us)
Async XLA Ops:
  7.2 3.4 copy-start
  7.2 3.4 copy-start.12
  7.2 4.1 copy-start.13
  7.2 3.3 copy-start.11
  7.2 2.1 copy-start.23
  7.2 99.1 %all-reduce.6.cloned.1.call-start = ((), (), s32[]{:S(2)}) async-start(), calls=%async_computation | async-start | bytes 1048576 | tf_op jit(solution)/shard_map/psum | solution.py:41
  8.6 4.1 copy-start.10
  11.3 1.4 copy-start.14
  12.7 188.5 %all-reduce.8.cloned.1.call-start = ((), (), s32[]{:S(2)}) async-start(), calls=%async_computation.1 | async-start | bytes 1048576 | tf_op jit(solution)/shard_map/psum | solution.py:55
  107.8 94.7 %copy-start.2 = (bf16[32,4096]{1,0:T(8,128)(2,1)}, bf16[32,4096]{1,0:T(8,128)(2,1)S(1)}, u32[]{:S(2)}) copy-start(bf16[32,4096]{1,0:T(8,128)(2,1)S(1)} %convert_element_type.55) | copy-start | bytes 786436
  109.8 188.4 %all-reduce.10.cloned.1.call-start = ((), (), s32[]{:S(2)}) async-start(), calls=%async_computation.2 | async-start | bytes 1048576 | tf_op jit(solution)/shard_map/psum | solution.py:55
  202.5 1.4 copy-start.15
  203.9 0.8 copy-start.1
  204.8 94.7 %copy-start.4 = (bf16[32,4096]{1,0:T(8,128)(2,1)}, bf16[32,4096]{1,0:T(8,128)(2,1)S(1)}, u32[]{:S(2)}) copy-start(bf16[32,4096]{1,0:T(8,128)(2,1)S(1)} %fusion.13) | copy-start | bytes 786436
  206.9 189.6 %all-reduce.12.cloned.1.call-start = ((), (), s32[]{:S(2)}) async-start(), calls=%async_computation.3 | async-start | bytes 1048576 | tf_op jit(solution)/shard_map/psum | solution.py:55
  299.6 3.6 copy-start.17
  301.1 2.0 copy-start.21
  303.9 96.8 %copy-start.9 = (f32[32,4096]{1,0:T(8,128)S(1)}, f32[32,4096]{1,0:T(8,128)}, u32[]{:S(2)}) copy-start(f32[32,4096]{1,0:T(8,128)} %get-tuple-element.6) | copy-start | bytes 1572868
  305.2 189.9 %all-reduce.14.cloned.1.call-start = ((), (), s32[]{:S(2)}) async-start(), calls=%async_computation.4 | async-start | bytes 1048576 | tf_op jit(solution)/shard_map/psum | solution.py:55
  396.5 4.1 copy-start.6
  400.0 0.7 copy-start.19
  400.9 0.7 copy-start.7
  402.3 1.4 copy-start.24
  402.4 92.7 %copy-start.8 = (bf16[32,4096]{1,0:T(8,128)(2,1)S(1)}, bf16[32,4096]{1,0:T(8,128)(2,1)}, u32[]{:S(2)}) copy-start(bf16[32,4096]{1,0:T(8,128)(2,1)} %copy-done.7) | copy-start | bytes 786436
  402.4 94.0 %copy-start.20 = (f32[32]{0:T(128)S(1)}, f32[32]{0:T(128)}, u32[]{:S(2)}) copy-start(f32[32]{0:T(128)} %copy-done.19) | copy-start | bytes 388
  402.4 94.0 %copy-start.3 = (bf16[32,4096]{1,0:T(8,128)(2,1)S(1)}, bf16[32,4096]{1,0:T(8,128)(2,1)}, u32[]{:S(2)}) copy-start(bf16[32,4096]{1,0:T(8,128)(2,1)} %copy-done.2) | copy-start | bytes 786436
  402.4 94.0 %copy-start.5 = (bf16[32,4096]{1,0:T(8,128)(2,1)S(1)}, bf16[32,4096]{1,0:T(8,128)(2,1)}, u32[]{:S(2)}) copy-start(bf16[32,4096]{1,0:T(8,128)(2,1)} %copy-done.4) | copy-start | bytes 786436
  402.4 94.0 %copy-start.16 = (f32[32]{0:T(128)S(1)}, f32[32]{0:T(128)}, u32[]{:S(2)}) copy-start(f32[32]{0:T(128)} %copy-done.15) | copy-start | bytes 388
  402.4 94.0 %copy-start.18 = (f32[32]{0:T(128)S(1)}, f32[32]{0:T(128)}, u32[]{:S(2)}) copy-start(f32[32]{0:T(128)} %copy-done.17) | copy-start | bytes 388
  403.7 126.5 %copy-start.22 = (f32[32]{0:T(128)S(1)}, f32[32]{0:T(128)}, u32[]{:S(2)}) copy-start(f32[32]{0:T(128)} %param.18) | copy-start | bytes 388
Sparse Core Ops, SparseCore 0:
  12.8 93.4 all-reduce.5
  110.0 91.1 all-reduce.7
  207.0 91.1 all-reduce.9
  305.3 91.1 all-reduce.11
  403.8 91.1 all-reduce.13
where the time goes:
time: 538 us; the launch traced here: 537 us
  waiting for transfers between devices  457 us (85%)
  blocking collectives  31.9 us (6%)
  other arithmetic  18.5 us (3%)
  between operations  15.5 us (3%)
  matrix products  10.1 us (2%)
    psum x4, waiting for transfers between devices, per_device(): local_sum = lax.psum(local_sum, 'ppl')  364 us
    psum x1, waiting for transfers between devices, per_device(): rhs = lax.psum(data_part, 'ppl') / noise_var + jnp.sqrt(ridge) * noise_coef  93.5 us
    psum x1, blocking collectives, per_device(): squares = lax.psum(jnp.sum(residual_new * residual_new, axis=1), 'ppl')  31.9 us
  transfers between devices with their start and end apart: 5, of which 5 were waited for; matrix products, arithmetic and copies ran while one was open for 0% of the time, Pallas kernels for 0%

commit v1 on v0

v1 whole, which is shorter than its diff:
```python
import functools

import jax
import jax.numpy as jnp
from jax import lax
from jax.sharding import PartitionSpec as P

ITERS = 4
PRIOR_DOF = 4.0
PRIOR_SCALE = 0.5
CONTRACT = (((1,), (1,)), ((), ()))
LANES = 128
F32, BF16 = jnp.float32, jnp.bfloat16


def swap(x, count, distance):
    return lax.ppermute(x, "ppl", [(i, i ^ distance) for i in range(count)])


def to_parts(value):
    first = lax.reduce_precision(value, 8, 7)
    second = lax.reduce_precision(value - first, 8, 7)
    third = value - first - second
    parts = jnp.concatenate([first, second, third], axis=1).astype(BF16)
    return jnp.pad(parts, ((0, 0), (0, LANES - 3)))


def from_parts(parts):
    wide = parts.astype(F32)
    return (wide[:, 2:3] + wide[:, 1:2]) + wide[:, 0:1]


def per_device(
    count,
    genotypes,
    residual,
    noise_people,
    noise_coef,
    coef_all,
    block_index,
    prior_prec,
    sigma2_old,
    gamma_draw,
    valid_counts,
):
    rows, width = genotypes.shape
    bits = count.bit_length() - 1
    top = bits - 2
    me = lax.axis_index("ppl")
    core, place = me & 1, me >> top
    half = width // 2
    chunk = half // 4
    chips = range(1, top)
    dot_t = functools.partial(lax.dot_general, dimension_numbers=CONTRACT, preferred_element_type=F32)
    dot = functools.partial(jnp.dot, preferred_element_type=F32)

    def columns(array, side, slot):
        return lax.dynamic_slice_in_dim(array, side * half + (place ^ slot) * chunk, chunk, 1)

    x_own = jnp.concatenate([columns(genotypes, core, t) for t in range(4)], axis=1)
    x_give = jnp.concatenate([columns(genotypes, 1 - core, t) for t in range(4)], axis=1)
    x_far = swap(x_give, count, 1)

    slots = jnp.arange(rows)
    mask_own = (slots < valid_counts[me]).astype(F32)[None, :]
    mask_far = (slots < valid_counts[me ^ 1]).astype(F32)[None, :]
    first_col = block_index[0] * width
    noise_var = sigma2_old[:, None]
    ridge = prior_prec[:, None]

    def over_people(data, extra, kind):
        if extra is not None:
            tail = to_parts(extra) if kind == BF16 else jnp.broadcast_to(extra, (extra.shape[0], LANES))
        pieces = []
        for t in range(4):
            piece = data[:, t * chunk : (t + 1) * chunk].astype(kind)
            pieces.append(piece if extra is None else jnp.concatenate([piece, tail], axis=1))
        got = [pieces[0]] + [swap(pieces[t], count, t << top) for t in (1, 2, 3)]
        body = [g[:, :chunk].astype(F32) for g in got]
        total = (body[0] + body[1]) + (body[2] + body[3])
        if extra is not None:
            tails = [from_parts(g[:, chunk:]) if kind == BF16 else g[:, chunk : chunk + 1] for g in got]
            scalar = (tails[0] + tails[1]) + (tails[2] + tails[3])
            total = jnp.concatenate([total, jnp.broadcast_to(scalar, (scalar.shape[0], LANES))], axis=1)
        for bit in chips:
            total = total + swap(total, count, 1 << bit)
        return total

    old_coef = lax.dynamic_slice_in_dim(coef_all, first_col, width, 1)
    fitted_old = dot_t(old_coef.astype(BF16), genotypes)
    partial_res = mask_own * (residual + fitted_old)
    target = (mask_own * (partial_res + jnp.sqrt(noise_var) * noise_people)).astype(BF16)
    target_far = swap(target, count, 1)
    data = over_people(dot(target, x_own) + dot(target_far, x_far), None, F32)
    search = data / noise_var + jnp.sqrt(ridge) * columns(noise_coef, core, 0)

    image_own = image_far = jnp.zeros_like(partial_res)
    fitted = jnp.zeros_like(partial_res)
    direction = jnp.zeros((search.shape[0], half), F32)
    batch_half = direction
    norm_now = length = None
    for number in range(ITERS):
        low = search.astype(BF16)
        packed = jnp.concatenate([low, to_parts(jnp.sum(search * search, axis=1, keepdims=True))], axis=1)
        got = [packed] + [swap(packed, count, t << top) for t in (1, 2, 3)]
        low = jnp.concatenate([g[:, :chunk] for g in got], axis=1)
        norms = [from_parts(g[:, chunk:]) for g in got]
        norm_half = (norms[0] + norms[1]) + (norms[2] + norms[3])
        wide = low.astype(F32)
        sums = [norm_half, jnp.sum(wide * wide, axis=1, keepdims=True), jnp.sum(wide * direction, axis=1, keepdims=True)]
        part_own, part_far = dot_t(low, x_own), dot_t(low, x_far)
        sent = jnp.concatenate([part_own, part_far, jnp.pad(jnp.concatenate(sums, axis=1), ((0, 0), (0, LANES - 3)))], axis=1)
        back = swap(sent, count, 1)
        tail = sent[:, 2 * rows :] + back[:, 2 * rows :]
        norm_next, low_low, low_dir = tail[:, 0:1], tail[:, 1:2], tail[:, 2:3]
        image_own_new = mask_own * (part_own + back[:, rows : 2 * rows])
        image_far_new = mask_far * (part_far + back[:, :rows])
        if number == 0:
            direction, length = wide, low_low
            image_own, image_far = image_own_new, image_far_new
        else:
            beta = norm_next / norm_now
            direction = wide + beta * direction
            length = low_low + beta * (2.0 * low_dir + beta * length)
            image_own = image_own_new + beta * image_own
            image_far = image_far_new + beta * image_far
        norm_now = norm_next
        rounded_own, rounded_far = image_own.astype(BF16), image_far.astype(BF16)
        energy_own = jnp.sum(image_own * rounded_own.astype(F32), axis=1, keepdims=True)
        if number == ITERS - 1:
            break
        energy = energy_own + jnp.sum(image_far * rounded_far.astype(F32), axis=1, keepdims=True)
        sum_people = over_people(dot(rounded_own, x_own) + dot(rounded_far, x_far), energy, F32 if number == 0 else BF16)
        step = norm_now / (sum_people[:, chunk : chunk + 1] / noise_var + ridge * length)
        search = search - step * (sum_people[:, :chunk] / noise_var + ridge * direction[:, :chunk])
        batch_half = batch_half + step * direction
        fitted = fitted + step * image_own

    before = partial_res - fitted
    tails = [energy_own]
    tails += [jnp.sum(a * b, axis=1, keepdims=True) for a, b in ((before, before), (before, image_own), (image_own, image_own))]
    total = jnp.pad(jnp.concatenate(tails, axis=1), ((0, 0), (0, LANES - 4)))
    for bit in range(top):
        total = total + swap(total, count, 1 << bit)
    got = [total] + [swap(total, count, t << top) for t in (1, 2, 3)]
    total = (got[0] + got[1]) + (got[2] + got[3])
    step = norm_now / (total[:, 0:1] / noise_var + ridge * length)
    residual_new = before - step * image_own
    squares = total[:, 1] - step[:, 0] * (2.0 * total[:, 2] - step[:, 0] * total[:, 3])
    present = jnp.sum(valid_counts).astype(F32)
    sigma2_new = (squares + PRIOR_DOF * PRIOR_SCALE) / ((present + PRIOR_DOF) * gamma_draw)
    pair = jnp.concatenate([batch_half, direction], axis=1)
    pair_far = swap(pair, count, 1)
    coef_new = coef_all
    for side, both in ((core, pair), (1 - core, pair_far)):
        done = both[:, :half] + step * both[:, half:]
        for t in range(4):
            where = first_col + side * half + (place ^ t) * chunk
            coef_new = lax.dynamic_update_slice_in_dim(coef_new, done[:, t * chunk : (t + 1) * chunk], where, 1)
    return (coef_new, residual_new, sigma2_new)


def solution(mesh):
    return jax.shard_map(
        functools.partial(per_device, mesh.shape["ppl"]),
        mesh=mesh,
        in_specs=(
            P(("trait", "ppl"), None),
            P("trait", "ppl"),
            P("trait", "ppl"),
            P("trait", None),
            P("trait", None),
            P("trait"),
            P("trait"),
            P("trait"),
            P("trait"),
            P("trait"),
        ),
        out_specs=(P("trait", None), P("trait", "ppl"), P("trait")),
        check_vma=False,
    )
```

time: 538 us -> 136 us (0.25)
  waiting for transfers between devices: 457 us -> 50.1 us
  starting transfers between devices: 0.21 us -> 49.7 us
  blocking collectives: 31.9 us -> 0 us
  between operations: 15.5 us -> 2.61 us
  local copies, waits for them, and re-layouts: 3.54 us -> 10.7 us
    psum x5 -> x0, waiting for transfers between devices: 457 us -> none  [the longest x4 364 us: per_device(): local_sum = lax.psum(local_sum, 'ppl')]
    ppermute x0 -> x40, waiting for transfers between devices: none -> 50.1 us  [swap(): return lax.ppermute(x, 'ppl', [(i, i ^ distance) for i in range(count)])]
    ppermute x0 -> x40, starting transfers between devices: none -> 49.7 us  [swap(): return lax.ppermute(x, 'ppl', [(i, i ^ distance) for i in range(count)])]
    psum x1 -> x0, blocking collectives: 31.9 us -> none  [per_device(): squares = lax.psum(jnp.sum(residual_new * residual_new, axis=1), 'ppl')]
    reduce_sum x10 -> x13, other arithmetic: 12.5 us -> 2.55 us  [the longest x4 0.72 us: per_device(): jnp.sum(wide * wide, axis=1, keepdims=True)]
  transfers between devices with their start and end apart: 5 -> 40, of which waited for: 5 -> 28; matrix products, arithmetic and copies ran while one was open for 0% -> 8% of each run, Pallas kernels for 0% -> 0%
where the time goes in v1:
time: 136 us
  waiting for transfers between devices  50.1 us (37%)
  starting transfers between devices  49.7 us (37%)
  other arithmetic  14.6 us (11%)
  local copies, waits for them, and re-layouts  10.7 us (8%)
  matrix products  7.95 us (6%)
  between operations  2.61 us (2%)
    ppermute x40, waiting for transfers between devices, swap(): return lax.ppermute(x, 'ppl', [(i, i ^ distance) for i in range(count)])  50.1 us
    ppermute x40, starting transfers between devices, swap(): return lax.ppermute(x, 'ppl', [(i, i ^ distance) for i in range(count)])  49.7 us
    dynamic_update_slice x8, local copies, waits for them, and re-layouts, per_device(): lax.dynamic_update_slice_in_dim(coef_new, done[:, t * chunk:(t + 1) * chu...  5.08 us
    dot_general x8, matrix products, per_device(): part_own, part_far = (dot_t(low, x_own), dot_t(low, x_far))  3.3 us
  transfers between devices with their start and end apart: 40, of which 28 were waited for; matrix products, arithmetic and copies ran while one was open for 8% of the time, Pallas kernels for 0%

profile of v1, /device:TPU:0, one launch (start us, length us, event | category | flops | bytes accessed | tf_op | source)
XLA Modules:
  0.0 135.7 jit_solution(5294109842463764613)
XLA Ops:
  7.1 2.3 %multiply_convert_fusion = (bf16[32,256]{1,0:T(8,128)(2,1)S(1)}, f32[32,256]{1,0:T(8,128)S(1)}) fusion(f32[32,256]{1,0:T(8,128)S(1)} %copy-done.2, f32[32]{0:T(128)S(1)} %sqrt.8, f32[256]{0:T(256)S(1)} %compare_convert_fusion.1, f32[32,256]{1,0:T(8,128)S(1)} %copy-done.3, bf16[256,4096]{1,0:T(8,128)(2,1)} %param.10, f32[32,8192]{1,0:T(8,128)S(1)} %copy.137, ...), kind=kOutput, calls=%fused_computation.128 | convolution fusion | flops 67158016 | bytes 2475524 | tf_op jit(solution)/shard_map/dot_general | solution.py:90
  11.4 3.1 %collective-permute-start.2 = (f32[32,512]{1,0:T(8,128)S(1)}, f32[32,512]{1,0:T(8,128)S(1)}, u32[]{:S(2)}, u32[]{:S(2)}) collective-permute-start(f32[32,512]{1,0:T(8,128)S(1)} %get-tuple-element.61), channel_id=1, source_target_pairs={{0,4},{1,5},{2,6},{3,7},{4,0},{5,1},{6,2},{7,3},{8,12},{9,13},{10,... | collective-permute-start | bytes 196616 | tf_op jit(solution)/shard_map/ppermute | solution.py:17
  14.5 2.6 %collective-permute-start.3 = (f32[32,512]{1,0:T(8,128)S(1)}, f32[32,512]{1,0:T(8,128)S(1)}, u32[]{:S(2)}, u32[]{:S(2)}) collective-permute-start(f32[32,512]{1,0:T(8,128)S(1)} %get-tuple-element.60), channel_id=1, source_target_pairs={{0,8},{1,9},{2,10},{3,11},{4,12},{5,13},{6,14},{7,15},{8,0},{9,1},... | collective-permute-start | bytes 196616 | tf_op jit(solution)/shard_map/ppermute | solution.py:17
  17.1 4.9 %collective-permute-done.3 = f32[32,512]{1,0:T(8,128)S(1)} collective-permute-done((f32[32,512]{1,0:T(8,128)S(1)}, f32[32,512]{1,0:T(8,128)S(1)}, u32[]{:S(2)}, u32[]{:S(2)}) %collective-permute-start.3) | collective-permute-done | bytes 65568 | tf_op jit(solution)/shard_map/ppermute | solution.py:17
  23.3 1.6 %collective-permute-start.5 = (f32[32,512]{1,0:T(8,128)S(1)}, f32[32,512]{1,0:T(8,128)S(1)}, u32[]{:S(2)}, u32[]{:S(2)}) collective-permute-start(f32[32,512]{1,0:T(8,128)S(1)} %fusion.24), channel_id=1, source_target_pairs={{0,2},{1,3},{2,0},{3,1},{4,6},{5,7},{6,4},{7,5},{8,10},{9,11},{10,... | collective-permute-start | bytes 196616 | tf_op jit(solution)/shard_map/ppermute | solution.py:17
  24.9 2.7 %collective-permute-done.5 = f32[32,512]{1,0:T(8,128)S(1)} collective-permute-done((f32[32,512]{1,0:T(8,128)S(1)}, f32[32,512]{1,0:T(8,128)S(1)}, u32[]{:S(2)}, u32[]{:S(2)}) %collective-permute-start.5) | collective-permute-done | bytes 65568 | tf_op jit(solution)/shard_map/ppermute | solution.py:17
  28.8 1.9 %collective-permute-start.8 = (bf16[32,640]{1,0:T(8,128)(2,1)S(1)}, bf16[32,640]{1,0:T(8,128)(2,1)S(1)}, u32[]{:S(2)}, u32[]{:S(2)}) collective-permute-start(bf16[32,640]{1,0:T(8,128)(2,1)S(1)} %pad_maximum_fusion.23), channel_id=1, source_target_pairs={{0,12},{1,13},{2,14},{3,15},{4,8},{5,9},{6,10},{7,11},{8,4},{9,5},... | collective-permute-start | bytes 122888 | tf_op jit(solution)/shard_map/ppermute | solution.py:17
  31.0 2.2 %collective-permute-start.6 = (bf16[32,640]{1,0:T(8,128)(2,1)S(1)}, bf16[32,640]{1,0:T(8,128)(2,1)S(1)}, u32[]{:S(2)}, u32[]{:S(2)}) collective-permute-start(bf16[32,640]{1,0:T(8,128)(2,1)S(1)} %pad_maximum_fusion.23), channel_id=1, source_target_pairs={{0,4},{1,5},{2,6},{3,7},{4,0},{5,1},{6,2},{7,3},{8,12},{9,13},{10,... | collective-permute-start | bytes 122888 | tf_op jit(solution)/shard_map/ppermute | solution.py:17
  40.1 2.0 %collective-permute-start.12 = (f32[32,640]{1,0:T(8,128)}, f32[32,640]{1,0:T(8,128)S(1)}, u32[]{:S(2)}, u32[]{:S(2)}) collective-permute-start(f32[32,640]{1,0:T(8,128)} %get-tuple-element.76), channel_id=1, source_target_pairs={{0,12},{1,13},{2,14},{3,15},{4,8},{5,9},{6,10},{7,11},{8,4},{9,5},... | collective-permute-start | bytes 245768 | tf_op jit(solution)/shard_map/ppermute | solution.py:17
  42.9 1.6 %collective-permute-start.10 = (f32[32,640]{1,0:T(8,128)S(1)}, f32[32,640]{1,0:T(8,128)}, u32[]{:S(2)}, u32[]{:S(2)}) collective-permute-start(f32[32,640]{1,0:T(8,128)S(1)} %get-tuple-element.74), channel_id=1, source_target_pairs={{0,4},{1,5},{2,6},{3,7},{4,0},{5,1},{6,2},{7,3},{8,12},{9,13},{10,... | collective-permute-start | bytes 245768 | tf_op jit(solution)/shard_map/ppermute | solution.py:17
  44.6 2.9 %collective-permute-done.12 = f32[32,640]{1,0:T(8,128)S(1)} collective-permute-done((f32[32,640]{1,0:T(8,128)}, f32[32,640]{1,0:T(8,128)S(1)}, u32[]{:S(2)}, u32[]{:S(2)}) %collective-permute-start.12) | collective-permute-done | bytes 81952 | tf_op jit(solution)/shard_map/ppermute | solution.py:17
  47.5 3.4 %collective-permute-done.11 = f32[32,640]{1,0:T(8,128)S(1)} collective-permute-done((f32[32,640]{1,0:T(8,128)S(1)}, f32[32,640]{1,0:T(8,128)S(1)}, u32[]{:S(2)}, u32[]{:S(2)}) %collective-permute-start.11) | collective-permute-done | bytes 81952 | tf_op jit(solution)/shard_map/ppermute | solution.py:17
  52.7 1.6 %collective-permute-start.13 = (f32[32,640]{1,0:T(8,128)S(1)}, f32[32,640]{1,0:T(8,128)S(1)}, u32[]{:S(2)}, u32[]{:S(2)}) collective-permute-start(f32[32,640]{1,0:T(8,128)S(1)} %pad_maximum_fusion.11), channel_id=1, source_target_pairs={{0,2},{1,3},{2,0},{3,1},{4,6},{5,7},{6,4},{7,5},{8,10},{9,11},{10,... | collective-permute-start | bytes 245768 | tf_op jit(solution)/shard_map/ppermute | solution.py:17
  54.3 2.8 %collective-permute-done.13 = f32[32,640]{1,0:T(8,128)S(1)} collective-permute-done((f32[32,640]{1,0:T(8,128)S(1)}, f32[32,640]{1,0:T(8,128)S(1)}, u32[]{:S(2)}, u32[]{:S(2)}) %collective-permute-start.13) | collective-permute-done | bytes 81952 | tf_op jit(solution)/shard_map/ppermute | solution.py:17
  57.7 1.9 %collective-permute-start.16 = (bf16[32,640]{1,0:T(8,128)(2,1)S(1)}, bf16[32,640]{1,0:T(8,128)(2,1)S(1)}, u32[]{:S(2)}, u32[]{:S(2)}) collective-permute-start(bf16[32,640]{1,0:T(8,128)(2,1)S(1)} %pad_maximum_fusion.24), channel_id=1, source_target_pairs={{0,12},{1,13},{2,14},{3,15},{4,8},{5,9},{6,10},{7,11},{8,4},{9,5},... | collective-permute-start | bytes 122888 | tf_op jit(solution)/shard_map/ppermute | solution.py:17
  59.7 2.5 %collective-permute-start.14 = (bf16[32,640]{1,0:T(8,128)(2,1)S(1)}, bf16[32,640]{1,0:T(8,128)(2,1)S(1)}, u32[]{:S(2)}, u32[]{:S(2)}) collective-permute-start(bf16[32,640]{1,0:T(8,128)(2,1)S(1)} %pad_maximum_fusion.24), channel_id=1, source_target_pairs={{0,4},{1,5},{2,6},{3,7},{4,0},{5,1},{6,2},{7,3},{8,12},{9,13},{10,... | collective-permute-start | bytes 122888 | tf_op jit(solution)/shard_map/ppermute | solution.py:17
  68.6 2.0 %collective-permute-start.20 = (bf16[32,640]{1,0:T(8,128)(2,1)S(1)}, bf16[32,640]{1,0:T(8,128)(2,1)S(1)}, u32[]{:S(2)}, u32[]{:S(2)}) collective-permute-start(bf16[32,640]{1,0:T(8,128)(2,1)S(1)} %get-tuple-element.89), channel_id=1, source_target_pairs={{0,12},{1,13},{2,14},{3,15},{4,8},{5,9},{6,10},{7,11},{8,4},{9,5},... | collective-permute-start | bytes 122888 | tf_op jit(solution)/shard_map/ppermute | solution.py:17
  73.0 1.8 %collective-permute-done.20 = bf16[32,640]{1,0:T(8,128)(2,1)S(1)} collective-permute-done((bf16[32,640]{1,0:T(8,128)(2,1)S(1)}, bf16[32,640]{1,0:T(8,128)(2,1)S(1)}, u32[]{:S(2)}, u32[]{:S(2)}) %collective-permute-start.20) | collective-permute-done | bytes 40992 | tf_op jit(solution)/shard_map/ppermute | solution.py:17
  76.7 1.6 %collective-permute-start.21 = (f32[32,640]{1,0:T(8,128)S(1)}, f32[32,640]{1,0:T(8,128)S(1)}, u32[]{:S(2)}, u32[]{:S(2)}) collective-permute-start(f32[32,640]{1,0:T(8,128)S(1)} %pad_maximum_fusion.13), channel_id=1, source_target_pairs={{0,2},{1,3},{2,0},{3,1},{4,6},{5,7},{6,4},{7,5},{8,10},{9,11},{10,... | collective-permute-start | bytes 245768 | tf_op jit(solution)/shard_map/ppermute | solution.py:17
  78.3 2.8 %collective-permute-done.21 = f32[32,640]{1,0:T(8,128)S(1)} collective-permute-done((f32[32,640]{1,0:T(8,128)S(1)}, f32[32,640]{1,0:T(8,128)S(1)}, u32[]{:S(2)}, u32[]{:S(2)}) %collective-permute-start.21) | collective-permute-done | bytes 81952 | tf_op jit(solution)/shard_map/ppermute | solution.py:17
  81.7 1.9 %collective-permute-start.24 = (bf16[32,640]{1,0:T(8,128)(2,1)S(1)}, bf16[32,640]{1,0:T(8,128)(2,1)S(1)}, u32[]{:S(2)}, u32[]{:S(2)}) collective-permute-start(bf16[32,640]{1,0:T(8,128)(2,1)S(1)} %pad_maximum_fusion.25), channel_id=1, source_target_pairs={{0,12},{1,13},{2,14},{3,15},{4,8},{5,9},{6,10},{7,11},{8,4},{9,5},... | collective-permute-start | bytes 122888 | tf_op jit(solution)/shard_map/ppermute | solution.py:17
  83.9 2.2 %collective-permute-start.22 = (bf16[32,640]{1,0:T(8,128)(2,1)S(1)}, bf16[32,640]{1,0:T(8,128)(2,1)S(1)}, u32[]{:S(2)}, u32[]{:S(2)}) collective-permute-start(bf16[32,640]{1,0:T(8,128)(2,1)S(1)} %pad_maximum_fusion.25), channel_id=1, source_target_pairs={{0,4},{1,5},{2,6},{3,7},{4,0},{5,1},{6,2},{7,3},{8,12},{9,13},{10,... | collective-permute-start | bytes 122888 | tf_op jit(solution)/shard_map/ppermute | solution.py:17
  92.6 2.0 %collective-permute-start.28 = (bf16[32,640]{1,0:T(8,128)(2,1)S(1)}, bf16[32,640]{1,0:T(8,128)(2,1)S(1)}, u32[]{:S(2)}, u32[]{:S(2)}) collective-permute-start(bf16[32,640]{1,0:T(8,128)(2,1)S(1)} %get-tuple-element.82), channel_id=1, source_target_pairs={{0,12},{1,13},{2,14},{3,15},{4,8},{5,9},{6,10},{7,11},{8,4},{9,5},... | collective-permute-start | bytes 122888 | tf_op jit(solution)/shard_map/ppermute | solution.py:17
  97.1 1.8 %collective-permute-done.28 = bf16[32,640]{1,0:T(8,128)(2,1)S(1)} collective-permute-done((bf16[32,640]{1,0:T(8,128)(2,1)S(1)}, bf16[32,640]{1,0:T(8,128)(2,1)S(1)}, u32[]{:S(2)}, u32[]{:S(2)}) %collective-permute-start.28) | collective-permute-done | bytes 40992 | tf_op jit(solution)/shard_map/ppermute | solution.py:17
  100.8 1.6 %collective-permute-start.29 = (f32[32,640]{1,0:T(8,128)S(1)}, f32[32,640]{1,0:T(8,128)S(1)}, u32[]{:S(2)}, u32[]{:S(2)}) collective-permute-start(f32[32,640]{1,0:T(8,128)S(1)} %pad_maximum_fusion.15), channel_id=1, source_target_pairs={{0,2},{1,3},{2,0},{3,1},{4,6},{5,7},{6,4},{7,5},{8,10},{9,11},{10,... | collective-permute-start | bytes 245768 | tf_op jit(solution)/shard_map/ppermute | solution.py:17
  102.5 2.8 %collective-permute-done.29 = f32[32,640]{1,0:T(8,128)S(1)} collective-permute-done((f32[32,640]{1,0:T(8,128)S(1)}, f32[32,640]{1,0:T(8,128)S(1)}, u32[]{:S(2)}, u32[]{:S(2)}) %collective-permute-start.29) | collective-permute-done | bytes 81952 | tf_op jit(solution)/shard_map/ppermute | solution.py:17
  105.8 1.8 %collective-permute-start.32 = (bf16[32,640]{1,0:T(8,128)(2,1)S(1)}, bf16[32,640]{1,0:T(8,128)(2,1)S(1)}, u32[]{:S(2)}, u32[]{:S(2)}) collective-permute-start(bf16[32,640]{1,0:T(8,128)(2,1)S(1)} %pad_maximum_fusion.26), channel_id=1, source_target_pairs={{0,12},{1,13},{2,14},{3,15},{4,8},{5,9},{6,10},{7,11},{8,4},{9,5},... | collective-permute-start | bytes 122888 | tf_op jit(solution)/shard_map/ppermute | solution.py:17
  108.0 2.3 %collective-permute-start.30 = (bf16[32,640]{1,0:T(8,128)(2,1)S(1)}, bf16[32,640]{1,0:T(8,128)(2,1)S(1)}, u32[]{:S(2)}, u32[]{:S(2)}) collective-permute-start(bf16[32,640]{1,0:T(8,128)(2,1)S(1)} %pad_maximum_fusion.26), channel_id=1, source_target_pairs={{0,4},{1,5},{2,6},{3,7},{4,0},{5,1},{6,2},{7,3},{8,12},{9,13},{10,... | collective-permute-start | bytes 122888 | tf_op jit(solution)/shard_map/ppermute | solution.py:17
  118.8 2.2 %collective-permute-done.35 = f32[32,128]{1,0:T(8,128)S(1)} collective-permute-done((f32[32,128]{1,0:T(8,128)S(1)}, f32[32,128]{1,0:T(8,128)S(1)}, u32[]{:S(2)}, u32[]{:S(2)}) %collective-permute-start.35) | collective-permute-done | bytes 16416 | tf_op jit(solution)/shard_map/ppermute | solution.py:17
  121.0 1.9 %collective-permute-start.37 = (f32[32,128]{1,0:T(8,128)S(1)}, f32[32,128]{1,0:T(8,128)S(1)}, u32[]{:S(2)}, u32[]{:S(2)}) collective-permute-start(f32[32,128]{1,0:T(8,128)S(1)} %add.761), channel_id=1, source_target_pairs={{0,8},{1,9},{2,10},{3,11},{4,12},{5,13},{6,14},{7,15},{8,0},{9,1},... | collective-permute-start | bytes 49160 | tf_op jit(solution)/shard_map/ppermute | solution.py:17
  122.9 2.1 %collective-permute-start.38 = (f32[32,128]{1,0:T(8,128)S(1)}, f32[32,128]{1,0:T(8,128)S(1)}, u32[]{:S(2)}, u32[]{:S(2)}) collective-permute-start(f32[32,128]{1,0:T(8,128)S(1)} %add.761), channel_id=1, source_target_pairs={{0,12},{1,13},{2,14},{3,15},{4,8},{5,9},{6,10},{7,11},{8,4},{9,5},... | collective-permute-start | bytes 49160 | tf_op jit(solution)/shard_map/ppermute | solution.py:17
  126.3 2.1 %collective-permute-done.38 = f32[32,128]{1,0:T(8,128)S(1)} collective-permute-done((f32[32,128]{1,0:T(8,128)S(1)}, f32[32,128]{1,0:T(8,128)S(1)}, u32[]{:S(2)}, u32[]{:S(2)}) %collective-permute-start.38) | collective-permute-done | bytes 16416 | tf_op jit(solution)/shard_map/ppermute | solution.py:17
  (246 shorter events, 60.1 us)
Async XLA Ops:
  4.7 6.4 %collective-permute-start.1 = (bf16[256,2048]{1,0:T(8,128)(2,1)}, bf16[256,2048]{1,0:T(8,128)(2,1)S(1)}, u32[]{:S(2)}, u32[]{:S(2)}) collective-permute-start(bf16[256,2048]{1,0:T(8,128)(2,1)} %pad_maximum_fusion.1), channel_id=1, source_target_pairs={{0,1},{1,0},{2,3},{3,2},{4,5},{5,4},{6,7},{7,6},{8,9},{9,8},{10,11... | collective-permute-start | bytes 3145736 | tf_op jit(solution)/shard_map/ppermute | solution.py:17
  11.4 5.7 %collective-permute-start.2 = (f32[32,512]{1,0:T(8,128)S(1)}, f32[32,512]{1,0:T(8,128)S(1)}, u32[]{:S(2)}, u32[]{:S(2)}) collective-permute-start(f32[32,512]{1,0:T(8,128)S(1)} %get-tuple-element.61), channel_id=1, source_target_pairs={{0,4},{1,5},{2,6},{3,7},{4,0},{5,1},{6,2},{7,3},{8,12},{9,13},{10,... | collective-permute-start | bytes 196616 | tf_op jit(solution)/shard_map/ppermute | solution.py:17
  14.5 7.5 %collective-permute-start.3 = (f32[32,512]{1,0:T(8,128)S(1)}, f32[32,512]{1,0:T(8,128)S(1)}, u32[]{:S(2)}, u32[]{:S(2)}) collective-permute-start(f32[32,512]{1,0:T(8,128)S(1)} %get-tuple-element.60), channel_id=1, source_target_pairs={{0,8},{1,9},{2,10},{3,11},{4,12},{5,13},{6,14},{7,15},{8,0},{9,1},... | collective-permute-start | bytes 196616 | tf_op jit(solution)/shard_map/ppermute | solution.py:17
  17.1 6.2 %collective-permute-start.4 = (f32[32,512]{1,0:T(8,128)S(1)}, f32[32,512]{1,0:T(8,128)S(1)}, u32[]{:S(2)}, u32[]{:S(2)}) collective-permute-start(f32[32,512]{1,0:T(8,128)S(1)} %get-tuple-element.59), channel_id=1, source_target_pairs={{0,12},{1,13},{2,14},{3,15},{4,8},{5,9},{6,10},{7,11},{8,4},{9,5},... | collective-permute-start | bytes 196616 | tf_op jit(solution)/shard_map/ppermute | solution.py:17
  23.3 4.3 %collective-permute-start.5 = (f32[32,512]{1,0:T(8,128)S(1)}, f32[32,512]{1,0:T(8,128)S(1)}, u32[]{:S(2)}, u32[]{:S(2)}) collective-permute-start(f32[32,512]{1,0:T(8,128)S(1)} %fusion.24), channel_id=1, source_target_pairs={{0,2},{1,3},{2,0},{3,1},{4,6},{5,7},{6,4},{7,5},{8,10},{9,11},{10,... | collective-permute-start | bytes 196616 | tf_op jit(solution)/shard_map/ppermute | solution.py:17
  28.8 5.9 %collective-permute-start.8 = (bf16[32,640]{1,0:T(8,128)(2,1)S(1)}, bf16[32,640]{1,0:T(8,128)(2,1)S(1)}, u32[]{:S(2)}, u32[]{:S(2)}) collective-permute-start(bf16[32,640]{1,0:T(8,128)(2,1)S(1)} %pad_maximum_fusion.23), channel_id=1, source_target_pairs={{0,12},{1,13},{2,14},{3,15},{4,8},{5,9},{6,10},{7,11},{8,4},{9,5},... | collective-permute-start | bytes 122888 | tf_op jit(solution)/shard_map/ppermute | solution.py:17
  30.7 5.1 %collective-permute-start.7 = (bf16[32,640]{1,0:T(8,128)(2,1)S(1)}, bf16[32,640]{1,0:T(8,128)(2,1)S(1)}, u32[]{:S(2)}, u32[]{:S(2)}) collective-permute-start(bf16[32,640]{1,0:T(8,128)(2,1)S(1)} %pad_maximum_fusion.23), channel_id=1, source_target_pairs={{0,8},{1,9},{2,10},{3,11},{4,12},{5,13},{6,14},{7,15},{8,0},{9,1},... | collective-permute-start | bytes 122888 | tf_op jit(solution)/shard_map/ppermute | solution.py:17
  31.0 4.8 %collective-permute-start.6 = (bf16[32,640]{1,0:T(8,128)(2,1)S(1)}, bf16[32,640]{1,0:T(8,128)(2,1)S(1)}, u32[]{:S(2)}, u32[]{:S(2)}) collective-permute-start(bf16[32,640]{1,0:T(8,128)(2,1)S(1)} %pad_maximum_fusion.23), channel_id=1, source_target_pairs={{0,4},{1,5},{2,6},{3,7},{4,0},{5,1},{6,2},{7,3},{8,12},{9,13},{10,... | collective-permute-start | bytes 122888 | tf_op jit(solution)/shard_map/ppermute | solution.py:17
  40.1 7.4 %collective-permute-start.12 = (f32[32,640]{1,0:T(8,128)}, f32[32,640]{1,0:T(8,128)S(1)}, u32[]{:S(2)}, u32[]{:S(2)}) collective-permute-start(f32[32,640]{1,0:T(8,128)} %get-tuple-element.76), channel_id=1, source_target_pairs={{0,12},{1,13},{2,14},{3,15},{4,8},{5,9},{6,10},{7,11},{8,4},{9,5},... | collective-permute-start | bytes 245768 | tf_op jit(solution)/shard_map/ppermute | solution.py:17
  42.1 8.8 %collective-permute-start.11 = (f32[32,640]{1,0:T(8,128)S(1)}, f32[32,640]{1,0:T(8,128)S(1)}, u32[]{:S(2)}, u32[]{:S(2)}) collective-permute-start(f32[32,640]{1,0:T(8,128)S(1)} %get-tuple-element.75), channel_id=1, source_target_pairs={{0,8},{1,9},{2,10},{3,11},{4,12},{5,13},{6,14},{7,15},{8,0},{9,1},... | collective-permute-start | bytes 245768 | tf_op jit(solution)/shard_map/ppermute | solution.py:17
  42.9 8.0 %collective-permute-start.10 = (f32[32,640]{1,0:T(8,128)S(1)}, f32[32,640]{1,0:T(8,128)}, u32[]{:S(2)}, u32[]{:S(2)}) collective-permute-start(f32[32,640]{1,0:T(8,128)S(1)} %get-tuple-element.74), channel_id=1, source_target_pairs={{0,4},{1,5},{2,6},{3,7},{4,0},{5,1},{6,2},{7,3},{8,12},{9,13},{10,... | collective-permute-start | bytes 245768 | tf_op jit(solution)/shard_map/ppermute | solution.py:17
  52.7 4.5 %collective-permute-start.13 = (f32[32,640]{1,0:T(8,128)S(1)}, f32[32,640]{1,0:T(8,128)S(1)}, u32[]{:S(2)}, u32[]{:S(2)}) collective-permute-start(f32[32,640]{1,0:T(8,128)S(1)} %pad_maximum_fusion.11), channel_id=1, source_target_pairs={{0,2},{1,3},{2,0},{3,1},{4,6},{5,7},{6,4},{7,5},{8,10},{9,11},{10,... | collective-permute-start | bytes 245768 | tf_op jit(solution)/shard_map/ppermute | solution.py:17
  57.7 5.9 %collective-permute-start.16 = (bf16[32,640]{1,0:T(8,128)(2,1)S(1)}, bf16[32,640]{1,0:T(8,128)(2,1)S(1)}, u32[]{:S(2)}, u32[]{:S(2)}) collective-permute-start(bf16[32,640]{1,0:T(8,128)(2,1)S(1)} %pad_maximum_fusion.24), channel_id=1, source_target_pairs={{0,12},{1,13},{2,14},{3,15},{4,8},{5,9},{6,10},{7,11},{8,4},{9,5},... | collective-permute-start | bytes 122888 | tf_op jit(solution)/shard_map/ppermute | solution.py:17
  59.7 4.9 %collective-permute-start.15 = (bf16[32,640]{1,0:T(8,128)(2,1)S(1)}, bf16[32,640]{1,0:T(8,128)(2,1)S(1)}, u32[]{:S(2)}, u32[]{:S(2)}) collective-permute-start(bf16[32,640]{1,0:T(8,128)(2,1)S(1)} %pad_maximum_fusion.24), channel_id=1, source_target_pairs={{0,8},{1,9},{2,10},{3,11},{4,12},{5,13},{6,14},{7,15},{8,0},{9,1},... | collective-permute-start | bytes 122888 | tf_op jit(solution)/shard_map/ppermute | solution.py:17
  59.7 4.9 %collective-permute-start.14 = (bf16[32,640]{1,0:T(8,128)(2,1)S(1)}, bf16[32,640]{1,0:T(8,128)(2,1)S(1)}, u32[]{:S(2)}, u32[]{:S(2)}) collective-permute-start(bf16[32,640]{1,0:T(8,128)(2,1)S(1)} %pad_maximum_fusion.24), channel_id=1, source_target_pairs={{0,4},{1,5},{2,6},{3,7},{4,0},{5,1},{6,2},{7,3},{8,12},{9,13},{10,... | collective-permute-start | bytes 122888 | tf_op jit(solution)/shard_map/ppermute | solution.py:17
  68.6 6.3 %collective-permute-start.20 = (bf16[32,640]{1,0:T(8,128)(2,1)S(1)}, bf16[32,640]{1,0:T(8,128)(2,1)S(1)}, u32[]{:S(2)}, u32[]{:S(2)}) collective-permute-start(bf16[32,640]{1,0:T(8,128)(2,1)S(1)} %get-tuple-element.89), channel_id=1, source_target_pairs={{0,12},{1,13},{2,14},{3,15},{4,8},{5,9},{6,10},{7,11},{8,4},{9,5},... | collective-permute-start | bytes 122888 | tf_op jit(solution)/shard_map/ppermute | solution.py:17
  70.5 5.8 %collective-permute-start.19 = (bf16[32,640]{1,0:T(8,128)(2,1)S(1)}, bf16[32,640]{1,0:T(8,128)(2,1)S(1)}, u32[]{:S(2)}, u32[]{:S(2)}) collective-permute-start(bf16[32,640]{1,0:T(8,128)(2,1)S(1)} %get-tuple-element.90), channel_id=1, source_target_pairs={{0,8},{1,9},{2,10},{3,11},{4,12},{5,13},{6,14},{7,15},{8,0},{9,1},... | collective-permute-start | bytes 122888 | tf_op jit(solution)/shard_map/ppermute | solution.py:17
  71.7 4.7 %collective-permute-start.18 = (bf16[32,640]{1,0:T(8,128)(2,1)S(1)}, bf16[32,640]{1,0:T(8,128)(2,1)S(1)}, u32[]{:S(2)}, u32[]{:S(2)}) collective-permute-start(bf16[32,640]{1,0:T(8,128)(2,1)S(1)} %get-tuple-element.88), channel_id=1, source_target_pairs={{0,4},{1,5},{2,6},{3,7},{4,0},{5,1},{6,2},{7,3},{8,12},{9,13},{10,... | collective-permute-start | bytes 122888 | tf_op jit(solution)/shard_map/ppermute | solution.py:17
  76.7 4.5 %collective-permute-start.21 = (f32[32,640]{1,0:T(8,128)S(1)}, f32[32,640]{1,0:T(8,128)S(1)}, u32[]{:S(2)}, u32[]{:S(2)}) collective-permute-start(f32[32,640]{1,0:T(8,128)S(1)} %pad_maximum_fusion.13), channel_id=1, source_target_pairs={{0,2},{1,3},{2,0},{3,1},{4,6},{5,7},{6,4},{7,5},{8,10},{9,11},{10,... | collective-permute-start | bytes 245768 | tf_op jit(solution)/shard_map/ppermute | solution.py:17
  81.7 6.0 %collective-permute-start.24 = (bf16[32,640]{1,0:T(8,128)(2,1)S(1)}, bf16[32,640]{1,0:T(8,128)(2,1)S(1)}, u32[]{:S(2)}, u32[]{:S(2)}) collective-permute-start(bf16[32,640]{1,0:T(8,128)(2,1)S(1)} %pad_maximum_fusion.25), channel_id=1, source_target_pairs={{0,12},{1,13},{2,14},{3,15},{4,8},{5,9},{6,10},{7,11},{8,4},{9,5},... | collective-permute-start | bytes 122888 | tf_op jit(solution)/shard_map/ppermute | solution.py:17
  83.6 5.0 %collective-permute-start.23 = (bf16[32,640]{1,0:T(8,128)(2,1)S(1)}, bf16[32,640]{1,0:T(8,128)(2,1)S(1)}, u32[]{:S(2)}, u32[]{:S(2)}) collective-permute-start(bf16[32,640]{1,0:T(8,128)(2,1)S(1)} %pad_maximum_fusion.25), channel_id=1, source_target_pairs={{0,8},{1,9},{2,10},{3,11},{4,12},{5,13},{6,14},{7,15},{8,0},{9,1},... | collective-permute-start | bytes 122888 | tf_op jit(solution)/shard_map/ppermute | solution.py:17
  83.9 4.7 %collective-permute-start.22 = (bf16[32,640]{1,0:T(8,128)(2,1)S(1)}, bf16[32,640]{1,0:T(8,128)(2,1)S(1)}, u32[]{:S(2)}, u32[]{:S(2)}) collective-permute-start(bf16[32,640]{1,0:T(8,128)(2,1)S(1)} %pad_maximum_fusion.25), channel_id=1, source_target_pairs={{0,4},{1,5},{2,6},{3,7},{4,0},{5,1},{6,2},{7,3},{8,12},{9,13},{10,... | collective-permute-start | bytes 122888 | tf_op jit(solution)/shard_map/ppermute | solution.py:17
  92.6 6.3 %collective-permute-start.28 = (bf16[32,640]{1,0:T(8,128)(2,1)S(1)}, bf16[32,640]{1,0:T(8,128)(2,1)S(1)}, u32[]{:S(2)}, u32[]{:S(2)}) collective-permute-start(bf16[32,640]{1,0:T(8,128)(2,1)S(1)} %get-tuple-element.82), channel_id=1, source_target_pairs={{0,12},{1,13},{2,14},{3,15},{4,8},{5,9},{6,10},{7,11},{8,4},{9,5},... | collective-permute-start | bytes 122888 | tf_op jit(solution)/shard_map/ppermute | solution.py:17
  94.6 5.8 %collective-permute-start.27 = (bf16[32,640]{1,0:T(8,128)(2,1)S(1)}, bf16[32,640]{1,0:T(8,128)(2,1)S(1)}, u32[]{:S(2)}, u32[]{:S(2)}) collective-permute-start(bf16[32,640]{1,0:T(8,128)(2,1)S(1)} %get-tuple-element.83), channel_id=1, source_target_pairs={{0,8},{1,9},{2,10},{3,11},{4,12},{5,13},{6,14},{7,15},{8,0},{9,1},... | collective-permute-start | bytes 122888 | tf_op jit(solution)/shard_map/ppermute | solution.py:17
  95.7 4.7 %collective-permute-start.26 = (bf16[32,640]{1,0:T(8,128)(2,1)S(1)}, bf16[32,640]{1,0:T(8,128)(2,1)S(1)}, u32[]{:S(2)}, u32[]{:S(2)}) collective-permute-start(bf16[32,640]{1,0:T(8,128)(2,1)S(1)} %get-tuple-element.81), channel_id=1, source_target_pairs={{0,4},{1,5},{2,6},{3,7},{4,0},{5,1},{6,2},{7,3},{8,12},{9,13},{10,... | collective-permute-start | bytes 122888 | tf_op jit(solution)/shard_map/ppermute | solution.py:17
  100.8 4.5 %collective-permute-start.29 = (f32[32,640]{1,0:T(8,128)S(1)}, f32[32,640]{1,0:T(8,128)S(1)}, u32[]{:S(2)}, u32[]{:S(2)}) collective-permute-start(f32[32,640]{1,0:T(8,128)S(1)} %pad_maximum_fusion.15), channel_id=1, source_target_pairs={{0,2},{1,3},{2,0},{3,1},{4,6},{5,7},{6,4},{7,5},{8,10},{9,11},{10,... | collective-permute-start | bytes 245768 | tf_op jit(solution)/shard_map/ppermute | solution.py:17
  105.8 5.9 %collective-permute-start.32 = (bf16[32,640]{1,0:T(8,128)(2,1)S(1)}, bf16[32,640]{1,0:T(8,128)(2,1)S(1)}, u32[]{:S(2)}, u32[]{:S(2)}) collective-permute-start(bf16[32,640]{1,0:T(8,128)(2,1)S(1)} %pad_maximum_fusion.26), channel_id=1, source_target_pairs={{0,12},{1,13},{2,14},{3,15},{4,8},{5,9},{6,10},{7,11},{8,4},{9,5},... | collective-permute-start | bytes 122888 | tf_op jit(solution)/shard_map/ppermute | solution.py:17
  107.6 5.1 %collective-permute-start.31 = (bf16[32,640]{1,0:T(8,128)(2,1)S(1)}, bf16[32,640]{1,0:T(8,128)(2,1)S(1)}, u32[]{:S(2)}, u32[]{:S(2)}) collective-permute-start(bf16[32,640]{1,0:T(8,128)(2,1)S(1)} %pad_maximum_fusion.26), channel_id=1, source_target_pairs={{0,8},{1,9},{2,10},{3,11},{4,12},{5,13},{6,14},{7,15},{8,0},{9,1},... | collective-permute-start | bytes 122888 | tf_op jit(solution)/shard_map/ppermute | solution.py:17
  108.0 4.7 %collective-permute-start.30 = (bf16[32,640]{1,0:T(8,128)(2,1)S(1)}, bf16[32,640]{1,0:T(8,128)(2,1)S(1)}, u32[]{:S(2)}, u32[]{:S(2)}) collective-permute-start(bf16[32,640]{1,0:T(8,128)(2,1)S(1)} %pad_maximum_fusion.26), channel_id=1, source_target_pairs={{0,4},{1,5},{2,6},{3,7},{4,0},{5,1},{6,2},{7,3},{8,12},{9,13},{10,... | collective-permute-start | bytes 122888 | tf_op jit(solution)/shard_map/ppermute | solution.py:17
  121.0 5.3 %collective-permute-start.37 = (f32[32,128]{1,0:T(8,128)S(1)}, f32[32,128]{1,0:T(8,128)S(1)}, u32[]{:S(2)}, u32[]{:S(2)}) collective-permute-start(f32[32,128]{1,0:T(8,128)S(1)} %add.761), channel_id=1, source_target_pairs={{0,8},{1,9},{2,10},{3,11},{4,12},{5,13},{6,14},{7,15},{8,0},{9,1},... | collective-permute-start | bytes 49160 | tf_op jit(solution)/shard_map/ppermute | solution.py:17
  122.9 5.5 %collective-permute-start.38 = (f32[32,128]{1,0:T(8,128)S(1)}, f32[32,128]{1,0:T(8,128)S(1)}, u32[]{:S(2)}, u32[]{:S(2)}) collective-permute-start(f32[32,128]{1,0:T(8,128)S(1)} %add.761), channel_id=1, source_target_pairs={{0,12},{1,13},{2,14},{3,15},{4,8},{5,9},{6,10},{7,11},{8,4},{9,5},... | collective-permute-start | bytes 49160 | tf_op jit(solution)/shard_map/ppermute | solution.py:17
  129.2 3.8 %collective-permute-start.39 = (f32[32,4096]{1,0:T(8,128)S(1)}, f32[32,4096]{1,0:T(8,128)S(1)}, u32[]{:S(2)}, u32[]{:S(2)}) collective-permute-start(f32[32,4096]{1,0:T(8,128)S(1)} %pad_maximum_fusion.2), channel_id=1, source_target_pairs={{0,1},{1,0},{2,3},{3,2},{4,5},{5,4},{6,7},{7,6},{8,9},{9,8},{10,11... | collective-permute-start | bytes 1572872 | tf_op jit(solution)/shard_map/ppermute | solution.py:17
  (16 other events, 69.8 us)

commit v2 on v0

v2 whole, which is shorter than its diff:
```python
import functools

import jax
import jax.numpy as jnp
from jax import lax
from jax.experimental import pallas as pl
from jax.experimental.pallas import tpu as pltpu
from jax.sharding import PartitionSpec as P


ITERS = 4
PRIOR_DOF = 4.0
PRIOR_SCALE = 0.5
CONTRACT = (((1,), (1,)), ((), ()))
LANES = 128
QUAD = 4
F32, BF16 = jnp.float32, jnp.bfloat16


def to_parts(value):
    first = lax.reduce_precision(value, 8, 7)
    second = lax.reduce_precision(value - first, 8, 7)
    third = value - first - second
    parts = jnp.concatenate([first, second, third], axis=1).astype(BF16)
    return jnp.pad(parts, ((0, 0), (0, LANES - 3)))


def from_parts(parts):
    wide = parts.astype(F32)
    return (wide[:, 2:3] + wide[:, 1:2]) + wide[:, 0:1]


def row_sum(values):
    return jnp.sum(values, axis=1, keepdims=True)


def by_pairs(terms):
    return (terms[0] + terms[1]) + (terms[2] + terms[3])


def lanes(columns):
    return jnp.pad(jnp.concatenate(columns, axis=1), ((0, 0), (0, LANES - len(columns))))


def per_device(
    count,
    genotypes,
    residual,
    noise_people,
    noise_coef,
    coef_all,
    block_index,
    prior_prec,
    sigma2_old,
    gamma_draw,
    valid_counts,
):
    rows, width = genotypes.shape
    traits = residual.shape[0]
    quarter = width // QUAD
    me = lax.axis_index("ppl")
    own = me & (QUAD - 1)
    dot_t = functools.partial(lax.dot_general, dimension_numbers=CONTRACT, preferred_element_type=F32)
    dot = functools.partial(jnp.dot, preferred_element_type=F32)

    def swap(x, distance):
        return lax.ppermute(x, "ppl", [(i, i ^ distance) for i in range(count)])

    def over_z(x, read=lambda piece: piece):
        stride = QUAD
        while stride < count:
            ways = (1, 2, 3) if stride * 4 <= count else (1,)
            got = [read(x)] + [read(swap(x, way * stride)) for way in ways]
            x = got[0] + got[1] if len(got) == 2 else (got[0] + got[1]) + (got[2] + got[3])
            stride *= len(got)
            read = lambda piece: piece
        return x

    def unpack(piece):
        scalar = jnp.broadcast_to(from_parts(piece[:, quarter:]), (traits, LANES))
        return jnp.concatenate([piece[:, :quarter].astype(F32), scalar], axis=1)

    def columns(array, slot):
        return lax.dynamic_slice_in_dim(array, (own ^ slot) * quarter, quarter, 1)

    x_give = [columns(genotypes, u) for u in range(QUAD)]
    slots = jnp.arange(rows)
    mask = [(slots < valid_counts[me ^ u]).astype(F32)[None, :] for u in range(QUAD)]
    first_col = block_index[0] * width
    noise_var = sigma2_old[:, None]
    ridge = prior_prec[:, None]

    old_coef = lax.dynamic_slice_in_dim(coef_all, first_col, width, 1)
    fitted_old = dot_t(old_coef.astype(BF16), genotypes)
    partial_res = mask[0] * (residual + fitted_old)
    target = (mask[0] * (partial_res + jnp.sqrt(noise_var) * noise_people)).astype(BF16)
    data = [dot(target, x_give[u]) for u in range(QUAD)]
    back = swap(jnp.concatenate([data[1], data[3]], axis=1), 1)
    kept, given = data[0] + back[:, :quarter], data[2] + back[:, quarter:]
    given, x_give = lax.optimization_barrier((given, x_give))
    kept = kept + swap(given, 2)
    x = [x_give[0]] + [swap(x_give[u], u) for u in (1, 2, 3)]
    kept = over_z(kept)
    search = kept / noise_var + jnp.sqrt(ridge) * columns(noise_coef, 0)

    image = direction = length = norm_now = None
    lows, mix, weights = [], [], []
    for number in range(ITERS):
        low = search.astype(BF16)
        lows.append(low)
        wide = low.astype(F32)
        sums = [row_sum(search * search), row_sum(wide * wide)]
        if number:
            sums.append(row_sum(wide * direction))
        sent = jnp.concatenate([dot_t(low, x[u]) for u in range(QUAD)] + [lanes(sums)], axis=1)
        for way in (1, 2):
            back = swap(sent, way)
            cuts = [back[:, (u ^ way) * rows : ((u ^ way) + 1) * rows] for u in range(QUAD)]
            sent = sent + jnp.concatenate(cuts + [back[:, QUAD * rows :]], axis=1)
        tail = sent[:, QUAD * rows :]
        fresh = [mask[u] * sent[:, u * rows : (u + 1) * rows] for u in range(QUAD)]
        norm_next = tail[:, 0:1]
        if number == 0:
            image, direction, length = fresh, wide, tail[:, 1:2]
        else:
            beta = norm_next / norm_now
            image = [new + beta * old for new, old in zip(fresh, image)]
            direction = wide + beta * direction
            length = tail[:, 1:2] + beta * (2.0 * tail[:, 2:3] + beta * length)
            mix = [beta * m for m in mix]
        mix.append(jnp.ones_like(norm_next))
        weights.append(jnp.zeros_like(norm_next))
        norm_now = norm_next
        rounded = [value.astype(BF16) for value in image]
        energy = by_pairs([row_sum(a * b.astype(F32)) for a, b in zip(image, rounded)])
        if number == ITERS - 1:
            break
        part = sum(dot(rounded[u], x[u]) for u in range(QUAD))
        if number == 0:
            total = over_z(jnp.concatenate([part, jnp.broadcast_to(energy, (traits, LANES))], axis=1))
        else:
            total = over_z(jnp.concatenate([part.astype(BF16), to_parts(energy)], axis=1), unpack)
        if number == 0:
            before = [partial_res] + [swap(partial_res, u) for u in (1, 2, 3)]
            total, before = lax.optimization_barrier((total, before))
        if number == ITERS - 2:
            early = jnp.concatenate(lows, axis=1)
            early = [early] + [swap(early, u) for u in (1, 2, 3)]
            total, early = lax.optimization_barrier((total, early))
        step = norm_now / (total[:, quarter : quarter + 1] / noise_var + ridge * length)
        search = search - step * (total[:, :quarter] / noise_var + ridge * direction)
        before = [a - step * b for a, b in zip(before, image)]
        weights = [w + step * m for w, m in zip(weights, mix)]

    late = [lows[-1]] + [swap(lows[-1], u) for u in (1, 2, 3)]
    pairs = zip(before, image)
    products = [[row_sum(a * a), row_sum(a * b), row_sum(b * b)] for a, b in pairs]
    total = over_z(lanes([energy] + [by_pairs(column) for column in zip(*products)]))
    step = norm_now / (total[:, 0:1] / noise_var + ridge * length)
    residual_new = before[0] - step * image[0]
    squares = total[:, 1] - step[:, 0] * (2.0 * total[:, 2] - step[:, 0] * total[:, 3])
    present = jnp.sum(valid_counts).astype(F32)
    sigma2_new = (squares + PRIOR_DOF * PRIOR_SCALE) / ((present + PRIOR_DOF) * gamma_draw)
    weights = lanes([w + step * m for w, m in zip(weights, mix)])
    coef_new = write_coef(jnp.stack([block_index[0], own]).astype(jnp.int32), weights, early, late, coef_all)
    return (coef_new, residual_new, sigma2_new)


def write_coef(where, weights, early, late, coef_all):
    traits, quarter = late[0].shape
    width = QUAD * quarter
    blocks = coef_all.shape[1] // width
    kept = ITERS - 1

    def kernel(where_ref, weights_ref, *refs):
        early_refs, late_refs = refs[:QUAD], refs[QUAD : 2 * QUAD]
        coef_ref, out_ref, scratch, sems = refs[2 * QUAD :]
        block = where_ref[0]

        def hold(index):
            span = pl.ds(index * width, width)
            return pltpu.make_async_copy(coef_ref.at[:, span], out_ref.at[:, span], sems.at[index])

        def give(slot):
            start = pl.multiple_of(block * width + (where_ref[1] ^ slot) * quarter, LANES)
            return pltpu.make_async_copy(scratch.at[slot], out_ref.at[:, pl.ds(start, quarter)], sems.at[blocks + slot])

        for index in range(blocks):
            pl.when(block != index)(lambda index=index: hold(index).start())
        scale = [weights_ref[:, k : k + 1] for k in range(ITERS)]
        for slot in range(QUAD):
            value = scale[kept] * late_refs[slot][...].astype(F32)
            for k in range(kept):
                value += scale[k] * early_refs[slot][:, k * quarter : (k + 1) * quarter].astype(F32)
            scratch[slot] = value
            give(slot).start()
        for slot in range(QUAD):
            give(slot).wait()
        for index in range(blocks):
            pl.when(block != index)(lambda index=index: hold(index).wait())

    vmem = pl.BlockSpec(memory_space=pltpu.VMEM)
    return pl.pallas_call(
        kernel,
        out_shape=jax.ShapeDtypeStruct(coef_all.shape, coef_all.dtype),
        in_specs=[pl.BlockSpec(memory_space=pltpu.SMEM)] + [vmem] * (1 + 2 * QUAD) + [pl.BlockSpec(memory_space=pl.ANY)],
        out_specs=pl.BlockSpec(memory_space=pl.ANY),
        scratch_shapes=[pltpu.VMEM((QUAD, traits, quarter), F32), pltpu.SemaphoreType.DMA((blocks + QUAD,))],
    )(where, weights, *early, *late, coef_all)


def solution(mesh):
    return jax.shard_map(
        functools.partial(per_device, mesh.shape["ppl"]),
        mesh=mesh,
        in_specs=(
            P(("trait", "ppl"), None),
            P("trait", "ppl"),
            P("trait", "ppl"),
            P("trait", None),
            P("trait", None),
            P("trait"),
            P("trait"),
            P("trait"),
            P("trait"),
            P("trait"),
        ),
        out_specs=(P("trait", None), P("trait", "ppl"), P("trait")),
        check_vma=False,
    )
```

time: 538 us -> 160 us (0.30)
  waiting for transfers between devices: 457 us -> 67.8 us
  starting transfers between devices: 0.21 us -> 39 us
  blocking collectives: 31.9 us -> 0 us
  Pallas kernels: 0 us -> 18.3 us
  between operations: 15.5 us -> 2.86 us
    psum x5 -> x0, waiting for transfers between devices: 457 us -> none  [the longest x4 364 us: per_device(): local_sum = lax.psum(local_sum, 'ppl')]
    ppermute x0 -> x37, waiting for transfers between devices: none -> 67.8 us  [swap(): return lax.ppermute(x, 'ppl', [(i, i ^ distance) for i in range(count)])]
    ppermute x0 -> x37, starting transfers between devices: none -> 39 us  [swap(): return lax.ppermute(x, 'ppl', [(i, i ^ distance) for i in range(count)])]
    psum x1 -> x0, blocking collectives: 31.9 us -> none  [per_device(): squares = lax.psum(jnp.sum(residual_new * residual_new, axis=1), 'ppl')]
    pallas_call x0 -> x1, Pallas kernels: none -> 18.3 us  [write_coef(): pl.pallas_call(kernel, out_shape=jax.ShapeDtypeStruct(coef_all.shape, coe...]
    reduce_sum x10 -> x15, other arithmetic: 12.5 us -> 4.18 us  [the longest x14 3.55 us: row_sum(): return jnp.sum(values, axis=1, keepdims=True)]
  transfers between devices with their start and end apart: 5 -> 37, of which waited for: 5 -> 24; matrix products, arithmetic and copies ran while one was open for 0% -> 7% of each run, Pallas kernels for 0% -> 0%
where the time goes in v2:
time: 160 us
  waiting for transfers between devices  67.8 us (42%)
  starting transfers between devices  39 us (24%)
  Pallas kernels  18.3 us (11%)
  other arithmetic  14.6 us (9%)
  matrix products  10.1 us (6%)
  local copies, waits for them, and re-layouts  7.23 us (5%)
  between operations  2.86 us (2%)
    ppermute x37, waiting for transfers between devices, swap(): return lax.ppermute(x, 'ppl', [(i, i ^ distance) for i in range(count)])  67.8 us
    ppermute x37, starting transfers between devices, swap(): return lax.ppermute(x, 'ppl', [(i, i ^ distance) for i in range(count)])  39 us
    pallas_call x1, Pallas kernels, write_coef(): pl.pallas_call(kernel, out_shape=jax.ShapeDtypeStruct(coef_all.shape, coe...  18.3 us
    dot_general x16, matrix products, per_device(): dot_t(low, x[u])  4.07 us
    reduce_sum x14, other arithmetic, row_sum(): return jnp.sum(values, axis=1, keepdims=True)  3.55 us
  transfers between devices with their start and end apart: 37, of which 24 were waited for; matrix products, arithmetic and copies ran while one was open for 7% of the time, Pallas kernels for 0%

profile of v2, /device:TPU:0, one launch (start us, length us, event | category | flops | bytes accessed | tf_op | source)
XLA Modules:
  0.0 159.8 jit_solution(12404261720628096053)
XLA Ops:
  2.0 1.5 fusion.112
  4.2 2.6 %constant_dynamic-slice_fusion.3 = (bf16[256,1024]{1,0:T(8,128)(2,1)S(1)}, bf16[256,1024]{1,0:T(8,128)(2,1)}, bf16[256,1024]{1,0:T(8,128)(2,1)S(1)}, bf16[256,1024]{1,0:T(8,128)(2,1)S(1)}) fusion(bf16[256,4096]{1,0:T(8,128)(2,1)} %param.10, s32[]{:T(128)S(6)} %select_n.30, s32[]{:T(128)S(6)} %select_n.31, s32[]{:T(128)S(6)} %select_n.33, s32[]{:T(128)S(6)} %select_n.32), kind=kLoop, calls=%fused_computation.271 | loop fusion | bytes 4194320 | tf_op jit(solution)/shard_map/dynamic_slice | solution.py:84
  6.8 1.8 %multiply_convert_fusion = (bf16[32,256]{1,0:T(8,128)(2,1)S(1)}, f32[32,256]{1,0:T(8,128)S(1)}) fusion(f32[32,256]{1,0:T(8,128)S(1)} %copy-done.14, f32[32]{0:T(128)S(1)} %sqrt.8, f32[256]{0:T(256)S(1)} %compare_convert_fusion.3, f32[32,256]{1,0:T(8,128)S(1)} %copy-done.15, bf16[256,4096]{1,0:T(8,128)(2,1)S(1)} %copy-done, f32[32,8192]{1,0:T(8,128)} %refs_8_.1, ...), kind=kOutput, calls=%fused_computation.175 | convolution fusion | flops 67158016 | bytes 2475140 | tf_op jit(solution)/shard_map/dot_general | solution.py:94
  12.0 2.9 %collective-permute-start.1 = (f32[32,1024]{1,0:T(8,128)S(1)}, f32[32,1024]{1,0:T(8,128)S(1)}, u32[]{:S(2)}, u32[]{:S(2)}) collective-permute-start(f32[32,1024]{1,0:T(8,128)S(1)} %slice_add_fusion), channel_id=1, source_target_pairs={{0,2},{1,3},{2,0},{3,1},{4,6},{5,7},{6,4},{7,5},{8,10},{9,11},{10,... | collective-permute-start | bytes 393224 | tf_op jit(solution)/shard_map/ppermute | solution.py:67
  15.2 3.6 %collective-permute-done.1 = f32[32,1024]{1,0:T(8,128)S(1)} collective-permute-done((f32[32,1024]{1,0:T(8,128)S(1)}, f32[32,1024]{1,0:T(8,128)S(1)}, u32[]{:S(2)}, u32[]{:S(2)}) %collective-permute-start.1) | collective-permute-done | bytes 131104 | tf_op jit(solution)/shard_map/ppermute | solution.py:67
  18.8 2.9 %collective-permute-start.3 = (f32[32,1024]{1,0:T(8,128)S(1)}, f32[32,1024]{1,0:T(8,128)S(1)}, u32[]{:S(2)}, u32[]{:S(2)}) collective-permute-start(f32[32,1024]{1,0:T(8,128)S(1)} %fusion.24), channel_id=1, source_target_pairs={{0,8},{1,9},{2,10},{3,11},{4,12},{5,13},{6,14},{7,15},{8,0},{9,1},... | collective-permute-start | bytes 393224 | tf_op jit(solution)/shard_map/ppermute | solution.py:67
  21.7 1.3 collective-permute-start.4
  23.3 1.6 collective-permute-start.6
  24.9 6.5 %collective-permute-done.3 = f32[32,1024]{1,0:T(8,128)S(1)} collective-permute-done((f32[32,1024]{1,0:T(8,128)S(1)}, f32[32,1024]{1,0:T(8,128)S(1)}, u32[]{:S(2)}, u32[]{:S(2)}) %collective-permute-start.3) | collective-permute-done | bytes 131104 | tf_op jit(solution)/shard_map/ppermute | solution.py:67
  33.6 4.5 %collective-permute-done.6 = bf16[256,1024]{1,0:T(8,128)(2,1)S(1)} collective-permute-done((bf16[256,1024]{1,0:T(8,128)(2,1)S(1)}, bf16[256,1024]{1,0:T(8,128)(2,1)S(1)}, u32[]{:S(2)}, u32[]{:S(2)}) %collective-permute-start.6) | collective-permute-done | bytes 524320 | tf_op jit(solution)/shard_map/ppermute | solution.py:67
  38.4 9.9 %collective-permute-done.7 = bf16[256,1024]{1,0:T(8,128)(2,1)S(1)} collective-permute-done((bf16[256,1024]{1,0:T(8,128)(2,1)S(1)}, bf16[256,1024]{1,0:T(8,128)(2,1)S(1)}, u32[]{:S(2)}, u32[]{:S(2)}) %collective-permute-start.7) | collective-permute-done | bytes 524320 | tf_op jit(solution)/shard_map/ppermute | solution.py:67
  50.1 1.6 collective-permute-start.9
  53.6 2.7 %collective-permute-done.9 = f32[32,1152]{1,0:T(8,128)S(1)} collective-permute-done((f32[32,1152]{1,0:T(8,128)S(1)}, f32[32,1152]{1,0:T(8,128)S(1)}, u32[]{:S(2)}, u32[]{:S(2)}) %collective-permute-start.9) | collective-permute-done | bytes 147488 | tf_op jit(solution)/shard_map/ppermute | solution.py:67
  57.4 2.9 %collective-permute-start.11 = (f32[32,1152]{1,0:T(8,128)S(1)}, f32[32,1152]{1,0:T(8,128)S(1)}, u32[]{:S(2)}, u32[]{:S(2)}) collective-permute-start(f32[32,1152]{1,0:T(8,128)S(1)} %pad_maximum_fusion.2), channel_id=1, source_target_pairs={{0,8},{1,9},{2,10},{3,11},{4,12},{5,13},{6,14},{7,15},{8,0},{9,1},... | collective-permute-start | bytes 442376 | tf_op jit(solution)/shard_map/ppermute | solution.py:67
  60.3 1.4 collective-permute-start.12
  61.6 1.5 collective-permute-start.14
  63.3 8.0 %collective-permute-done.11 = f32[32,1152]{1,0:T(8,128)S(1)} collective-permute-done((f32[32,1152]{1,0:T(8,128)S(1)}, f32[32,1152]{1,0:T(8,128)S(1)}, u32[]{:S(2)}, u32[]{:S(2)}) %collective-permute-start.11) | collective-permute-done | bytes 147488 | tf_op jit(solution)/shard_map/ppermute | solution.py:67
  71.5 3.4 %collective-permute-done.15 = f32[32,256]{1,0:T(8,128)S(1)} collective-permute-done((f32[32,256]{1,0:T(8,128)S(1)}, f32[32,256]{1,0:T(8,128)S(1)}, u32[]{:S(2)}, u32[]{:S(2)}) %collective-permute-start.15) | collective-permute-done | bytes 32800 | tf_op jit(solution)/shard_map/ppermute | solution.py:67
  80.1 4.6 %collective-permute-done.17 = f32[32,1152]{1,0:T(8,128)S(1)} collective-permute-done((f32[32,1152]{1,0:T(8,128)S(1)}, f32[32,1152]{1,0:T(8,128)S(1)}, u32[]{:S(2)}, u32[]{:S(2)}) %collective-permute-start.17) | collective-permute-done | bytes 147488 | tf_op jit(solution)/shard_map/ppermute | solution.py:67
  86.1 2.5 %collective-permute-start.20 = (bf16[32,1152]{1,0:T(8,128)(2,1)S(1)}, bf16[32,1152]{1,0:T(8,128)(2,1)S(1)}, u32[]{:S(2)}, u32[]{:S(2)}) collective-permute-start(bf16[32,1152]{1,0:T(8,128)(2,1)S(1)} %pad_maximum_fusion.7), channel_id=1, source_target_pairs={{0,12},{1,13},{2,14},{3,15},{4,8},{5,9},{6,10},{7,11},{8,4},{9,5},... | collective-permute-start | bytes 221192 | tf_op jit(solution)/shard_map/ppermute | solution.py:67
  88.7 1.9 %collective-permute-start.18 = (bf16[32,1152]{1,0:T(8,128)(2,1)S(1)}, bf16[32,1152]{1,0:T(8,128)(2,1)S(1)}, u32[]{:S(2)}, u32[]{:S(2)}) collective-permute-start(bf16[32,1152]{1,0:T(8,128)(2,1)S(1)} %pad_maximum_fusion.7), channel_id=1, source_target_pairs={{0,4},{1,5},{2,6},{3,7},{4,0},{5,1},{6,2},{7,3},{8,12},{9,13},{10,... | collective-permute-start | bytes 221192 | tf_op jit(solution)/shard_map/ppermute | solution.py:67
  90.8 1.6 collective-permute-done.20
  92.5 2.1 %collective-permute-done.19 = bf16[32,1152]{1,0:T(8,128)(2,1)S(1)} collective-permute-done((bf16[32,1152]{1,0:T(8,128)(2,1)S(1)}, bf16[32,1152]{1,0:T(8,128)(2,1)S(1)}, u32[]{:S(2)}, u32[]{:S(2)}) %collective-permute-start.19) | collective-permute-done | bytes 73760 | tf_op jit(solution)/shard_map/ppermute | solution.py:67
  97.9 1.4 collective-permute-done.21
  102.6 3.5 %collective-permute-done.22 = f32[32,1152]{1,0:T(8,128)S(1)} collective-permute-done((f32[32,1152]{1,0:T(8,128)S(1)}, f32[32,1152]{1,0:T(8,128)S(1)}, u32[]{:S(2)}, u32[]{:S(2)}) %collective-permute-start.22) | collective-permute-done | bytes 147488 | tf_op jit(solution)/shard_map/ppermute | solution.py:67
  108.0 2.6 %collective-permute-start.24 = (bf16[32,1152]{1,0:T(8,128)(2,1)S(1)}, bf16[32,1152]{1,0:T(8,128)(2,1)S(1)}, u32[]{:S(2)}, u32[]{:S(2)}) collective-permute-start(bf16[32,1152]{1,0:T(8,128)(2,1)S(1)} %pad_maximum_fusion.8), channel_id=1, source_target_pairs={{0,8},{1,9},{2,10},{3,11},{4,12},{5,13},{6,14},{7,15},{8,0},{9,1},... | collective-permute-start | bytes 221192 | tf_op jit(solution)/shard_map/ppermute | solution.py:67
  111.9 2.5 %collective-permute-start.25 = (bf16[32,1152]{1,0:T(8,128)(2,1)S(1)}, bf16[32,1152]{1,0:T(8,128)(2,1)S(1)}, u32[]{:S(2)}, u32[]{:S(2)}) collective-permute-start(bf16[32,1152]{1,0:T(8,128)(2,1)S(1)} %pad_maximum_fusion.8), channel_id=1, source_target_pairs={{0,12},{1,13},{2,14},{3,15},{4,8},{5,9},{6,10},{7,11},{8,4},{9,5},... | collective-permute-start | bytes 221192 | tf_op jit(solution)/shard_map/ppermute | solution.py:67
  115.4 2.6 %collective-permute-done.25 = bf16[32,1152]{1,0:T(8,128)(2,1)S(1)} collective-permute-done((bf16[32,1152]{1,0:T(8,128)(2,1)S(1)}, bf16[32,1152]{1,0:T(8,128)(2,1)S(1)}, u32[]{:S(2)}, u32[]{:S(2)}) %collective-permute-start.25) | collective-permute-done | bytes 73760 | tf_op jit(solution)/shard_map/ppermute | solution.py:67
  121.2 1.4 collective-permute-done.29
  124.1 4.6 %collective-permute-done.30 = f32[32,1152]{1,0:T(8,128)S(1)} collective-permute-done((f32[32,1152]{1,0:T(8,128)S(1)}, f32[32,1152]{1,0:T(8,128)S(1)}, u32[]{:S(2)}, u32[]{:S(2)}) %collective-permute-start.30) | collective-permute-done | bytes 147488 | tf_op jit(solution)/shard_map/ppermute | solution.py:67
  129.7 2.5 %collective-permute-start.33 = (f32[32,128]{1,0:T(8,128)S(1)}, f32[32,128]{1,0:T(8,128)S(1)}, u32[]{:S(2)}, u32[]{:S(2)}) collective-permute-start(f32[32,128]{1,0:T(8,128)S(1)} %pad.34), channel_id=1, source_target_pairs={{0,12},{1,13},{2,14},{3,15},{4,8},{5,9},{6,10},{7,11},{8,4},{9,5},... | collective-permute-start | bytes 49160 | tf_op jit(solution)/shard_map/ppermute | solution.py:67
  141.5 18.3 %shard_map.121 = f32[32,8192]{1,0:T(8,128)} custom-call(s32[2]{0:T(128)} %pad_add_fusion.where_ref, f32[32,128]{1,0:T(8,128)} %select_maximum_fusion.weights_ref, bf16[32,3072]{1,0:T(8,128)(2,1)} %copy-done.2, bf16[32,3072]{1,0:T(8,128)(2,1)} %collective-permute-done.26.refs_1_, bf16[32,3072]{1,0:T(8,128)(2,1)} %collective-permute-done.27.refs_2_, ...), custom_call_target="tpu_custom_call" | custom-call | tf_op jit(solution)/shard_map/pallas_call | solution.py:203
  (262 shorter events, 44.3 us)
Async XLA Ops:
  12.0 6.7 %collective-permute-start.1 = (f32[32,1024]{1,0:T(8,128)S(1)}, f32[32,1024]{1,0:T(8,128)S(1)}, u32[]{:S(2)}, u32[]{:S(2)}) collective-permute-start(f32[32,1024]{1,0:T(8,128)S(1)} %slice_add_fusion), channel_id=1, source_target_pairs={{0,2},{1,3},{2,0},{3,1},{4,6},{5,7},{6,4},{7,5},{8,10},{9,11},{10,... | collective-permute-start | bytes 393224 | tf_op jit(solution)/shard_map/ppermute | solution.py:67
  18.8 12.6 %collective-permute-start.3 = (f32[32,1024]{1,0:T(8,128)S(1)}, f32[32,1024]{1,0:T(8,128)S(1)}, u32[]{:S(2)}, u32[]{:S(2)}) collective-permute-start(f32[32,1024]{1,0:T(8,128)S(1)} %fusion.24), channel_id=1, source_target_pairs={{0,8},{1,9},{2,10},{3,11},{4,12},{5,13},{6,14},{7,15},{8,0},{9,1},... | collective-permute-start | bytes 393224 | tf_op jit(solution)/shard_map/ppermute | solution.py:67
  21.7 9.7 %collective-permute-start.4 = (f32[32,1024]{1,0:T(8,128)S(1)}, f32[32,1024]{1,0:T(8,128)S(1)}, u32[]{:S(2)}, u32[]{:S(2)}) collective-permute-start(f32[32,1024]{1,0:T(8,128)S(1)} %fusion.24), channel_id=1, source_target_pairs={{0,12},{1,13},{2,14},{3,15},{4,8},{5,9},{6,10},{7,11},{8,4},{9,5},... | collective-permute-start | bytes 393224 | tf_op jit(solution)/shard_map/ppermute | solution.py:67
  23.0 8.7 %collective-permute-start.2 = (f32[32,1024]{1,0:T(8,128)S(1)}, f32[32,1024]{1,0:T(8,128)S(1)}, u32[]{:S(2)}, u32[]{:S(2)}) collective-permute-start(f32[32,1024]{1,0:T(8,128)S(1)} %fusion.24), channel_id=1, source_target_pairs={{0,4},{1,5},{2,6},{3,7},{4,0},{5,1},{6,2},{7,3},{8,12},{9,13},{10,... | collective-permute-start | bytes 393224 | tf_op jit(solution)/shard_map/ppermute | solution.py:67
  23.3 10.1 %collective-permute-start.5 = (bf16[256,1024]{1,0:T(8,128)(2,1)}, bf16[256,1024]{1,0:T(8,128)(2,1)S(1)}, u32[]{:S(2)}, u32[]{:S(2)}) collective-permute-start(bf16[256,1024]{1,0:T(8,128)(2,1)} %get-tuple-element.20), channel_id=1, source_target_pairs={{0,1},{1,0},{2,3},{3,2},{4,5},{5,4},{6,7},{7,6},{8,9},{9,8},{10,11... | collective-permute-start | bytes 1572872 | tf_op jit(solution)/shard_map/ppermute | solution.py:67
  23.3 14.9 %collective-permute-start.6 = (bf16[256,1024]{1,0:T(8,128)(2,1)S(1)}, bf16[256,1024]{1,0:T(8,128)(2,1)S(1)}, u32[]{:S(2)}, u32[]{:S(2)}) collective-permute-start(bf16[256,1024]{1,0:T(8,128)(2,1)S(1)} %get-tuple-element.21), channel_id=1, source_target_pairs={{0,2},{1,3},{2,0},{3,1},{4,6},{5,7},{6,4},{7,5},{8,10},{9,11},{10,... | collective-permute-start | bytes 1572872 | tf_op jit(solution)/shard_map/ppermute | solution.py:67
  31.4 16.9 %collective-permute-start.7 = (bf16[256,1024]{1,0:T(8,128)(2,1)S(1)}, bf16[256,1024]{1,0:T(8,128)(2,1)S(1)}, u32[]{:S(2)}, u32[]{:S(2)}) collective-permute-start(bf16[256,1024]{1,0:T(8,128)(2,1)S(1)} %get-tuple-element.22), channel_id=1, source_target_pairs={{0,3},{1,2},{2,1},{3,0},{4,7},{5,6},{6,5},{7,4},{8,11},{9,10},{10,... | collective-permute-start | bytes 1572872 | tf_op jit(solution)/shard_map/ppermute | solution.py:67
  50.1 6.2 %collective-permute-start.9 = (f32[32,1152]{1,0:T(8,128)S(1)}, f32[32,1152]{1,0:T(8,128)S(1)}, u32[]{:S(2)}, u32[]{:S(2)}) collective-permute-start(f32[32,1152]{1,0:T(8,128)S(1)} %add.626), channel_id=1, source_target_pairs={{0,2},{1,3},{2,0},{3,1},{4,6},{5,7},{6,4},{7,5},{8,10},{9,11},{10,... | collective-permute-start | bytes 442376 | tf_op jit(solution)/shard_map/ppermute | solution.py:67
  57.4 13.9 %collective-permute-start.11 = (f32[32,1152]{1,0:T(8,128)S(1)}, f32[32,1152]{1,0:T(8,128)S(1)}, u32[]{:S(2)}, u32[]{:S(2)}) collective-permute-start(f32[32,1152]{1,0:T(8,128)S(1)} %pad_maximum_fusion.2), channel_id=1, source_target_pairs={{0,8},{1,9},{2,10},{3,11},{4,12},{5,13},{6,14},{7,15},{8,0},{9,1},... | collective-permute-start | bytes 442376 | tf_op jit(solution)/shard_map/ppermute | solution.py:67
  60.3 11.0 %collective-permute-start.12 = (f32[32,1152]{1,0:T(8,128)S(1)}, f32[32,1152]{1,0:T(8,128)S(1)}, u32[]{:S(2)}, u32[]{:S(2)}) collective-permute-start(f32[32,1152]{1,0:T(8,128)S(1)} %pad_maximum_fusion.2), channel_id=1, source_target_pairs={{0,12},{1,13},{2,14},{3,15},{4,8},{5,9},{6,10},{7,11},{8,4},{9,5},... | collective-permute-start | bytes 442376 | tf_op jit(solution)/shard_map/ppermute | solution.py:67
  61.6 9.8 %collective-permute-start.10 = (f32[32,1152]{1,0:T(8,128)S(1)}, f32[32,1152]{1,0:T(8,128)S(1)}, u32[]{:S(2)}, u32[]{:S(2)}) collective-permute-start(f32[32,1152]{1,0:T(8,128)S(1)} %pad_maximum_fusion.2), channel_id=1, source_target_pairs={{0,4},{1,5},{2,6},{3,7},{4,0},{5,1},{6,2},{7,3},{8,12},{9,13},{10,... | collective-permute-start | bytes 442376 | tf_op jit(solution)/shard_map/ppermute | solution.py:67
  61.6 9.9 %collective-permute-start.13 = (f32[32,256]{1,0:T(8,128)S(1)}, f32[32,256]{1,0:T(8,128)S(1)}, u32[]{:S(2)}, u32[]{:S(2)}) collective-permute-start(f32[32,256]{1,0:T(8,128)S(1)} %get-tuple-element.25), channel_id=1, source_target_pairs={{0,1},{1,0},{2,3},{3,2},{4,5},{5,4},{6,7},{7,6},{8,9},{9,8},{10,11... | collective-permute-start | bytes 98312 | tf_op jit(solution)/shard_map/ppermute | solution.py:67
  61.6 9.9 %collective-permute-start.14 = (f32[32,256]{1,0:T(8,128)S(1)}, f32[32,256]{1,0:T(8,128)S(1)}, u32[]{:S(2)}, u32[]{:S(2)}) collective-permute-start(f32[32,256]{1,0:T(8,128)S(1)} %get-tuple-element.25), channel_id=1, source_target_pairs={{0,2},{1,3},{2,0},{3,1},{4,6},{5,7},{6,4},{7,5},{8,10},{9,11},{10,... | collective-permute-start | bytes 98312 | tf_op jit(solution)/shard_map/ppermute | solution.py:67
  71.3 3.6 %collective-permute-start.15 = (f32[32,256]{1,0:T(8,128)S(1)}, f32[32,256]{1,0:T(8,128)S(1)}, u32[]{:S(2)}, u32[]{:S(2)}) collective-permute-start(f32[32,256]{1,0:T(8,128)S(1)} %get-tuple-element.25), channel_id=1, source_target_pairs={{0,3},{1,2},{2,1},{3,0},{4,7},{5,6},{6,5},{7,4},{8,11},{9,10},{10,... | collective-permute-start | bytes 98312 | tf_op jit(solution)/shard_map/ppermute | solution.py:67
  78.8 6.0 %collective-permute-start.17 = (f32[32,1152]{1,0:T(8,128)S(1)}, f32[32,1152]{1,0:T(8,128)S(1)}, u32[]{:S(2)}, u32[]{:S(2)}) collective-permute-start(f32[32,1152]{1,0:T(8,128)S(1)} %add.642), channel_id=1, source_target_pairs={{0,2},{1,3},{2,0},{3,1},{4,6},{5,7},{6,4},{7,5},{8,10},{9,11},{10,... | collective-permute-start | bytes 442376 | tf_op jit(solution)/shard_map/ppermute | solution.py:67
  86.1 6.2 %collective-permute-start.20 = (bf16[32,1152]{1,0:T(8,128)(2,1)S(1)}, bf16[32,1152]{1,0:T(8,128)(2,1)S(1)}, u32[]{:S(2)}, u32[]{:S(2)}) collective-permute-start(bf16[32,1152]{1,0:T(8,128)(2,1)S(1)} %pad_maximum_fusion.7), channel_id=1, source_target_pairs={{0,12},{1,13},{2,14},{3,15},{4,8},{5,9},{6,10},{7,11},{8,4},{9,5},... | collective-permute-start | bytes 221192 | tf_op jit(solution)/shard_map/ppermute | solution.py:67
  88.7 5.9 %collective-permute-start.19 = (bf16[32,1152]{1,0:T(8,128)(2,1)S(1)}, bf16[32,1152]{1,0:T(8,128)(2,1)S(1)}, u32[]{:S(2)}, u32[]{:S(2)}) collective-permute-start(bf16[32,1152]{1,0:T(8,128)(2,1)S(1)} %pad_maximum_fusion.7), channel_id=1, source_target_pairs={{0,8},{1,9},{2,10},{3,11},{4,12},{5,13},{6,14},{7,15},{8,0},{9,1},... | collective-permute-start | bytes 221192 | tf_op jit(solution)/shard_map/ppermute | solution.py:67
  88.7 6.1 %collective-permute-start.18 = (bf16[32,1152]{1,0:T(8,128)(2,1)S(1)}, bf16[32,1152]{1,0:T(8,128)(2,1)S(1)}, u32[]{:S(2)}, u32[]{:S(2)}) collective-permute-start(bf16[32,1152]{1,0:T(8,128)(2,1)S(1)} %pad_maximum_fusion.7), channel_id=1, source_target_pairs={{0,4},{1,5},{2,6},{3,7},{4,0},{5,1},{6,2},{7,3},{8,12},{9,13},{10,... | collective-permute-start | bytes 221192 | tf_op jit(solution)/shard_map/ppermute | solution.py:67
  99.3 6.8 %collective-permute-start.22 = (f32[32,1152]{1,0:T(8,128)S(1)}, f32[32,1152]{1,0:T(8,128)S(1)}, u32[]{:S(2)}, u32[]{:S(2)}) collective-permute-start(f32[32,1152]{1,0:T(8,128)S(1)} %add.672), channel_id=1, source_target_pairs={{0,2},{1,3},{2,0},{3,1},{4,6},{5,7},{6,4},{7,5},{8,10},{9,11},{10,... | collective-permute-start | bytes 442376 | tf_op jit(solution)/shard_map/ppermute | solution.py:67
  100.6 18.0 %collective-permute-start.26 = (bf16[32,3072]{1,0:T(8,128)(2,1)S(1)}, bf16[32,3072]{1,0:T(8,128)(2,1)}, u32[]{:S(2)}, u32[]{:S(2)}) collective-permute-start(bf16[32,3072]{1,0:T(8,128)(2,1)S(1)} %pad_maximum_fusion.1.refs_0_), channel_id=1, source_target_pairs={{0,1},{1,0},{2,3},{3,2},{4,5},{5,4},{6,7},{7,6},{8,9},{9,8},{10,11... | collective-permute-start | bytes 589832 | tf_op jit(solution)/shard_map/ppermute | solution.py:67
  100.7 17.9 %collective-permute-start.27 = (bf16[32,3072]{1,0:T(8,128)(2,1)S(1)}, bf16[32,3072]{1,0:T(8,128)(2,1)}, u32[]{:S(2)}, u32[]{:S(2)}) collective-permute-start(bf16[32,3072]{1,0:T(8,128)(2,1)S(1)} %pad_maximum_fusion.1.refs_0_), channel_id=1, source_target_pairs={{0,2},{1,3},{2,0},{3,1},{4,6},{5,7},{6,4},{7,5},{8,10},{9,11},{10,... | collective-permute-start | bytes 589832 | tf_op jit(solution)/shard_map/ppermute | solution.py:67
  101.6 17.1 %collective-permute-start.28 = (bf16[32,3072]{1,0:T(8,128)(2,1)S(1)}, bf16[32,3072]{1,0:T(8,128)(2,1)}, u32[]{:S(2)}, u32[]{:S(2)}) collective-permute-start(bf16[32,3072]{1,0:T(8,128)(2,1)S(1)} %pad_maximum_fusion.1.refs_0_), channel_id=1, source_target_pairs={{0,3},{1,2},{2,1},{3,0},{4,7},{5,6},{6,5},{7,4},{8,11},{9,10},{10,... | collective-permute-start | bytes 589832 | tf_op jit(solution)/shard_map/ppermute | solution.py:67
  107.5 4.4 %collective-permute-start.23 = (bf16[32,1152]{1,0:T(8,128)(2,1)S(1)}, bf16[32,1152]{1,0:T(8,128)(2,1)S(1)}, u32[]{:S(2)}, u32[]{:S(2)}) collective-permute-start(bf16[32,1152]{1,0:T(8,128)(2,1)S(1)} %pad_maximum_fusion.8), channel_id=1, source_target_pairs={{0,4},{1,5},{2,6},{3,7},{4,0},{5,1},{6,2},{7,3},{8,12},{9,13},{10,... | collective-permute-start | bytes 221192 | tf_op jit(solution)/shard_map/ppermute | solution.py:67
  108.0 7.2 %collective-permute-start.24 = (bf16[32,1152]{1,0:T(8,128)(2,1)S(1)}, bf16[32,1152]{1,0:T(8,128)(2,1)S(1)}, u32[]{:S(2)}, u32[]{:S(2)}) collective-permute-start(bf16[32,1152]{1,0:T(8,128)(2,1)S(1)} %pad_maximum_fusion.8), channel_id=1, source_target_pairs={{0,8},{1,9},{2,10},{3,11},{4,12},{5,13},{6,14},{7,15},{8,0},{9,1},... | collective-permute-start | bytes 221192 | tf_op jit(solution)/shard_map/ppermute | solution.py:67
  111.9 6.2 %collective-permute-start.25 = (bf16[32,1152]{1,0:T(8,128)(2,1)S(1)}, bf16[32,1152]{1,0:T(8,128)(2,1)S(1)}, u32[]{:S(2)}, u32[]{:S(2)}) collective-permute-start(bf16[32,1152]{1,0:T(8,128)(2,1)S(1)} %pad_maximum_fusion.8), channel_id=1, source_target_pairs={{0,12},{1,13},{2,14},{3,15},{4,8},{5,9},{6,10},{7,11},{8,4},{9,5},... | collective-permute-start | bytes 221192 | tf_op jit(solution)/shard_map/ppermute | solution.py:67
  122.7 6.0 %collective-permute-start.30 = (f32[32,1152]{1,0:T(8,128)S(1)}, f32[32,1152]{1,0:T(8,128)S(1)}, u32[]{:S(2)}, u32[]{:S(2)}) collective-permute-start(f32[32,1152]{1,0:T(8,128)S(1)} %add.702), channel_id=1, source_target_pairs={{0,2},{1,3},{2,0},{3,1},{4,6},{5,7},{6,4},{7,5},{8,10},{9,11},{10,... | collective-permute-start | bytes 442376 | tf_op jit(solution)/shard_map/ppermute | solution.py:67
  129.7 6.8 %collective-permute-start.32 = (f32[32,128]{1,0:T(8,128)S(1)}, f32[32,128]{1,0:T(8,128)S(1)}, u32[]{:S(2)}, u32[]{:S(2)}) collective-permute-start(f32[32,128]{1,0:T(8,128)S(1)} %pad.34), channel_id=1, source_target_pairs={{0,8},{1,9},{2,10},{3,11},{4,12},{5,13},{6,14},{7,15},{8,0},{9,1},... | collective-permute-start | bytes 49160 | tf_op jit(solution)/shard_map/ppermute | solution.py:67
  129.7 7.3 %collective-permute-start.33 = (f32[32,128]{1,0:T(8,128)S(1)}, f32[32,128]{1,0:T(8,128)S(1)}, u32[]{:S(2)}, u32[]{:S(2)}) collective-permute-start(f32[32,128]{1,0:T(8,128)S(1)} %pad.34), channel_id=1, source_target_pairs={{0,12},{1,13},{2,14},{3,15},{4,8},{5,9},{6,10},{7,11},{8,4},{9,5},... | collective-permute-start | bytes 49160 | tf_op jit(solution)/shard_map/ppermute | solution.py:67
  132.3 4.7 %collective-permute-start.31 = (f32[32,128]{1,0:T(8,128)S(1)}, f32[32,128]{1,0:T(8,128)S(1)}, u32[]{:S(2)}, u32[]{:S(2)}) collective-permute-start(f32[32,128]{1,0:T(8,128)S(1)} %pad.34), channel_id=1, source_target_pairs={{0,4},{1,5},{2,6},{3,7},{4,0},{5,1},{6,2},{7,3},{8,12},{9,13},{10,... | collective-permute-start | bytes 49160 | tf_op jit(solution)/shard_map/ppermute | solution.py:67
  135.1 4.1 %collective-permute-start.34 = (bf16[32,1024]{1,0:T(8,128)(2,1)S(1)}, bf16[32,1024]{1,0:T(8,128)(2,1)S(1)}, u32[]{:S(2)}, u32[]{:S(2)}) collective-permute-start(bf16[32,1024]{1,0:T(8,128)(2,1)S(1)} %get-tuple-element.70.refs_4_), channel_id=1, source_target_pairs={{0,1},{1,0},{2,3},{3,2},{4,5},{5,4},{6,7},{7,6},{8,9},{9,8},{10,11... | collective-permute-start | bytes 196616 | tf_op jit(solution)/shard_map/ppermute | solution.py:67
  135.1 4.7 %collective-permute-start.35 = (bf16[32,1024]{1,0:T(8,128)(2,1)S(1)}, bf16[32,1024]{1,0:T(8,128)(2,1)S(1)}, u32[]{:S(2)}, u32[]{:S(2)}) collective-permute-start(bf16[32,1024]{1,0:T(8,128)(2,1)S(1)} %get-tuple-element.70.refs_4_), channel_id=1, source_target_pairs={{0,2},{1,3},{2,0},{3,1},{4,6},{5,7},{6,4},{7,5},{8,10},{9,11},{10,... | collective-permute-start | bytes 196616 | tf_op jit(solution)/shard_map/ppermute | solution.py:67
  136.5 4.4 %collective-permute-start.36 = (bf16[32,1024]{1,0:T(8,128)(2,1)S(1)}, bf16[32,1024]{1,0:T(8,128)(2,1)S(1)}, u32[]{:S(2)}, u32[]{:S(2)}) collective-permute-start(bf16[32,1024]{1,0:T(8,128)(2,1)S(1)} %get-tuple-element.70.refs_4_), channel_id=1, source_target_pairs={{0,3},{1,2},{2,1},{3,0},{4,7},{5,6},{6,5},{7,4},{8,11},{9,10},{10,... | collective-permute-start | bytes 196616 | tf_op jit(solution)/shard_map/ppermute | solution.py:67
  (27 other events, 238.7 us)

commit v3 on v0

v3 whole, which is shorter than its diff:
```python
import functools

import jax
import jax.numpy as jnp
from jax import lax
from jax.experimental import pallas as pl
from jax.experimental.pallas import tpu as pltpu
from jax.sharding import PartitionSpec as P


ITERS = 4
PRIOR_DOF = 4.0
PRIOR_SCALE = 0.5
LANES = 128
TILE = 8
QUAD = 4
F32, BF16 = jnp.float32, jnp.bfloat16
PEOPLE_KIND = (F32, BF16, BF16)
IMAGE_KIND = (F32, BF16, BF16, BF16)
VMEM = pl.BlockSpec(memory_space=pltpu.VMEM)
SMEM = pl.BlockSpec(memory_space=pltpu.SMEM)
ANY = pl.BlockSpec(memory_space=pl.ANY)


def dot(a, b):
    return lax.dot_general(a, b, (((1,), (0,)), ((), ())), preferred_element_type=F32)


def dot_t(a, b):
    return lax.dot_general(a, b, (((1,), (1,)), ((), ())), preferred_element_type=F32)


def row_sum(values):
    return jnp.sum(values, axis=1, keepdims=True)


def by_pairs(terms):
    return (terms[0] + terms[1]) + (terms[2] + terms[3])


def diagonal(shape):
    return lax.broadcasted_iota(jnp.int32, shape, 0) == lax.broadcasted_iota(jnp.int32, shape, 1)


def to_row(column):
    same = diagonal((column.shape[0], LANES))
    return jnp.sum(jnp.where(same, column, 0.0), axis=0, keepdims=True)


def to_column(row, traits):
    same = diagonal((traits, row.shape[1]))
    return jnp.sum(jnp.where(same, row, 0.0), axis=1, keepdims=True)


def parts_of(value, kind):
    if kind == F32:
        return [value]
    first = value.astype(BF16)
    rest = value - first.astype(F32)
    second = rest.astype(BF16)
    return [first.astype(F32), second.astype(F32), rest - second.astype(F32)]


def pack(wide, columns, kind):
    _, width = wide.shape
    blocks = [wide[:, at : at + LANES].astype(kind) for at in range(0, width, LANES)]
    rows = [part for column in columns for part in parts_of(to_row(column), kind)]
    if rows:
        pad = -len(rows) % TILE
        rows.append(jnp.zeros((pad, LANES), F32))
        blocks.append(jnp.concatenate(rows, axis=0).astype(kind))
    return jnp.concatenate(blocks, axis=0)


def unpack(packed, traits, width, count=0):
    lines = traits * width // LANES
    wide = jnp.concatenate([packed[at : at + traits].astype(F32) for at in range(0, lines, traits)], axis=1)
    per = 1 if packed.dtype == F32 else 3
    rows = packed[lines:].astype(F32)
    columns = []
    for index in range(count):
        mine = [rows[index * per + k : index * per + k + 1] for k in range(per)]
        row = mine[0] if per == 1 else (mine[2] + mine[1]) + mine[0]
        columns.append(to_column(row, traits))
    return wide, columns


def fuse(fn, *args):
    shapes = jax.eval_shape(fn, *args)

    def kernel(*refs):
        ins, outs = refs[: len(args)], refs[len(args) :]
        for out, value in zip(outs, fn(*(ref[...] for ref in ins))):
            out[...] = value

    return pl.pallas_call(kernel, out_shape=shapes, in_specs=[VMEM] * len(args), out_specs=[VMEM] * len(shapes))(*args)


def prepare(where, genotypes, coef_all, noise_coef, residual, noise_people, mask, sigma2_old, prior_prec):
    rows, width = genotypes.shape
    traits = residual.shape[0]
    quarter = width // QUAD

    def kernel(where_ref, geno_ref, coef_ref, noise_ref, res_ref, people_ref, mask_ref, sigma_ref, prior_ref, *refs):
        x_refs, (noise_out, partial_ref, kept_ref, given_ref, cross_ref, var_ref, ridge_ref, old_ref, sems) = refs[:QUAD], refs[QUAD:]
        copies = []
        for slot in range(QUAD):
            start = pl.multiple_of((where_ref[1] ^ slot) * quarter, LANES)
            first = pl.multiple_of(where_ref[0] * width + start, LANES)
            pair = (
                pltpu.make_async_copy(coef_ref.at[:, pl.ds(first, quarter)], old_ref.at[slot], sems.at[2 * slot]),
                pltpu.make_async_copy(geno_ref.at[:, pl.ds(start, quarter)], x_refs[slot], sems.at[2 * slot + 1]),
            )
            for copy in pair:
                copy.start()
            copies.append(pair)
        start = pl.multiple_of(where_ref[1] * quarter, LANES)
        last = pltpu.make_async_copy(noise_ref.at[:, pl.ds(start, quarter)], noise_out, sems.at[2 * QUAD])
        last.start()
        noise_var = to_column(sigma_ref[...], traits)
        var_ref[...] = noise_var
        ridge_ref[...] = to_column(prior_ref[...], traits)
        fitted = jnp.zeros((traits, rows), F32)
        for slot in range(QUAD):
            for copy in copies[slot]:
                copy.wait()
            fitted += dot_t(old_ref[slot].astype(BF16), x_refs[slot][...])
        present = mask_ref[0:1]
        partial = present * (res_ref[...] + fitted)
        partial_ref[...] = partial
        target = (present * (partial + jnp.sqrt(noise_var) * people_ref[...])).astype(BF16)
        lines = traits * quarter // LANES
        cross_ref[:lines] = pack(dot(target, x_refs[1][...]), (), F32)
        cross_ref[lines:] = pack(dot(target, x_refs[3][...]), (), F32)
        given_ref[...] = pack(dot(target, x_refs[2][...]), (), F32)
        kept_ref[...] = pack(dot(target, x_refs[0][...]), (), F32)
        last.wait()

    lines = traits * quarter // LANES
    shape = jax.ShapeDtypeStruct
    out_shape = [shape((rows, quarter), BF16)] * QUAD + [
        shape((traits, quarter), F32),
        shape((traits, rows), F32),
        shape((lines, LANES), F32),
        shape((lines, LANES), F32),
        shape((2 * lines, LANES), F32),
        shape((traits, 1), F32),
        shape((traits, 1), F32),
    ]
    return pl.pallas_call(
        kernel,
        out_shape=out_shape,
        in_specs=[SMEM, ANY, ANY, ANY] + [VMEM] * 5,
        out_specs=[VMEM] * len(out_shape),
        scratch_shapes=[pltpu.VMEM((QUAD, traits, quarter), F32), pltpu.SemaphoreType.DMA((2 * QUAD + 1,))],
    )(where, genotypes, coef_all, noise_coef, residual, noise_people, mask, sigma2_old, prior_prec)


def image_part(search, direction, x):
    low = search.astype(BF16)
    wide = low.astype(F32)
    sums = [row_sum(search * search), row_sum(wide * wide)]
    if direction is not None:
        sums.append(row_sum(wide * direction))
    image = jnp.concatenate([dot_t(low, block) for block in x], axis=1)
    return pack(image, sums, F32), search, low


def first_search(got0, got1, got2, got3, noise_coef, noise_var, ridge, *x):
    traits, quarter = noise_coef.shape
    total, _ = unpack((got0 + got1) + (got2 + got3), traits, quarter)
    return image_part(total / noise_var + jnp.sqrt(ridge) * noise_coef, None, x)


def next_search(got0, got1, got2, got3, search, direction, image, before, norm, length, noise_var, ridge, *x):
    traits, quarter = search.shape
    opened = [unpack(got, traits, quarter, 1) for got in (got0, got1, got2, got3)]
    total = by_pairs([wide for wide, _ in opened])
    energy = by_pairs([columns[0] for _, columns in opened])
    step = norm / (energy / noise_var + ridge * length)
    search = search - step * (total / noise_var + ridge * direction)
    return *image_part(search, direction, x), before - step * image, step


def cross(packed, way, traits, rows):
    lines = traits * rows // LANES
    blocks = [packed[(slot ^ way) * lines : ((slot ^ way) + 1) * lines] for slot in range(QUAD)]
    return jnp.concatenate(blocks + [packed[QUAD * lines :]], axis=0)


def over_core(kind, count, traits, rows, sent, back):
    total = sent + cross(back, 1, traits, rows)
    if kind == F32:
        return (total,)
    wide, columns = unpack(total, traits, QUAD * rows, count)
    return (pack(wide, columns, kind),)


def new_image(count, sent, back, mask, low, direction, image, norm_old, length):
    traits = low.shape[0]
    rows = mask.shape[1]
    wide, columns = unpack(sent, traits, QUAD * rows, count)
    far, far_columns = unpack(cross(back, 2, traits, rows), traits, QUAD * rows, count)
    columns = [a + b for a, b in zip(columns, far_columns)]
    present = jnp.concatenate([mask[slot : slot + 1] for slot in range(QUAD)], axis=1)
    fresh = present * (wide + far)
    norm, low_low = columns[:2]
    wide = low.astype(F32)
    if direction is None:
        return fresh, wide, norm, low_low, jnp.zeros_like(norm)
    beta = norm / norm_old
    length = low_low + beta * (2.0 * columns[2] + beta * length)
    return fresh + beta * image, wide + beta * direction, norm, length, beta


def slots_of(wide, rows):
    return [wide[:, slot * rows : (slot + 1) * rows] for slot in range(QUAD)]


def people_part(kind, first, sent, back, mask, low, *rest):
    if first:
        state, x = new_image(2, sent, back, mask, low, None, None, None, None), rest
    else:
        state, x = new_image(3, sent, back, mask, low, *rest[:4]), rest[4:]
    rounded = state[0].astype(BF16)
    rows = mask.shape[1]
    energy = by_pairs([row_sum(part) for part in slots_of(state[0] * rounded.astype(F32), rows)])
    total = by_pairs([dot(part, block) for part, block in zip(slots_of(rounded, rows), x)])
    return pack(total, [energy], kind), *state


def last_sums(sent, back, mask, low, direction, image, norm_old, length, before):
    image, _, norm, length, beta = new_image(3, sent, back, mask, low, direction, image, norm_old, length)
    rows = mask.shape[1]
    products = (image * image.astype(BF16).astype(F32), before * before, before * image, image * image)
    sums = [to_row(by_pairs([row_sum(part) for part in slots_of(product, rows)])) for product in products]
    packed = jnp.concatenate(sums + [jnp.zeros((TILE - len(sums), LANES), F32)], axis=0)
    return packed, image[:, :rows], norm, length, beta


def finish(where, got, norm, length, noise_var, ridge, gamma, before, image, steps, betas, early, late, coef_all):
    traits, quarter = late[0].shape
    rows = image.shape[1]
    width = QUAD * quarter
    blocks = coef_all.shape[1] // width
    kept = ITERS - 1
    args = [*got, norm, length, noise_var, ridge, gamma, before, image, *steps, *betas, *early, *late]
    split = [len(got), 7, kept, kept, QUAD, QUAD]

    def kernel(where_ref, *refs):
        groups, at = [], 0
        for size in split:
            groups.append(refs[at : at + size])
            at += size
        coef_ref, out_ref, res_ref, sigma_ref, scratch, sems = refs[at:]
        block = where_ref[0]

        def hold(index):
            span = pl.ds(index * width, width)
            return pltpu.make_async_copy(coef_ref.at[:, span], out_ref.at[:, span], sems.at[index])

        def give(slot):
            start = pl.multiple_of(block * width + (where_ref[1] ^ slot) * quarter, LANES)
            return pltpu.make_async_copy(scratch.at[slot], out_ref.at[:, pl.ds(start, quarter)], sems.at[blocks + slot])

        for index in range(blocks):
            pl.when(block != index)(lambda index=index: hold(index).start())
        got, (norm, length, noise_var, ridge, gamma, before, image), steps, betas, early, late = groups
        total = by_pairs([ref[...] for ref in got]) if len(got) == QUAD else got[0][...]
        energy, squares, mixed, energy_full = (to_column(total[k : k + 1], traits) for k in range(4))
        step = norm[...] / (energy / noise_var[...] + ridge[...] * length[...])
        scale, mix = [], []
        for number in range(ITERS):
            mix = [betas[number - 1][...] * m for m in mix] + [jnp.ones_like(step)]
            now = steps[number][...] if number < kept else step
            scale = [s + now * m for s, m in zip(scale + [jnp.zeros_like(step)], mix)]
        for slot in range(QUAD):
            value = scale[kept] * late[slot][...].astype(F32)
            for k in range(kept):
                value += scale[k] * early[slot][k * traits : (k + 1) * traits].astype(F32)
            scratch[slot] = value
            give(slot).start()
        res_ref[...] = before[:, :rows] - step * image[...]
        squares = squares - step * (2.0 * mixed - step * energy_full)
        present = where_ref[2].astype(F32)
        row = to_row(squares + PRIOR_DOF * PRIOR_SCALE)[:, :traits]
        sigma_ref[...] = row / ((present + PRIOR_DOF) * gamma[...])
        for slot in range(QUAD):
            give(slot).wait()
        for index in range(blocks):
            pl.when(block != index)(lambda index=index: hold(index).wait())

    shape = jax.ShapeDtypeStruct
    return pl.pallas_call(
        kernel,
        out_shape=[shape(coef_all.shape, F32), shape((traits, rows), F32), shape((1, traits), F32)],
        in_specs=[SMEM] + [VMEM] * (len(args) + 1),
        out_specs=[ANY, VMEM, VMEM],
        scratch_shapes=[pltpu.VMEM((QUAD, traits, quarter), F32), pltpu.SemaphoreType.DMA((blocks + QUAD,))],
    )(where, *args, coef_all)


def per_device(
    count,
    genotypes,
    residual,
    noise_people,
    noise_coef,
    coef_all,
    block_index,
    prior_prec,
    sigma2_old,
    gamma_draw,
    valid_counts,
):
    rows, width = genotypes.shape
    traits = residual.shape[0]
    quarter = width // QUAD
    me = lax.axis_index("ppl")
    own = me & (QUAD - 1)

    def swap(x, distance):
        return lax.ppermute(x, "ppl", [(i, i ^ distance) for i in range(count)])

    def share(x):
        return [x] + [swap(x, slot) for slot in (1, 2, 3)]

    def over_z(x, columns):
        stride, kind = QUAD, x.dtype
        while True:
            got = [x] + [swap(x, way * stride) for way in (1, 2, 3)]
            stride *= 4
            if stride >= count:
                return got

            def add(*got):
                opened = [unpack(piece, traits, quarter, columns) for piece in got]
                sums = [by_pairs(list(column)) for column in zip(*(c for _, c in opened))]
                return (pack(by_pairs([wide for wide, _ in opened]), sums, kind),)

            if x.shape[0] == TILE:
                x = by_pairs(got)
            else:
                (x,) = fuse(add, *got)

    slots = jnp.arange(rows)
    quad = valid_counts[jnp.bitwise_xor(me, jnp.arange(QUAD))]
    mask = (slots[None, :] < quad[:, None]).astype(F32)
    where = jnp.stack([block_index[0], own, jnp.sum(valid_counts)]).astype(jnp.int32)
    made = prepare(
        where, genotypes, coef_all, noise_coef, residual, noise_people, mask, sigma2_old.reshape(1, -1), prior_prec.reshape(1, -1)
    )
    x_give, (noise_quarter, partial_res, kept, given, sent, noise_var, ridge) = made[:QUAD], made[QUAD:]
    lines = kept.shape[0]
    back = swap(sent, 1)
    given = given + back[lines:]
    given, x_give = lax.optimization_barrier((given, x_give))
    kept = kept + back[:lines] + swap(given, 2)
    x = [x_give[0]] + [swap(x_give[slot], slot) for slot in (1, 2, 3)]
    got = over_z(kept, 0)

    steps, betas, lows = [], [], []
    for number in range(ITERS):
        if number == 0:
            sent, search, low = fuse(first_search, *got, noise_quarter, noise_var, ridge, *x)
        else:
            sent, search, low, before, step = fuse(
                next_search, *got, search, direction, image, before, norm, length, noise_var, ridge, *x
            )
            steps.append(step)
        lows.append(low)
        (sent,) = fuse(functools.partial(over_core, IMAGE_KIND[number], 3 if number else 2, traits, rows), sent, swap(sent, 1))
        back = swap(sent, 2)
        if number == ITERS - 1:
            sent, image, norm, length, beta = fuse(last_sums, sent, back, mask, low, direction, image, norm, length, before)
            betas.append(beta)
            break
        state = (direction, image, norm, length) if number else ()
        sent, image, direction, norm, length, beta = fuse(
            functools.partial(people_part, PEOPLE_KIND[number], number == 0), sent, back, mask, low, *state, *x
        )
        if number:
            betas.append(beta)
        got = over_z(sent, 1)
        if number == 0:
            before = share(partial_res)
            got, before = lax.optimization_barrier((got, before))
            before = jnp.concatenate(before, axis=1)
        if number == ITERS - 2:
            early = share(jnp.concatenate(lows, axis=0))
            got, early = lax.optimization_barrier((got, early))

    late = share(low)
    got = over_z(sent, 4)
    coef_new, residual_new, sigma2_new = finish(
        where, got, norm, length, noise_var, ridge, gamma_draw.reshape(1, -1), before, image, steps, betas, early, late, coef_all
    )
    return (coef_new, residual_new, sigma2_new.reshape(-1))


def solution(mesh):
    return jax.shard_map(
        functools.partial(per_device, mesh.shape["ppl"]),
        mesh=mesh,
        in_specs=(
            P(("trait", "ppl"), None),
            P("trait", "ppl"),
            P("trait", "ppl"),
            P("trait", None),
            P("trait", None),
            P("trait"),
            P("trait"),
            P("trait"),
            P("trait"),
            P("trait"),
        ),
        out_specs=(P("trait", None), P("trait", "ppl"), P("trait")),
        check_vma=False,
    )
```

time: 538 us -> 158 us (0.29)
  waiting for transfers between devices: 457 us -> 54.8 us
  starting transfers between devices: 0.21 us -> 44.8 us
  Pallas kernels: 0 us -> 40.3 us
  blocking collectives: 31.9 us -> 0 us
  between operations: 15.5 us -> 1.56 us
  other arithmetic: 18.5 us -> 5.83 us
  matrix products: 10.1 us -> 0 us
  local copies, waits for them, and re-layouts: 3.54 us -> 10 us
    psum x5 -> x0, waiting for transfers between devices: 457 us -> none  [the longest x4 364 us: per_device(): local_sum = lax.psum(local_sum, 'ppl')]
    ppermute x0 -> x37, waiting for transfers between devices: none -> 54.8 us  [swap(): return lax.ppermute(x, 'ppl', [(i, i ^ distance) for i in range(count)])]
    ppermute x0 -> x37, starting transfers between devices: none -> 44.8 us  [swap(): return lax.ppermute(x, 'ppl', [(i, i ^ distance) for i in range(count)])]
    pallas_call x0 -> x14, Pallas kernels: none -> 40.3 us  [the longest x12 31.2 us: fuse(): pl.pallas_call(kernel, out_shape=shapes, in_specs=[VMEM] * len(args), out...]
    psum x1 -> x0, blocking collectives: 31.9 us -> none  [per_device(): squares = lax.psum(jnp.sum(residual_new * residual_new, axis=1), 'ppl')]
    reduce_sum x10 -> x1, other arithmetic: 12.5 us -> 1.29 us  [per_device(): jnp.sum(valid_counts)]
    dot_general x10 -> x0, matrix products: 10.1 us -> none  [the longest x4 5.14 us: per_device(): jnp.dot(image.astype(jnp.bfloat16), genotypes, preferred_element_type=jnp...]
  transfers between devices with their start and end apart: 5 -> 37, of which waited for: 5 -> 23; matrix products, arithmetic and copies ran while one was open for 0% -> 1% of each run, Pallas kernels for 0% -> 4%
where the time goes in v3:
time: 158 us; the launch traced here: 157 us
  waiting for transfers between devices  54.8 us (35%)
  starting transfers between devices  44.8 us (28%)
  Pallas kernels  40.3 us (26%)
  local copies, waits for them, and re-layouts  10 us (6%)
  other arithmetic  5.83 us (4%)
    ppermute x37, waiting for transfers between devices, swap(): return lax.ppermute(x, 'ppl', [(i, i ^ distance) for i in range(count)])  54.8 us
    ppermute x37, starting transfers between devices, swap(): return lax.ppermute(x, 'ppl', [(i, i ^ distance) for i in range(count)])  44.8 us
    pallas_call x12, Pallas kernels, fuse(): pl.pallas_call(kernel, out_shape=shapes, in_specs=[VMEM] * len(args), out...  31.2 us
    unnamed x76, local copies, waits for them, and re-layouts  7.87 us
    pallas_call x1, Pallas kernels, prepare(): pl.pallas_call(kernel, out_shape=out_shape, in_specs=[SMEM, ANY, ANY, ANY...  5.46 us
    pallas_call x1, Pallas kernels, finish(): pl.pallas_call(kernel, out_shape=[shape(coef_all.shape, F32), shape((trai...  3.65 us
  transfers between devices with their start and end apart: 37, of which 23 were waited for; matrix products, arithmetic and copies ran while one was open for 1% of the time, Pallas kernels for 4%

profile of v3, /device:TPU:0, one launch (start us, length us, event | category | flops | bytes accessed | tf_op | source)
XLA Modules:
  0.0 157.4 jit_solution(3029712332386844117)
XLA Ops:
  5.9 5.5 %shard_map.121 = (bf16[256,1024]{1,0:T(8,128)(2,1)}, bf16[256,1024]{1,0:T(8,128)(2,1)}, bf16[256,1024]{1,0:T(8,128)(2,1)}, bf16[256,1024]{1,0:T(8,128)(2,1)}, f3...) custom-call(s32[3]{0:T(128)} %pad_add_fusion.where_ref, ...), custom_call_target="tpu_custom_call" | custom-call | tf_op jit(solution)/shard_map/pallas_call | solution.py:150
  14.2 2.9 %collective-permute-start.1 = (f32[256,128]{1,0:T(8,128)S(1)}, f32[256,128]{1,0:T(8,128)S(1)}, u32[]{:S(2)}, u32[]{:S(2)}) collective-permute-start(f32[256,128]{1,0:T(8,128)S(1)} %slice_add_fusion), channel_id=1, source_target_pairs={{0,2},{1,3},{2,0},{3,1},{4,6},{5,7},{6,4},{7,5},{8,10},{9,11},{10,... | collective-permute-start | bytes 393224 | tf_op jit(solution)/shard_map/ppermute | solution.py:323
  19.0 2.4 %collective-permute-done.1 = f32[256,128]{1,0:T(8,128)S(1)} collective-permute-done((f32[256,128]{1,0:T(8,128)S(1)}, f32[256,128]{1,0:T(8,128)S(1)}, u32[]{:S(2)}, u32[]{:S(2)}) %collective-permute-start.1) | collective-permute-done | bytes 131104 | tf_op jit(solution)/shard_map/ppermute | solution.py:323
  22.3 4.1 %collective-permute-start.4 = (f32[256,128]{1,0:T(8,128)S(1)}, f32[256,128]{1,0:T(8,128)S(1)}, u32[]{:S(2)}, u32[]{:S(2)}) collective-permute-start(f32[256,128]{1,0:T(8,128)S(1)} %fusion.refs_0_), channel_id=1, source_target_pairs={{0,12},{1,13},{2,14},{3,15},{4,8},{5,9},{6,10},{7,11},{8,4},{9,5},... | collective-permute-start | bytes 393224 | tf_op jit(solution)/shard_map/ppermute | solution.py:323
  26.5 3.7 %collective-permute-done.4.refs_3_ = f32[256,128]{1,0:T(8,128)S(1)} collective-permute-done((f32[256,128]{1,0:T(8,128)S(1)}, f32[256,128]{1,0:T(8,128)S(1)}, u32[]{:S(2)}, u32[]{:S(2)}) %collective-permute-start.4) | collective-permute-done | bytes 131104 | tf_op jit(solution)/shard_map/ppermute | solution.py:323
  30.2 4.8 %collective-permute-start.2 = (f32[256,128]{1,0:T(8,128)S(1)}, f32[256,128]{1,0:T(8,128)S(1)}, u32[]{:S(2)}, u32[]{:S(2)}) collective-permute-start(f32[256,128]{1,0:T(8,128)S(1)} %fusion.refs_0_), channel_id=1, source_target_pairs={{0,4},{1,5},{2,6},{3,7},{4,0},{5,1},{6,2},{7,3},{8,12},{9,13},{10,... | collective-permute-start | bytes 393224 | tf_op jit(solution)/shard_map/ppermute | solution.py:323
  36.4 2.5 %collective-permute-done.2.refs_1_ = f32[256,128]{1,0:T(8,128)S(1)} collective-permute-done((f32[256,128]{1,0:T(8,128)S(1)}, f32[256,128]{1,0:T(8,128)S(1)}, u32[]{:S(2)}, u32[]{:S(2)}) %collective-permute-start.2) | collective-permute-done | bytes 131104 | tf_op jit(solution)/shard_map/ppermute | solution.py:323
  38.9 4.0 %collective-permute-done.7.refs_10_.refs_7_.refs_15_.refs_11_ = bf16[256,1024]{1,0:T(8,128)(2,1)S(1)} collective-permute-done((bf16[256,1024]{1,0:T(8,128)(2,1)}, bf16[256,1024]{1,0:T(8,128)(2,1)S(1)}, u32[]{:S(2)}, u32[]{:S(2)}) %collective-permute-start.7) | collective-permute-done | bytes 524320 | tf_op jit(solution)/shard_map/ppermute | solution.py:323
  43.7 3.2 %shard_map.122 = (f32[264,128]{1,0:T(8,128)}, f32[32,1024]{1,0:T(8,128)}, bf16[32,1024]{1,0:T(8,128)(2,1)}) custom-call(f32[256,128]{1,0:T(8,128)} %copy-done.3, f32[256,128]{1,0:T(8,128)} %copy-done.20, f32[256,128]{1,0:T(8,128)} %copy-done.19, f32[256,128]{1,0:T(8,128)} %copy-done.18, f32[32,1024]{1,0:T(8,128)} %get-tuple-element.85.refs_4_, ...), custom_call_target="tpu_custom_call" | custom-call | tf_op jit(solution)/shard_map/pallas_call | solution.py:96
  52.4 4.3 %collective-permute-done.9.refs_1_ = f32[264,128]{1,0:T(8,128)S(1)} collective-permute-done((f32[264,128]{1,0:T(8,128)}, f32[264,128]{1,0:T(8,128)S(1)}, u32[]{:S(2)}, u32[]{:S(2)}) %collective-permute-start.9) | collective-permute-done | bytes 135200 | tf_op jit(solution)/shard_map/ppermute | solution.py:323
  57.4 2.8 %shard_map.124 = (f32[264,128]{1,0:T(8,128)}, f32[32,1024]{1,0:T(8,128)}, f32[32,1024]{1,0:T(8,128)}, f32[32,1]{1,0:T(8,128)}, f32[32,1]{1,0:T(8,128)}, /*index=5*/f32[32,1]{1,0:T(8,128)}) custom-call(f32[264,128]{1,0:T(8,128)} %shard_map.123.refs_0_, f32[264,128]{1,0:T(8,128)} %copy-done.13, f32[4,256]{1,0:T(4,128)} %fusion.1.mask_ref.refs_2_, ...), custom_call_target="tpu_custom_call" | custom-call | tf_op jit(solution)/shard_map/pallas_call | solution.py:96
  60.2 3.9 %collective-permute-start.12 = (f32[264,128]{1,0:T(8,128)}, f32[264,128]{1,0:T(8,128)S(1)}, u32[]{:S(2)}, u32[]{:S(2)}) collective-permute-start(f32[264,128]{1,0:T(8,128)} %get-tuple-element.96.refs_0_), channel_id=1, source_target_pairs={{0,12},{1,13},{2,14},{3,15},{4,8},{5,9},{6,10},{7,11},{8,4},{9,5},... | collective-permute-start | bytes 405512 | tf_op jit(solution)/shard_map/ppermute | solution.py:323
  66.4 1.8 %collective-permute-done.15 = f32[32,256]{1,0:T(8,128)S(1)} collective-permute-done((f32[32,256]{1,0:T(8,128)S(1)}, f32[32,256]{1,0:T(8,128)S(1)}, u32[]{:S(2)}, u32[]{:S(2)}) %collective-permute-start.15) | collective-permute-done | bytes 32800 | tf_op jit(solution)/shard_map/ppermute | solution.py:323
  69.4 6.0 %collective-permute-done.11.refs_2_ = f32[264,128]{1,0:T(8,128)S(1)} collective-permute-done((f32[264,128]{1,0:T(8,128)}, f32[264,128]{1,0:T(8,128)S(1)}, u32[]{:S(2)}, u32[]{:S(2)}) %collective-permute-start.11) | collective-permute-done | bytes 135200 | tf_op jit(solution)/shard_map/ppermute | solution.py:323
  76.2 3.5 %shard_map.125 = (f32[264,128]{1,0:T(8,128)}, f32[32,1024]{1,0:T(8,128)}, bf16[32,1024]{1,0:T(8,128)(2,1)}, f32[32,1024]{1,0:T(8,128)}, f32[32,1]{1,0:T(8,128)}) custom-call(f32[264,128]{1,0:T(8,128)} %get-tuple-element.96.refs_0_, f32[264,128]{1,0:T(8,128)} %copy-done.12, f32[264,128]{1,0:T(8,128)} %copy-done.11, f32[264,128]{1,0:T(8,128)} %copy-done.10, ...), custom_call_target="tpu_custom_call" | custom-call | tf_op jit(solution)/shard_map/pallas_call | solution.py:96
  85.2 3.0 %collective-permute-done.17.refs_1_ = bf16[272,128]{1,0:T(8,128)(2,1)S(1)} collective-permute-done((bf16[272,128]{1,0:T(8,128)(2,1)}, bf16[272,128]{1,0:T(8,128)(2,1)S(1)}, u32[]{:S(2)}, u32[]{:S(2)}) %collective-permute-start.17) | collective-permute-done | bytes 69664 | tf_op jit(solution)/shard_map/ppermute | solution.py:323
  88.9 3.0 %shard_map.127 = (bf16[264,128]{1,0:T(8,128)(2,1)}, f32[32,1024]{1,0:T(8,128)}, f32[32,1024]{1,0:T(8,128)}, f32[32,1]{1,0:T(8,128)}, f32[32,1]{1,0:T(8,128)}, /*index=5*/f32[32,1]{1,0:T(8,128)}) custom-call(bf16[272,128]{1,0:T(8,128)(2,1)} %shard_map.126.refs_0_, bf16[272,128]{1,0:T(8,128)(2,1)} %copy-done.22, f32[4,256]{1,0:T(4,128)} %fusion.1.mask_ref.refs_2_, ...), custom_call_target="tpu_custom_call" | custom-call | tf_op jit(solution)/shard_map/pallas_call | solution.py:96
  91.8 2.5 %collective-permute-start.20 = (bf16[264,128]{1,0:T(8,128)(2,1)}, bf16[264,128]{1,0:T(8,128)(2,1)S(1)}, u32[]{:S(2)}, u32[]{:S(2)}) collective-permute-start(bf16[264,128]{1,0:T(8,128)(2,1)} %get-tuple-element.111.refs_0_), channel_id=1, source_target_pairs={{0,12},{1,13},{2,14},{3,15},{4,8},{5,9},{6,10},{7,11},{8,4},{9,5},... | collective-permute-start | bytes 202760 | tf_op jit(solution)/shard_map/ppermute | solution.py:323
  94.4 1.9 %collective-permute-start.18 = (bf16[264,128]{1,0:T(8,128)(2,1)}, bf16[264,128]{1,0:T(8,128)(2,1)S(1)}, u32[]{:S(2)}, u32[]{:S(2)}) collective-permute-start(bf16[264,128]{1,0:T(8,128)(2,1)} %get-tuple-element.111.refs_0_), channel_id=1, source_target_pairs={{0,4},{1,5},{2,6},{3,7},{4,0},{5,1},{6,2},{7,3},{8,12},{9,13},{10,... | collective-permute-start | bytes 202760 | tf_op jit(solution)/shard_map/ppermute | solution.py:323
  96.3 2.1 %collective-permute-done.20.refs_3_ = bf16[264,128]{1,0:T(8,128)(2,1)S(1)} collective-permute-done((bf16[264,128]{1,0:T(8,128)(2,1)}, bf16[264,128]{1,0:T(8,128)(2,1)S(1)}, u32[]{:S(2)}, u32[]{:S(2)}) %collective-permute-start.20) | collective-permute-done | bytes 67616 | tf_op jit(solution)/shard_map/ppermute | solution.py:323
  100.9 3.4 %shard_map.128 = (f32[264,128]{1,0:T(8,128)}, f32[32,1024]{1,0:T(8,128)}, bf16[32,1024]{1,0:T(8,128)(2,1)}, f32[32,1024]{1,0:T(8,128)}, f32[32,1]{1,0:T(8,128)}) custom-call(bf16[264,128]{1,0:T(8,128)(2,1)} %get-tuple-element.111.refs_0_, bf16[264,128]{1,0:T(8,128)(2,1)} %copy-done.29, bf16[264,128]{1,0:T(8,128)(2,1)} %copy-done.28, ...), custom_call_target="tpu_custom_call" | custom-call | tf_op jit(solution)/shard_map/pallas_call | solution.py:96
  111.2 6.9 %collective-permute-done.22.refs_1_ = bf16[272,128]{1,0:T(8,128)(2,1)S(1)} collective-permute-done((bf16[272,128]{1,0:T(8,128)(2,1)}, bf16[272,128]{1,0:T(8,128)(2,1)S(1)}, u32[]{:S(2)}, u32[]{:S(2)}) %collective-permute-start.22) | collective-permute-done | bytes 69664 | tf_op jit(solution)/shard_map/ppermute | solution.py:323
  118.7 3.0 %shard_map.130 = (bf16[264,128]{1,0:T(8,128)(2,1)}, f32[32,1024]{1,0:T(8,128)}, f32[32,1024]{1,0:T(8,128)}, f32[32,1]{1,0:T(8,128)}, f32[32,1]{1,0:T(8,128)}, /*index=5*/f32[32,1]{1,0:T(8,128)}) custom-call(bf16[272,128]{1,0:T(8,128)(2,1)} %shard_map.129.refs_0_, bf16[272,128]{1,0:T(8,128)(2,1)} %copy-done.23, f32[4,256]{1,0:T(4,128)} %fusion.1.mask_ref.refs_2_, ...), custom_call_target="tpu_custom_call" | custom-call | tf_op jit(solution)/shard_map/pallas_call | solution.py:96
  121.7 2.2 %collective-permute-start.25 = (bf16[264,128]{1,0:T(8,128)(2,1)}, bf16[264,128]{1,0:T(8,128)(2,1)S(1)}, u32[]{:S(2)}, u32[]{:S(2)}) collective-permute-start(bf16[264,128]{1,0:T(8,128)(2,1)} %get-tuple-element.121.refs_0_), channel_id=1, source_target_pairs={{0,12},{1,13},{2,14},{3,15},{4,8},{5,9},{6,10},{7,11},{8,4},{9,5},... | collective-permute-start | bytes 202760 | tf_op jit(solution)/shard_map/ppermute | solution.py:323
  124.0 2.2 %collective-permute-start.23 = (bf16[264,128]{1,0:T(8,128)(2,1)}, bf16[264,128]{1,0:T(8,128)(2,1)S(1)}, u32[]{:S(2)}, u32[]{:S(2)}) collective-permute-start(bf16[264,128]{1,0:T(8,128)(2,1)} %get-tuple-element.121.refs_0_), channel_id=1, source_target_pairs={{0,4},{1,5},{2,6},{3,7},{4,0},{5,1},{6,2},{7,3},{8,12},{9,13},{10,... | collective-permute-start | bytes 202760 | tf_op jit(solution)/shard_map/ppermute | solution.py:323
  126.2 2.0 %collective-permute-done.25.refs_3_ = bf16[264,128]{1,0:T(8,128)(2,1)S(1)} collective-permute-done((bf16[264,128]{1,0:T(8,128)(2,1)}, bf16[264,128]{1,0:T(8,128)(2,1)S(1)}, u32[]{:S(2)}, u32[]{:S(2)}) %collective-permute-start.25) | collective-permute-done | bytes 67616 | tf_op jit(solution)/shard_map/ppermute | solution.py:323
  128.2 2.4 %collective-permute-done.24.refs_2_ = bf16[264,128]{1,0:T(8,128)(2,1)S(1)} collective-permute-done((bf16[264,128]{1,0:T(8,128)(2,1)}, bf16[264,128]{1,0:T(8,128)(2,1)S(1)}, u32[]{:S(2)}, u32[]{:S(2)}) %collective-permute-start.24) | collective-permute-done | bytes 67616 | tf_op jit(solution)/shard_map/ppermute | solution.py:323
  131.3 3.4 %shard_map.131 = (f32[264,128]{1,0:T(8,128)}, f32[32,1024]{1,0:T(8,128)}, bf16[32,1024]{1,0:T(8,128)(2,1)}, f32[32,1024]{1,0:T(8,128)}, f32[32,1]{1,0:T(8,128)}) custom-call(bf16[264,128]{1,0:T(8,128)(2,1)} %get-tuple-element.121.refs_0_, bf16[264,128]{1,0:T(8,128)(2,1)} %copy-done.26, bf16[264,128]{1,0:T(8,128)(2,1)} %copy-done.25, ...), custom_call_target="tpu_custom_call" | custom-call | tf_op jit(solution)/shard_map/pallas_call | solution.py:96
  143.9 2.1 %shard_map.133 = (f32[8,128]{1,0:T(8,128)}, f32[32,256]{1,0:T(8,128)}, f32[32,1]{1,0:T(8,128)}, f32[32,1]{1,0:T(8,128)}, f32[32,1]{1,0:T(8,128)}) custom-call(bf16[272,128]{1,0:T(8,128)(2,1)} %shard_map.132.refs_0_, bf16[272,128]{1,0:T(8,128)(2,1)} %copy-done.21, f32[4,256]{1,0:T(4,128)} %fusion.1.mask_ref.refs_2_, ...), custom_call_target="tpu_custom_call" | custom-call | tf_op jit(solution)/shard_map/pallas_call | solution.py:96
  146.0 2.4 %collective-permute-start.33 = (f32[8,128]{1,0:T(8,128)}, f32[8,128]{1,0:T(8,128)S(1)}, u32[]{:S(2)}, u32[]{:S(2)}) collective-permute-start(f32[8,128]{1,0:T(8,128)} %get-tuple-element.134.refs_0_), channel_id=1, source_target_pairs={{0,12},{1,13},{2,14},{3,15},{4,8},{5,9},{6,10},{7,11},{8,4},{9,5},... | collective-permute-start | bytes 12296 | tf_op jit(solution)/shard_map/ppermute | solution.py:323
  148.4 2.0 %collective-permute-start.31 = (f32[8,128]{1,0:T(8,128)}, f32[8,128]{1,0:T(8,128)S(1)}, u32[]{:S(2)}, u32[]{:S(2)}) collective-permute-start(f32[8,128]{1,0:T(8,128)} %get-tuple-element.134.refs_0_), channel_id=1, source_target_pairs={{0,4},{1,5},{2,6},{3,7},{4,0},{5,1},{6,2},{7,3},{8,12},{9,13},{10,... | collective-permute-start | bytes 12296 | tf_op jit(solution)/shard_map/ppermute | solution.py:323
  153.7 3.7 %shard_map.134 = (f32[32,8192]{1,0:T(8,128)}, f32[32,256]{1,0:T(8,128)}, f32[1,32]{1,0:T(1,128)}) custom-call(s32[3]{0:T(128)} %pad_add_fusion.where_ref, f32[8,128]{1,0:T(8,128)} %get-tuple-element.134.refs_0_, f32[8,128]{1,0:T(8,128)} %copy-done.36, f32[8,128]{1,0:T(8,128)} %copy-done.35, f32[8,128]{1,0:T(8,128)} %copy-done.34, ...), custom_call_target="tpu_custom_call" | custom-call | tf_op jit(solution)/shard_map/pallas_call | solution.py:294
  (142 shorter events, 52.0 us)
Async XLA Ops:
  14.2 7.2 %collective-permute-start.1 = (f32[256,128]{1,0:T(8,128)S(1)}, f32[256,128]{1,0:T(8,128)S(1)}, u32[]{:S(2)}, u32[]{:S(2)}) collective-permute-start(f32[256,128]{1,0:T(8,128)S(1)} %slice_add_fusion), channel_id=1, source_target_pairs={{0,2},{1,3},{2,0},{3,1},{4,6},{5,7},{6,4},{7,5},{8,10},{9,11},{10,... | collective-permute-start | bytes 393224 | tf_op jit(solution)/shard_map/ppermute | solution.py:323
  17.1 21.8 %collective-permute-start.5 = (bf16[256,1024]{1,0:T(8,128)(2,1)}, bf16[256,1024]{1,0:T(8,128)(2,1)S(1)}, u32[]{:S(2)}, u32[]{:S(2)}) collective-permute-start(bf16[256,1024]{1,0:T(8,128)(2,1)} %get-tuple-element.89), channel_id=1, source_target_pairs={{0,1},{1,0},{2,3},{3,2},{4,5},{5,4},{6,7},{7,6},{8,9},{9,8},{10,11... | collective-permute-start | bytes 1572872 | tf_op jit(solution)/shard_map/ppermute | solution.py:323
  17.1 21.8 %collective-permute-start.6 = (bf16[256,1024]{1,0:T(8,128)(2,1)}, bf16[256,1024]{1,0:T(8,128)(2,1)S(1)}, u32[]{:S(2)}, u32[]{:S(2)}) collective-permute-start(bf16[256,1024]{1,0:T(8,128)(2,1)} %get-tuple-element.90), channel_id=1, source_target_pairs={{0,2},{1,3},{2,0},{3,1},{4,6},{5,7},{6,4},{7,5},{8,10},{9,11},{10,... | collective-permute-start | bytes 1572872 | tf_op jit(solution)/shard_map/ppermute | solution.py:323
  17.3 25.6 %collective-permute-start.7 = (bf16[256,1024]{1,0:T(8,128)(2,1)}, bf16[256,1024]{1,0:T(8,128)(2,1)S(1)}, u32[]{:S(2)}, u32[]{:S(2)}) collective-permute-start(bf16[256,1024]{1,0:T(8,128)(2,1)} %get-tuple-element.91), channel_id=1, source_target_pairs={{0,3},{1,2},{2,1},{3,0},{4,7},{5,6},{6,5},{7,4},{8,11},{9,10},{10,... | collective-permute-start | bytes 1572872 | tf_op jit(solution)/shard_map/ppermute | solution.py:323
  22.3 7.9 %collective-permute-start.4 = (f32[256,128]{1,0:T(8,128)S(1)}, f32[256,128]{1,0:T(8,128)S(1)}, u32[]{:S(2)}, u32[]{:S(2)}) collective-permute-start(f32[256,128]{1,0:T(8,128)S(1)} %fusion.refs_0_), channel_id=1, source_target_pairs={{0,12},{1,13},{2,14},{3,15},{4,8},{5,9},{6,10},{7,11},{8,4},{9,5},... | collective-permute-start | bytes 393224 | tf_op jit(solution)/shard_map/ppermute | solution.py:323
  26.4 9.9 %collective-permute-start.3 = (f32[256,128]{1,0:T(8,128)S(1)}, f32[256,128]{1,0:T(8,128)S(1)}, u32[]{:S(2)}, u32[]{:S(2)}) collective-permute-start(f32[256,128]{1,0:T(8,128)S(1)} %fusion.refs_0_), channel_id=1, source_target_pairs={{0,8},{1,9},{2,10},{3,11},{4,12},{5,13},{6,14},{7,15},{8,0},{9,1},... | collective-permute-start | bytes 393224 | tf_op jit(solution)/shard_map/ppermute | solution.py:323
  30.2 8.7 %collective-permute-start.2 = (f32[256,128]{1,0:T(8,128)S(1)}, f32[256,128]{1,0:T(8,128)S(1)}, u32[]{:S(2)}, u32[]{:S(2)}) collective-permute-start(f32[256,128]{1,0:T(8,128)S(1)} %fusion.refs_0_), channel_id=1, source_target_pairs={{0,4},{1,5},{2,6},{3,7},{4,0},{5,1},{6,2},{7,3},{8,12},{9,13},{10,... | collective-permute-start | bytes 393224 | tf_op jit(solution)/shard_map/ppermute | solution.py:323
  50.8 6.0 %collective-permute-start.9 = (f32[264,128]{1,0:T(8,128)}, f32[264,128]{1,0:T(8,128)S(1)}, u32[]{:S(2)}, u32[]{:S(2)}) collective-permute-start(f32[264,128]{1,0:T(8,128)} %shard_map.123.refs_0_), channel_id=1, source_target_pairs={{0,2},{1,3},{2,0},{3,1},{4,6},{5,7},{6,4},{7,5},{8,10},{9,11},{10,... | collective-permute-start | bytes 405512 | tf_op jit(solution)/shard_map/ppermute | solution.py:323
  60.2 9.2 %collective-permute-start.12 = (f32[264,128]{1,0:T(8,128)}, f32[264,128]{1,0:T(8,128)S(1)}, u32[]{:S(2)}, u32[]{:S(2)}) collective-permute-start(f32[264,128]{1,0:T(8,128)} %get-tuple-element.96.refs_0_), channel_id=1, source_target_pairs={{0,12},{1,13},{2,14},{3,15},{4,8},{5,9},{6,10},{7,11},{8,4},{9,5},... | collective-permute-start | bytes 405512 | tf_op jit(solution)/shard_map/ppermute | solution.py:323
  64.1 11.3 %collective-permute-start.11 = (f32[264,128]{1,0:T(8,128)}, f32[264,128]{1,0:T(8,128)S(1)}, u32[]{:S(2)}, u32[]{:S(2)}) collective-permute-start(f32[264,128]{1,0:T(8,128)} %get-tuple-element.96.refs_0_), channel_id=1, source_target_pairs={{0,8},{1,9},{2,10},{3,11},{4,12},{5,13},{6,14},{7,15},{8,0},{9,1},... | collective-permute-start | bytes 405512 | tf_op jit(solution)/shard_map/ppermute | solution.py:323
  64.1 11.3 %collective-permute-start.10 = (f32[264,128]{1,0:T(8,128)}, f32[264,128]{1,0:T(8,128)S(1)}, u32[]{:S(2)}, u32[]{:S(2)}) collective-permute-start(f32[264,128]{1,0:T(8,128)} %get-tuple-element.96.refs_0_), channel_id=1, source_target_pairs={{0,4},{1,5},{2,6},{3,7},{4,0},{5,1},{6,2},{7,3},{8,12},{9,13},{10,... | collective-permute-start | bytes 405512 | tf_op jit(solution)/shard_map/ppermute | solution.py:323
  64.8 3.5 %collective-permute-start.15 = (f32[32,256]{1,0:T(8,128)S(1)}, f32[32,256]{1,0:T(8,128)S(1)}, u32[]{:S(2)}, u32[]{:S(2)}) collective-permute-start(f32[32,256]{1,0:T(8,128)S(1)} %copy-done.33), channel_id=1, source_target_pairs={{0,3},{1,2},{2,1},{3,0},{4,7},{5,6},{6,5},{7,4},{8,11},{9,10},{10,... | collective-permute-start | bytes 98312 | tf_op jit(solution)/shard_map/ppermute | solution.py:323
  64.8 4.0 %collective-permute-start.14 = (f32[32,256]{1,0:T(8,128)S(1)}, f32[32,256]{1,0:T(8,128)S(1)}, u32[]{:S(2)}, u32[]{:S(2)}) collective-permute-start(f32[32,256]{1,0:T(8,128)S(1)} %copy-done.33), channel_id=1, source_target_pairs={{0,2},{1,3},{2,0},{3,1},{4,6},{5,7},{6,4},{7,5},{8,10},{9,11},{10,... | collective-permute-start | bytes 98312 | tf_op jit(solution)/shard_map/ppermute | solution.py:323
  83.7 4.5 %collective-permute-start.17 = (bf16[272,128]{1,0:T(8,128)(2,1)}, bf16[272,128]{1,0:T(8,128)(2,1)S(1)}, u32[]{:S(2)}, u32[]{:S(2)}) collective-permute-start(bf16[272,128]{1,0:T(8,128)(2,1)} %shard_map.126.refs_0_), channel_id=1, source_target_pairs={{0,2},{1,3},{2,0},{3,1},{4,6},{5,7},{6,4},{7,5},{8,10},{9,11},{10,... | collective-permute-start | bytes 208904 | tf_op jit(solution)/shard_map/ppermute | solution.py:323
  91.8 6.6 %collective-permute-start.20 = (bf16[264,128]{1,0:T(8,128)(2,1)}, bf16[264,128]{1,0:T(8,128)(2,1)S(1)}, u32[]{:S(2)}, u32[]{:S(2)}) collective-permute-start(bf16[264,128]{1,0:T(8,128)(2,1)} %get-tuple-element.111.refs_0_), channel_id=1, source_target_pairs={{0,12},{1,13},{2,14},{3,15},{4,8},{5,9},{6,10},{7,11},{8,4},{9,5},... | collective-permute-start | bytes 202760 | tf_op jit(solution)/shard_map/ppermute | solution.py:323
  94.4 5.8 %collective-permute-start.19 = (bf16[264,128]{1,0:T(8,128)(2,1)}, bf16[264,128]{1,0:T(8,128)(2,1)S(1)}, u32[]{:S(2)}, u32[]{:S(2)}) collective-permute-start(bf16[264,128]{1,0:T(8,128)(2,1)} %get-tuple-element.111.refs_0_), channel_id=1, source_target_pairs={{0,8},{1,9},{2,10},{3,11},{4,12},{5,13},{6,14},{7,15},{8,0},{9,1},... | collective-permute-start | bytes 202760 | tf_op jit(solution)/shard_map/ppermute | solution.py:323
  94.4 5.8 %collective-permute-start.18 = (bf16[264,128]{1,0:T(8,128)(2,1)}, bf16[264,128]{1,0:T(8,128)(2,1)S(1)}, u32[]{:S(2)}, u32[]{:S(2)}) collective-permute-start(bf16[264,128]{1,0:T(8,128)(2,1)} %get-tuple-element.111.refs_0_), channel_id=1, source_target_pairs={{0,4},{1,5},{2,6},{3,7},{4,0},{5,1},{6,2},{7,3},{8,12},{9,13},{10,... | collective-permute-start | bytes 202760 | tf_op jit(solution)/shard_map/ppermute | solution.py:323
  104.3 3.1 %collective-permute-start.21 = (f32[264,128]{1,0:T(8,128)}, f32[264,128]{1,0:T(8,128)S(1)}, u32[]{:S(2)}, u32[]{:S(2)}) collective-permute-start(f32[264,128]{1,0:T(8,128)} %get-tuple-element.118.refs_0_), channel_id=1, source_target_pairs={{0,1},{1,0},{2,3},{3,2},{4,5},{5,4},{6,7},{7,6},{8,9},{9,8},{10,11... | collective-permute-start | bytes 405512 | tf_op jit(solution)/shard_map/ppermute | solution.py:323
  105.2 18.7 %collective-permute-start.28 = (bf16[96,1024]{1,0:T(8,128)(2,1)S(1)}, bf16[96,1024]{1,0:T(8,128)(2,1)S(1)}, u32[]{:S(2)}, u32[]{:S(2)}) collective-permute-start(bf16[96,1024]{1,0:T(8,128)(2,1)S(1)} %constant_dynamic-update-slice_fusion.refs_17_), channel_id=1, source_target_pairs={{0,3},{1,2},{2,1},{3,0},{4,7},{5,6},{6,5},{7,4},{8,11},{9,10},{10,... | collective-permute-start | bytes 589832 | tf_op jit(solution)/shard_map/ppermute | solution.py:323
  106.8 19.4 %collective-permute-start.27 = (bf16[96,1024]{1,0:T(8,128)(2,1)S(1)}, bf16[96,1024]{1,0:T(8,128)(2,1)S(1)}, u32[]{:S(2)}, u32[]{:S(2)}) collective-permute-start(bf16[96,1024]{1,0:T(8,128)(2,1)S(1)} %constant_dynamic-update-slice_fusion.refs_17_), channel_id=1, source_target_pairs={{0,2},{1,3},{2,0},{3,1},{4,6},{5,7},{6,4},{7,5},{8,10},{9,11},{10,... | collective-permute-start | bytes 589832 | tf_op jit(solution)/shard_map/ppermute | solution.py:323
  107.3 18.9 %collective-permute-start.26 = (bf16[96,1024]{1,0:T(8,128)(2,1)S(1)}, bf16[96,1024]{1,0:T(8,128)(2,1)S(1)}, u32[]{:S(2)}, u32[]{:S(2)}) collective-permute-start(bf16[96,1024]{1,0:T(8,128)(2,1)S(1)} %constant_dynamic-update-slice_fusion.refs_17_), channel_id=1, source_target_pairs={{0,1},{1,0},{2,3},{3,2},{4,5},{5,4},{6,7},{7,6},{8,9},{9,8},{10,11... | collective-permute-start | bytes 589832 | tf_op jit(solution)/shard_map/ppermute | solution.py:323
  109.7 8.4 %collective-permute-start.22 = (bf16[272,128]{1,0:T(8,128)(2,1)}, bf16[272,128]{1,0:T(8,128)(2,1)S(1)}, u32[]{:S(2)}, u32[]{:S(2)}) collective-permute-start(bf16[272,128]{1,0:T(8,128)(2,1)} %shard_map.129.refs_0_), channel_id=1, source_target_pairs={{0,2},{1,3},{2,0},{3,1},{4,6},{5,7},{6,4},{7,5},{8,10},{9,11},{10,... | collective-permute-start | bytes 208904 | tf_op jit(solution)/shard_map/ppermute | solution.py:323
  121.7 6.5 %collective-permute-start.25 = (bf16[264,128]{1,0:T(8,128)(2,1)}, bf16[264,128]{1,0:T(8,128)(2,1)S(1)}, u32[]{:S(2)}, u32[]{:S(2)}) collective-permute-start(bf16[264,128]{1,0:T(8,128)(2,1)} %get-tuple-element.121.refs_0_), channel_id=1, source_target_pairs={{0,12},{1,13},{2,14},{3,15},{4,8},{5,9},{6,10},{7,11},{8,4},{9,5},... | collective-permute-start | bytes 202760 | tf_op jit(solution)/shard_map/ppermute | solution.py:323
  123.9 6.7 %collective-permute-start.24 = (bf16[264,128]{1,0:T(8,128)(2,1)}, bf16[264,128]{1,0:T(8,128)(2,1)S(1)}, u32[]{:S(2)}, u32[]{:S(2)}) collective-permute-start(bf16[264,128]{1,0:T(8,128)(2,1)} %get-tuple-element.121.refs_0_), channel_id=1, source_target_pairs={{0,8},{1,9},{2,10},{3,11},{4,12},{5,13},{6,14},{7,15},{8,0},{9,1},... | collective-permute-start | bytes 202760 | tf_op jit(solution)/shard_map/ppermute | solution.py:323
  124.0 6.7 %collective-permute-start.23 = (bf16[264,128]{1,0:T(8,128)(2,1)}, bf16[264,128]{1,0:T(8,128)(2,1)S(1)}, u32[]{:S(2)}, u32[]{:S(2)}) collective-permute-start(bf16[264,128]{1,0:T(8,128)(2,1)} %get-tuple-element.121.refs_0_), channel_id=1, source_target_pairs={{0,4},{1,5},{2,6},{3,7},{4,0},{5,1},{6,2},{7,3},{8,12},{9,13},{10,... | collective-permute-start | bytes 202760 | tf_op jit(solution)/shard_map/ppermute | solution.py:323
  138.7 4.5 %collective-permute-start.30 = (bf16[272,128]{1,0:T(8,128)(2,1)}, bf16[272,128]{1,0:T(8,128)(2,1)S(1)}, u32[]{:S(2)}, u32[]{:S(2)}) collective-permute-start(bf16[272,128]{1,0:T(8,128)(2,1)} %shard_map.132.refs_0_), channel_id=1, source_target_pairs={{0,2},{1,3},{2,0},{3,1},{4,6},{5,7},{6,4},{7,5},{8,10},{9,11},{10,... | collective-permute-start | bytes 208904 | tf_op jit(solution)/shard_map/ppermute | solution.py:323
  140.3 8.1 %collective-permute-start.36 = (bf16[32,1024]{1,0:T(8,128)(2,1)}, bf16[32,1024]{1,0:T(8,128)(2,1)S(1)}, u32[]{:S(2)}, u32[]{:S(2)}) collective-permute-start(bf16[32,1024]{1,0:T(8,128)(2,1)} %get-tuple-element.132.refs_3_.refs_21_), channel_id=1, source_target_pairs={{0,3},{1,2},{2,1},{3,0},{4,7},{5,6},{6,5},{7,4},{8,11},{9,10},{10,... | collective-permute-start | bytes 196616 | tf_op jit(solution)/shard_map/ppermute | solution.py:323
  140.3 10.1 %collective-permute-start.35 = (bf16[32,1024]{1,0:T(8,128)(2,1)}, bf16[32,1024]{1,0:T(8,128)(2,1)S(1)}, u32[]{:S(2)}, u32[]{:S(2)}) collective-permute-start(bf16[32,1024]{1,0:T(8,128)(2,1)} %get-tuple-element.132.refs_3_.refs_21_), channel_id=1, source_target_pairs={{0,2},{1,3},{2,0},{3,1},{4,6},{5,7},{6,4},{7,5},{8,10},{9,11},{10,... | collective-permute-start | bytes 196616 | tf_op jit(solution)/shard_map/ppermute | solution.py:323
  141.8 8.6 %collective-permute-start.34 = (bf16[32,1024]{1,0:T(8,128)(2,1)}, bf16[32,1024]{1,0:T(8,128)(2,1)S(1)}, u32[]{:S(2)}, u32[]{:S(2)}) collective-permute-start(bf16[32,1024]{1,0:T(8,128)(2,1)} %get-tuple-element.132.refs_3_.refs_21_), channel_id=1, source_target_pairs={{0,1},{1,0},{2,3},{3,2},{4,5},{5,4},{6,7},{7,6},{8,9},{9,8},{10,11... | collective-permute-start | bytes 196616 | tf_op jit(solution)/shard_map/ppermute | solution.py:323
  146.0 5.6 %collective-permute-start.33 = (f32[8,128]{1,0:T(8,128)}, f32[8,128]{1,0:T(8,128)S(1)}, u32[]{:S(2)}, u32[]{:S(2)}) collective-permute-start(f32[8,128]{1,0:T(8,128)} %get-tuple-element.134.refs_0_), channel_id=1, source_target_pairs={{0,12},{1,13},{2,14},{3,15},{4,8},{5,9},{6,10},{7,11},{8,4},{9,5},... | collective-permute-start | bytes 12296 | tf_op jit(solution)/shard_map/ppermute | solution.py:323
  148.4 4.7 %collective-permute-start.32 = (f32[8,128]{1,0:T(8,128)}, f32[8,128]{1,0:T(8,128)S(1)}, u32[]{:S(2)}, u32[]{:S(2)}) collective-permute-start(f32[8,128]{1,0:T(8,128)} %get-tuple-element.134.refs_0_), channel_id=1, source_target_pairs={{0,8},{1,9},{2,10},{3,11},{4,12},{5,13},{6,14},{7,15},{8,0},{9,1},... | collective-permute-start | bytes 12296 | tf_op jit(solution)/shard_map/ppermute | solution.py:323
  148.4 4.7 %collective-permute-start.31 = (f32[8,128]{1,0:T(8,128)}, f32[8,128]{1,0:T(8,128)S(1)}, u32[]{:S(2)}, u32[]{:S(2)}) collective-permute-start(f32[8,128]{1,0:T(8,128)} %get-tuple-element.134.refs_0_), channel_id=1, source_target_pairs={{0,4},{1,5},{2,6},{3,7},{4,0},{5,1},{6,2},{7,3},{8,12},{9,13},{10,... | collective-permute-start | bytes 12296 | tf_op jit(solution)/shard_map/ppermute | solution.py:323
  (42 other events, 265.8 us)

commit v4 on v3

--- a/solution.py
+++ b/solution.py
@@ -20,6 +20,7 @@
 VMEM = pl.BlockSpec(memory_space=pltpu.VMEM)
 SMEM = pl.BlockSpec(memory_space=pltpu.SMEM)
 ANY = pl.BlockSpec(memory_space=pl.ANY)
+PARAMS = pltpu.CompilerParams(vmem_limit_bytes=12 << 20)
 
 
 def dot(a, b):
@@ -93,20 +94,27 @@
         for out, value in zip(outs, fn(*(ref[...] for ref in ins))):
             out[...] = value
 
-    return pl.pallas_call(kernel, out_shape=shapes, in_specs=[VMEM] * len(args), out_specs=[VMEM] * len(shapes))(*args)
-
-
-def prepare(where, genotypes, coef_all, noise_coef, residual, noise_people, mask, sigma2_old, prior_prec):
+    return pl.pallas_call(kernel, out_shape=shapes, compiler_params=PARAMS, in_specs=[VMEM] * len(args), out_specs=[VMEM] * len(shapes))(*args)
+
+
+def place_in_quad():
+    return lax.axis_index("ppl") & (QUAD - 1)
+
+
+def prepare(block_index, valid_counts, genotypes, coef_all, noise_coef, residual, noise_people, sigma2_old, prior_prec):
     rows, width = genotypes.shape
     traits = residual.shape[0]
     quarter = width // QUAD
 
-    def kernel(where_ref, geno_ref, coef_ref, noise_ref, res_ref, people_ref, mask_ref, sigma_ref, prior_ref, *refs):
-        x_refs, (noise_out, partial_ref, kept_ref, given_ref, cross_ref, var_ref, ridge_ref, old_ref, sems) = refs[:QUAD], refs[QUAD:]
+    def kernel(block_ref, valid_ref, geno_ref, coef_ref, noise_ref, res_ref, people_ref, sigma_ref, prior_ref, *refs):
+        x_refs, refs = refs[:QUAD], refs[QUAD:]
+        noise_out, partial_ref, kept_ref, given_ref, cross_ref, var_ref, ridge_ref, mask_ref, old_ref, sems = refs
+        me = lax.axis_index("ppl")
+        own = place_in_quad()
         copies = []
         for slot in range(QUAD):
-            start = pl.multiple_of((where_ref[1] ^ slot) * quarter, LANES)
-            first = pl.multiple_of(where_ref[0] * width + start, LANES)
+            start = pl.multiple_of((own ^ slot) * quarter, LANES)
+            first = pl.multiple_of(block_ref[0] * width + start, LANES)
             pair = (
                 pltpu.make_async_copy(coef_ref.at[:, pl.ds(first, quarter)], old_ref.at[slot], sems.at[2 * slot]),
                 pltpu.make_async_copy(geno_ref.at[:, pl.ds(start, quarter)], x_refs[slot], sems.at[2 * slot + 1]),
@@ -114,7 +122,7 @@
             for copy in pair:
                 copy.start()
             copies.append(pair)
-        start = pl.multiple_of(where_ref[1] * quarter, LANES)
+        start = pl.multiple_of(own * quarter, LANES)
         last = pltpu.make_async_copy(noise_ref.at[:, pl.ds(start, quarter)], noise_out, sems.at[2 * QUAD])
         last.start()
         noise_var = to_column(sigma_ref[...], traits)
@@ -125,7 +133,10 @@
             for copy in copies[slot]:
                 copy.wait()
             fitted += dot_t(old_ref[slot].astype(BF16), x_refs[slot][...])
-        present = mask_ref[0:1]
+        slots = lax.broadcasted_iota(jnp.int32, (1, rows), 1)
+        for slot in range(QUAD):
+            mask_ref[:, slot * rows : (slot + 1) * rows] = (slots < valid_ref[me ^ slot]).astype(F32)
+        present = (slots < valid_ref[me]).astype(F32)
         partial = present * (res_ref[...] + fitted)
         partial_ref[...] = partial
         target = (present * (partial + jnp.sqrt(noise_var) * people_ref[...])).astype(BF16)
@@ -146,14 +157,16 @@
         shape((2 * lines, LANES), F32),
         shape((traits, 1), F32),
         shape((traits, 1), F32),
+        shape((1, QUAD * rows), F32),
     ]
     return pl.pallas_call(
         kernel,
+        compiler_params=PARAMS,
         out_shape=out_shape,
-        in_specs=[SMEM, ANY, ANY, ANY] + [VMEM] * 5,
+        in_specs=[SMEM, SMEM, ANY, ANY, ANY] + [VMEM] * 4,
         out_specs=[VMEM] * len(out_shape),
         scratch_shapes=[pltpu.VMEM((QUAD, traits, quarter), F32), pltpu.SemaphoreType.DMA((2 * QUAD + 1,))],
-    )(where, genotypes, coef_all, noise_coef, residual, noise_people, mask, sigma2_old, prior_prec)
+    )(block_index, valid_counts, genotypes, coef_all, noise_coef, residual, noise_people, sigma2_old, prior_prec)
 
 
 def image_part(search, direction, x):
@@ -198,12 +211,11 @@
 
 def new_image(count, sent, back, mask, low, direction, image, norm_old, length):
     traits = low.shape[0]
-    rows = mask.shape[1]
+    rows = mask.shape[1] // QUAD
     wide, columns = unpack(sent, traits, QUAD * rows, count)
     far, far_columns = unpack(cross(back, 2, traits, rows), traits, QUAD * rows, count)
     columns = [a + b for a, b in zip(columns, far_columns)]
-    present = jnp.concatenate([mask[slot : slot + 1] for slot in range(QUAD)], axis=1)
-    fresh = present * (wide + far)
+    fresh = mask * (wide + far)
     norm, low_low = columns[:2]
     wide = low.astype(F32)
     if direction is None:
@@ -223,7 +235,7 @@
     else:
         state, x = new_image(3, sent, back, mask, low, *rest[:4]), rest[4:]
     rounded = state[0].astype(BF16)
-    rows = mask.shape[1]
+    rows = mask.shape[1] // QUAD
     energy = by_pairs([row_sum(part) for part in slots_of(state[0] * rounded.astype(F32), rows)])
     total = by_pairs([dot(part, block) for part, block in zip(slots_of(rounded, rows), x)])
     return pack(total, [energy], kind), *state
@@ -231,14 +243,14 @@
 
 def last_sums(sent, back, mask, low, direction, image, norm_old, length, before):
     image, _, norm, length, beta = new_image(3, sent, back, mask, low, direction, image, norm_old, length)
-    rows = mask.shape[1]
+    rows = mask.shape[1] // QUAD
     products = (image * image.astype(BF16).astype(F32), before * before, before * image, image * image)
     sums = [to_row(by_pairs([row_sum(part) for part in slots_of(product, rows)])) for product in products]
     packed = jnp.concatenate(sums + [jnp.zeros((TILE - len(sums), LANES), F32)], axis=0)
     return packed, image[:, :rows], norm, length, beta
 
 
-def finish(where, got, norm, length, noise_var, ridge, gamma, before, image, steps, betas, early, late, coef_all):
+def finish(block_index, valid_counts, got, norm, length, noise_var, ridge, gamma, before, image, steps, betas, early, late, coef_all):
     traits, quarter = late[0].shape
     rows = image.shape[1]
     width = QUAD * quarter
@@ -247,20 +259,20 @@
     args = [*got, norm, length, noise_var, ridge, gamma, before, image, *steps, *betas, *early, *late]
     split = [len(got), 7, kept, kept, QUAD, QUAD]
 
-    def kernel(where_ref, *refs):
+    def kernel(block_ref, valid_ref, *refs):
         groups, at = [], 0
         for size in split:
             groups.append(refs[at : at + size])
             at += size
         coef_ref, out_ref, res_ref, sigma_ref, scratch, sems = refs[at:]
-        block = where_ref[0]
+        block, own = block_ref[0], place_in_quad()
 
         def hold(index):
             span = pl.ds(index * width, width)
             return pltpu.make_async_copy(coef_ref.at[:, span], out_ref.at[:, span], sems.at[index])
 
         def give(slot):
-            start = pl.multiple_of(block * width + (where_ref[1] ^ slot) * quarter, LANES)
+            start = pl.multiple_of(block * width + (own ^ slot) * quarter, LANES)
             return pltpu.make_async_copy(scratch.at[slot], out_ref.at[:, pl.ds(start, quarter)], sems.at[blocks + slot])
 
         for index in range(blocks):
@@ -282,7 +294,7 @@
             give(slot).start()
         res_ref[...] = before[:, :rows] - step * image[...]
         squares = squares - step * (2.0 * mixed - step * energy_full)
-        present = where_ref[2].astype(F32)
+        present = sum(valid_ref[k] for k in range(valid_counts.shape[0])).astype(F32)
         row = to_row(squares + PRIOR_DOF * PRIOR_SCALE)[:, :traits]
         sigma_ref[...] = row / ((present + PRIOR_DOF) * gamma[...])
         for slot in range(QUAD):
@@ -293,11 +305,12 @@
     shape = jax.ShapeDtypeStruct
     return pl.pallas_call(
         kernel,
+        compiler_params=PARAMS,
         out_shape=[shape(coef_all.shape, F32), shape((traits, rows), F32), shape((1, traits), F32)],
-        in_specs=[SMEM] + [VMEM] * (len(args) + 1),
+        in_specs=[SMEM, SMEM] + [VMEM] * (len(args) + 1),
         out_specs=[ANY, VMEM, VMEM],
         scratch_shapes=[pltpu.VMEM((QUAD, traits, quarter), F32), pltpu.SemaphoreType.DMA((blocks + QUAD,))],
-    )(where, *args, coef_all)
+    )(block_index, valid_counts, *args, coef_all)
 
 
 def per_device(
@@ -316,8 +329,6 @@
     rows, width = genotypes.shape
     traits = residual.shape[0]
     quarter = width // QUAD
-    me = lax.axis_index("ppl")
-    own = me & (QUAD - 1)
 
     def swap(x, distance):
         return lax.ppermute(x, "ppl", [(i, i ^ distance) for i in range(count)])
@@ -343,19 +354,16 @@
             else:
                 (x,) = fuse(add, *got)
 
-    slots = jnp.arange(rows)
-    quad = valid_counts[jnp.bitwise_xor(me, jnp.arange(QUAD))]
-    mask = (slots[None, :] < quad[:, None]).astype(F32)
-    where = jnp.stack([block_index[0], own, jnp.sum(valid_counts)]).astype(jnp.int32)
     made = prepare(
-        where, genotypes, coef_all, noise_coef, residual, noise_people, mask, sigma2_old.reshape(1, -1), prior_prec.reshape(1, -1)
+        block_index, valid_counts, genotypes, coef_all, noise_coef, residual, noise_people, sigma2_old[None, :], prior_prec[None, :]
     )
-    x_give, (noise_quarter, partial_res, kept, given, sent, noise_var, ridge) = made[:QUAD], made[QUAD:]
+    x_give, (noise_quarter, partial_res, kept, given, sent, noise_var, ridge, mask) = made[:QUAD], made[QUAD:]
     lines = kept.shape[0]
     back = swap(sent, 1)
     given = given + back[lines:]
     given, x_give = lax.optimization_barrier((given, x_give))
-    kept = kept + back[:lines] + swap(given, 2)
+    far = swap(given, 2)
+    kept = kept + back[:lines] + far
     x = [x_give[0]] + [swap(x_give[slot], slot) for slot in (1, 2, 3)]
     got = over_z(kept, 0)
 
@@ -393,7 +401,21 @@
     late = share(low)
     got = over_z(sent, 4)
     coef_new, residual_new, sigma2_new = finish(
-        where, got, norm, length, noise_var, ridge, gamma_draw.reshape(1, -1), before, image, steps, betas, early, late, coef_all
+        block_index,
+        valid_counts,
+        got,
+        norm,
+        length,
+        noise_var,
+        ridge,
+        gamma_draw[None, :],
+        before,
+        image,
+        steps,
+        betas,
+        early,
+        late,
+        coef_all,
     )
     return (coef_new, residual_new, sigma2_new.reshape(-1))
 

time: 158 us -> 122 us (0.77)
  Pallas kernels: 40.3 us -> 12 us
  other arithmetic: 5.83 us -> 0.05 us
  local copies, waits for them, and re-layouts: 10 us -> 7.38 us
    pallas_call x14, Pallas kernels: 40.3 us -> 12 us  [the longest x12 6.71 us: fuse(): pl.pallas_call(kernel, out_shape=shapes, compiler_params=PARAMS, in_specs...]
    unnamed x76 -> x24, local copies, waits for them, and re-layouts: 7.87 us -> 7.37 us
  transfers between devices with their start and end apart: 37 -> 37, of which waited for: 23 -> 23; matrix products, arithmetic and copies ran while one was open for 1% -> 0% of each run, Pallas kernels for 4% -> 1%
where the time goes in v4:
time: 122 us
  waiting for transfers between devices  55.6 us (46%)
  starting transfers between devices  45.1 us (37%)
  Pallas kernels  12 us (10%)
  local copies, waits for them, and re-layouts  7.38 us (6%)
  between operations  1.44 us (1%)
    ppermute x37, waiting for transfers between devices, swap(): return lax.ppermute(x, 'ppl', [(i, i ^ distance) for i in range(count)])  55.6 us
    ppermute x37, starting transfers between devices, swap(): return lax.ppermute(x, 'ppl', [(i, i ^ distance) for i in range(count)])  45.1 us
    unnamed x24, local copies, waits for them, and re-layouts  7.37 us
    pallas_call x12, Pallas kernels, fuse(): pl.pallas_call(kernel, out_shape=shapes, compiler_params=PARAMS, in_specs...  6.71 us
    pallas_call x1, Pallas kernels, prepare(): pl.pallas_call(kernel, compiler_params=PARAMS, out_shape=out_shape, in_sp...  2.85 us
  transfers between devices with their start and end apart: 37, of which 23 were waited for; matrix products, arithmetic and copies ran while one was open for 0% of the time, Pallas kernels for 1%

profile of v4, /device:TPU:0, one launch (start us, length us, event | category | flops | bytes accessed | tf_op | source)
XLA Modules:
  0.0 121.5 jit_solution(11951860353586443499)
XLA Ops:
  2.5 1.6 %copy-done.2 = bf16[256,4096]{1,0:T(8,128)(2,1)S(1)} copy-done((bf16[256,4096]{1,0:T(8,128)(2,1)S(1)}, bf16[256,4096]{1,0:T(8,128)(2,1)}, u32[]{:S(2)}) %copy-start.2) | copy-done | bytes 2097176
  8.6 2.8 %shard_map.121 = (bf16[256,1024]{1,0:T(8,128)(2,1)S(1)}, bf16[256,1024]{1,0:T(8,128)(2,1)S(1)}, bf16[256,1024]{1,0:T(8,128)(2,1)S(1)}, bf16[256,1024]{1,0:T(8,12...) custom-call(s32[1]{0:T(128)S(6)} %copy.15.block_ref, ...), custom_call_target="tpu_custom_call" | custom-call | tf_op jit(solution)/shard_map/pallas_call | solution.py:162
  13.2 2.9 %collective-permute-start.1 = (f32[256,128]{1,0:T(8,128)S(1)}, f32[256,128]{1,0:T(8,128)S(1)}, u32[]{:S(2)}, u32[]{:S(2)}) collective-permute-start(f32[256,128]{1,0:T(8,128)S(1)} %slice_add_fusion), channel_id=1, source_target_pairs={{0,2},{1,3},{2,0},{3,1},{4,6},{5,7},{6,4},{7,5},{8,10},{9,11},{10,... | collective-permute-start | bytes 393224 | tf_op jit(solution)/shard_map/ppermute | solution.py:334
  16.4 1.6 %collective-permute-start.7 = (bf16[256,1024]{1,0:T(8,128)(2,1)S(1)}, bf16[256,1024]{1,0:T(8,128)(2,1)S(1)}, u32[]{:S(2)}, u32[]{:S(2)}) collective-permute-start(bf16[256,1024]{1,0:T(8,128)(2,1)S(1)} %get-tuple-element.92), channel_id=1, source_target_pairs={{0,3},{1,2},{2,1},{3,0},{4,7},{5,6},{6,5},{7,4},{8,11},{9,10},{10,... | collective-permute-start | bytes 1572872 | tf_op jit(solution)/shard_map/ppermute | solution.py:334
  18.0 2.5 %collective-permute-done.1 = f32[256,128]{1,0:T(8,128)S(1)} collective-permute-done((f32[256,128]{1,0:T(8,128)S(1)}, f32[256,128]{1,0:T(8,128)S(1)}, u32[]{:S(2)}, u32[]{:S(2)}) %collective-permute-start.1) | collective-permute-done | bytes 131104 | tf_op jit(solution)/shard_map/ppermute | solution.py:334
  20.5 4.2 %collective-permute-start.4 = (f32[256,128]{1,0:T(8,128)S(1)}, f32[256,128]{1,0:T(8,128)S(1)}, u32[]{:S(2)}, u32[]{:S(2)}) collective-permute-start(f32[256,128]{1,0:T(8,128)S(1)} %fusion.refs_0_), channel_id=1, source_target_pairs={{0,12},{1,13},{2,14},{3,15},{4,8},{5,9},{6,10},{7,11},{8,4},{9,5},... | collective-permute-start | bytes 393224 | tf_op jit(solution)/shard_map/ppermute | solution.py:334
  24.7 3.6 %collective-permute-done.4.refs_3_ = f32[256,128]{1,0:T(8,128)S(1)} collective-permute-done((f32[256,128]{1,0:T(8,128)S(1)}, f32[256,128]{1,0:T(8,128)S(1)}, u32[]{:S(2)}, u32[]{:S(2)}) %collective-permute-start.4) | collective-permute-done | bytes 131104 | tf_op jit(solution)/shard_map/ppermute | solution.py:334
  28.3 4.8 %collective-permute-start.2 = (f32[256,128]{1,0:T(8,128)S(1)}, f32[256,128]{1,0:T(8,128)S(1)}, u32[]{:S(2)}, u32[]{:S(2)}) collective-permute-start(f32[256,128]{1,0:T(8,128)S(1)} %fusion.refs_0_), channel_id=1, source_target_pairs={{0,4},{1,5},{2,6},{3,7},{4,0},{5,1},{6,2},{7,3},{8,12},{9,13},{10,... | collective-permute-start | bytes 393224 | tf_op jit(solution)/shard_map/ppermute | solution.py:334
  34.5 2.5 %collective-permute-done.2.refs_1_ = f32[256,128]{1,0:T(8,128)S(1)} collective-permute-done((f32[256,128]{1,0:T(8,128)S(1)}, f32[256,128]{1,0:T(8,128)S(1)}, u32[]{:S(2)}, u32[]{:S(2)}) %collective-permute-start.2) | collective-permute-done | bytes 131104 | tf_op jit(solution)/shard_map/ppermute | solution.py:334
  37.0 4.8 %collective-permute-done.7.refs_10_.refs_7_.refs_15_.refs_11_ = bf16[256,1024]{1,0:T(8,128)(2,1)S(1)} collective-permute-done((bf16[256,1024]{1,0:T(8,128)(2,1)S(1)}, bf16[256,1024]{1,0:T(8,128)(2,1)S(1)}, u32[]{:S(2)}, u32[]{:S(2)}) %collective-permute-start.7) | collective-permute-done | bytes 524320 | tf_op jit(solution)/shard_map/ppermute | solution.py:334
  44.0 1.8 %collective-permute-start.9 = (f32[264,128]{1,0:T(8,128)S(1)}, f32[264,128]{1,0:T(8,128)S(1)}, u32[]{:S(2)}, u32[]{:S(2)}) collective-permute-start(f32[264,128]{1,0:T(8,128)S(1)} %shard_map.123.refs_0_), channel_id=1, source_target_pairs={{0,2},{1,3},{2,0},{3,1},{4,6},{5,7},{6,4},{7,5},{8,10},{9,11},{10,... | collective-permute-start | bytes 405512 | tf_op jit(solution)/shard_map/ppermute | solution.py:334
  45.8 4.1 %collective-permute-done.9.refs_1_ = f32[264,128]{1,0:T(8,128)S(1)} collective-permute-done((f32[264,128]{1,0:T(8,128)S(1)}, f32[264,128]{1,0:T(8,128)S(1)}, u32[]{:S(2)}, u32[]{:S(2)}) %collective-permute-start.9) | collective-permute-done | bytes 135200 | tf_op jit(solution)/shard_map/ppermute | solution.py:334
  50.9 3.8 %collective-permute-start.12 = (f32[264,128]{1,0:T(8,128)S(1)}, f32[264,128]{1,0:T(8,128)S(1)}, u32[]{:S(2)}, u32[]{:S(2)}) collective-permute-start(f32[264,128]{1,0:T(8,128)S(1)} %get-tuple-element.98.refs_0_), channel_id=1, source_target_pairs={{0,12},{1,13},{2,14},{3,15},{4,8},{5,9},{6,10},{7,11},{8,4},{9,5},... | collective-permute-start | bytes 405512 | tf_op jit(solution)/shard_map/ppermute | solution.py:334
  55.4 1.7 %collective-permute-start.14 = (f32[32,256]{1,0:T(8,128)S(1)}, f32[32,256]{1,0:T(8,128)S(1)}, u32[]{:S(2)}, u32[]{:S(2)}) collective-permute-start(f32[32,256]{1,0:T(8,128)S(1)} %get-tuple-element.105), channel_id=1, source_target_pairs={{0,2},{1,3},{2,0},{3,1},{4,6},{5,7},{6,4},{7,5},{8,10},{9,11},{10,... | collective-permute-start | bytes 98312 | tf_op jit(solution)/shard_map/ppermute | solution.py:334
  57.0 1.7 %collective-permute-done.15 = f32[32,256]{1,0:T(8,128)S(1)} collective-permute-done((f32[32,256]{1,0:T(8,128)S(1)}, f32[32,256]{1,0:T(8,128)S(1)}, u32[]{:S(2)}, u32[]{:S(2)}) %collective-permute-start.15) | collective-permute-done | bytes 32800 | tf_op jit(solution)/shard_map/ppermute | solution.py:334
  60.0 5.9 %collective-permute-done.11.refs_2_ = f32[264,128]{1,0:T(8,128)S(1)} collective-permute-done((f32[264,128]{1,0:T(8,128)S(1)}, f32[264,128]{1,0:T(8,128)S(1)}, u32[]{:S(2)}, u32[]{:S(2)}) %collective-permute-start.11) | collective-permute-done | bytes 135200 | tf_op jit(solution)/shard_map/ppermute | solution.py:334
  68.2 1.6 %collective-permute-start.17 = (bf16[272,128]{1,0:T(8,128)(2,1)S(1)}, bf16[272,128]{1,0:T(8,128)(2,1)S(1)}, u32[]{:S(2)}, u32[]{:S(2)}) collective-permute-start(bf16[272,128]{1,0:T(8,128)(2,1)S(1)} %shard_map.126.refs_0_), channel_id=1, source_target_pairs={{0,2},{1,3},{2,0},{3,1},{4,6},{5,7},{6,4},{7,5},{8,10},{9,11},{10,... | collective-permute-start | bytes 208904 | tf_op jit(solution)/shard_map/ppermute | solution.py:334
  69.8 2.8 %collective-permute-done.17.refs_1_ = bf16[272,128]{1,0:T(8,128)(2,1)S(1)} collective-permute-done((bf16[272,128]{1,0:T(8,128)(2,1)S(1)}, bf16[272,128]{1,0:T(8,128)(2,1)S(1)}, u32[]{:S(2)}, u32[]{:S(2)}) %collective-permute-start.17) | collective-permute-done | bytes 69664 | tf_op jit(solution)/shard_map/ppermute | solution.py:334
  73.2 2.5 %collective-permute-start.20 = (bf16[264,128]{1,0:T(8,128)(2,1)S(1)}, bf16[264,128]{1,0:T(8,128)(2,1)S(1)}, u32[]{:S(2)}, u32[]{:S(2)}) collective-permute-start(bf16[264,128]{1,0:T(8,128)(2,1)S(1)} %get-tuple-element.113.refs_0_), channel_id=1, source_target_pairs={{0,12},{1,13},{2,14},{3,15},{4,8},{5,9},{6,10},{7,11},{8,4},{9,5},... | collective-permute-start | bytes 202760 | tf_op jit(solution)/shard_map/ppermute | solution.py:334
  75.7 1.9 %collective-permute-start.18 = (bf16[264,128]{1,0:T(8,128)(2,1)S(1)}, bf16[264,128]{1,0:T(8,128)(2,1)S(1)}, u32[]{:S(2)}, u32[]{:S(2)}) collective-permute-start(bf16[264,128]{1,0:T(8,128)(2,1)S(1)} %get-tuple-element.113.refs_0_), channel_id=1, source_target_pairs={{0,4},{1,5},{2,6},{3,7},{4,0},{5,1},{6,2},{7,3},{8,12},{9,13},{10,... | collective-permute-start | bytes 202760 | tf_op jit(solution)/shard_map/ppermute | solution.py:334
  77.6 1.9 %collective-permute-done.20.refs_3_ = bf16[264,128]{1,0:T(8,128)(2,1)S(1)} collective-permute-done((bf16[264,128]{1,0:T(8,128)(2,1)S(1)}, bf16[264,128]{1,0:T(8,128)(2,1)S(1)}, u32[]{:S(2)}, u32[]{:S(2)}) %collective-permute-start.20) | collective-permute-done | bytes 67616 | tf_op jit(solution)/shard_map/ppermute | solution.py:334
  79.6 1.7 %collective-permute-done.19.refs_2_ = bf16[264,128]{1,0:T(8,128)(2,1)S(1)} collective-permute-done((bf16[264,128]{1,0:T(8,128)(2,1)S(1)}, bf16[264,128]{1,0:T(8,128)(2,1)S(1)}, u32[]{:S(2)}, u32[]{:S(2)}) %collective-permute-start.19) | collective-permute-done | bytes 67616 | tf_op jit(solution)/shard_map/ppermute | solution.py:334
  82.2 1.6 %collective-permute-start.28 = (bf16[96,1024]{1,0:T(8,128)(2,1)S(1)}, bf16[96,1024]{1,0:T(8,128)(2,1)S(1)}, u32[]{:S(2)}, u32[]{:S(2)}) collective-permute-start(bf16[96,1024]{1,0:T(8,128)(2,1)S(1)} %constant_dynamic-update-slice_fusion.refs_17_), channel_id=1, source_target_pairs={{0,3},{1,2},{2,1},{3,0},{4,7},{5,6},{6,5},{7,4},{8,11},{9,10},{10,... | collective-permute-start | bytes 589832 | tf_op jit(solution)/shard_map/ppermute | solution.py:334
  84.5 1.6 %collective-permute-start.22 = (bf16[272,128]{1,0:T(8,128)(2,1)S(1)}, bf16[272,128]{1,0:T(8,128)(2,1)S(1)}, u32[]{:S(2)}, u32[]{:S(2)}) collective-permute-start(bf16[272,128]{1,0:T(8,128)(2,1)S(1)} %shard_map.129.refs_0_), channel_id=1, source_target_pairs={{0,2},{1,3},{2,0},{3,1},{4,6},{5,7},{6,4},{7,5},{8,10},{9,11},{10,... | collective-permute-start | bytes 208904 | tf_op jit(solution)/shard_map/ppermute | solution.py:334
  86.1 9.1 %collective-permute-done.22.refs_1_ = bf16[272,128]{1,0:T(8,128)(2,1)S(1)} collective-permute-done((bf16[272,128]{1,0:T(8,128)(2,1)S(1)}, bf16[272,128]{1,0:T(8,128)(2,1)S(1)}, u32[]{:S(2)}, u32[]{:S(2)}) %collective-permute-start.22) | collective-permute-done | bytes 69664 | tf_op jit(solution)/shard_map/ppermute | solution.py:334
  95.8 2.2 %collective-permute-start.25 = (bf16[264,128]{1,0:T(8,128)(2,1)S(1)}, bf16[264,128]{1,0:T(8,128)(2,1)S(1)}, u32[]{:S(2)}, u32[]{:S(2)}) collective-permute-start(bf16[264,128]{1,0:T(8,128)(2,1)S(1)} %get-tuple-element.123.refs_0_), channel_id=1, source_target_pairs={{0,12},{1,13},{2,14},{3,15},{4,8},{5,9},{6,10},{7,11},{8,4},{9,5},... | collective-permute-start | bytes 202760 | tf_op jit(solution)/shard_map/ppermute | solution.py:334
  98.1 2.2 %collective-permute-start.23 = (bf16[264,128]{1,0:T(8,128)(2,1)S(1)}, bf16[264,128]{1,0:T(8,128)(2,1)S(1)}, u32[]{:S(2)}, u32[]{:S(2)}) collective-permute-start(bf16[264,128]{1,0:T(8,128)(2,1)S(1)} %get-tuple-element.123.refs_0_), channel_id=1, source_target_pairs={{0,4},{1,5},{2,6},{3,7},{4,0},{5,1},{6,2},{7,3},{8,12},{9,13},{10,... | collective-permute-start | bytes 202760 | tf_op jit(solution)/shard_map/ppermute | solution.py:334
  100.3 1.8 %collective-permute-done.25.refs_3_ = bf16[264,128]{1,0:T(8,128)(2,1)S(1)} collective-permute-done((bf16[264,128]{1,0:T(8,128)(2,1)S(1)}, bf16[264,128]{1,0:T(8,128)(2,1)S(1)}, u32[]{:S(2)}, u32[]{:S(2)}) %collective-permute-start.25) | collective-permute-done | bytes 67616 | tf_op jit(solution)/shard_map/ppermute | solution.py:334
  102.1 2.5 %collective-permute-done.24.refs_2_ = bf16[264,128]{1,0:T(8,128)(2,1)S(1)} collective-permute-done((bf16[264,128]{1,0:T(8,128)(2,1)S(1)}, bf16[264,128]{1,0:T(8,128)(2,1)S(1)}, u32[]{:S(2)}, u32[]{:S(2)}) %collective-permute-start.24) | collective-permute-done | bytes 67616 | tf_op jit(solution)/shard_map/ppermute | solution.py:334
  112.1 2.5 %collective-permute-start.33 = (f32[8,128]{1,0:T(8,128)S(1)}, f32[8,128]{1,0:T(8,128)S(1)}, u32[]{:S(2)}, u32[]{:S(2)}) collective-permute-start(f32[8,128]{1,0:T(8,128)S(1)} %get-tuple-element.136.refs_0_), channel_id=1, source_target_pairs={{0,12},{1,13},{2,14},{3,15},{4,8},{5,9},{6,10},{7,11},{8,4},{9,5},... | collective-permute-start | bytes 12296 | tf_op jit(solution)/shard_map/ppermute | solution.py:334
  114.6 2.0 %collective-permute-start.31 = (f32[8,128]{1,0:T(8,128)S(1)}, f32[8,128]{1,0:T(8,128)S(1)}, u32[]{:S(2)}, u32[]{:S(2)}) collective-permute-start(f32[8,128]{1,0:T(8,128)S(1)} %get-tuple-element.136.refs_0_), channel_id=1, source_target_pairs={{0,4},{1,5},{2,6},{3,7},{4,0},{5,1},{6,2},{7,3},{8,12},{9,13},{10,... | collective-permute-start | bytes 12296 | tf_op jit(solution)/shard_map/ppermute | solution.py:334
  119.1 2.4 %shard_map.134 = (f32[32,8192]{1,0:T(8,128)}, f32[32,256]{1,0:T(8,128)}, f32[1,32]{1,0:T(1,128)}) custom-call(s32[1]{0:T(128)S(6)} %copy.15.block_ref, s32[16]{0:T(128)S(1)} %copy-done.7, f32[8,128]{1,0:T(8,128)S(1)} %get-tuple-element.136.refs_0_, f32[8,128]{1,0:T(8,128)S(1)} %collective-permute-done.31.refs_1_, ...), custom_call_target="tpu_custom_call" | custom-call | tf_op jit(solution)/shard_map/pallas_call | solution.py:306
  (84 shorter events, 29.3 us)
Async XLA Ops:
  13.2 7.3 %collective-permute-start.1 = (f32[256,128]{1,0:T(8,128)S(1)}, f32[256,128]{1,0:T(8,128)S(1)}, u32[]{:S(2)}, u32[]{:S(2)}) collective-permute-start(f32[256,128]{1,0:T(8,128)S(1)} %slice_add_fusion), channel_id=1, source_target_pairs={{0,2},{1,3},{2,0},{3,1},{4,6},{5,7},{6,4},{7,5},{8,10},{9,11},{10,... | collective-permute-start | bytes 393224 | tf_op jit(solution)/shard_map/ppermute | solution.py:334
  16.2 20.9 %collective-permute-start.5 = (bf16[256,1024]{1,0:T(8,128)(2,1)S(1)}, bf16[256,1024]{1,0:T(8,128)(2,1)S(1)}, u32[]{:S(2)}, u32[]{:S(2)}) collective-permute-start(bf16[256,1024]{1,0:T(8,128)(2,1)S(1)} %get-tuple-element.90), channel_id=1, source_target_pairs={{0,1},{1,0},{2,3},{3,2},{4,5},{5,4},{6,7},{7,6},{8,9},{9,8},{10,11... | collective-permute-start | bytes 1572872 | tf_op jit(solution)/shard_map/ppermute | solution.py:334
  16.2 20.9 %collective-permute-start.6 = (bf16[256,1024]{1,0:T(8,128)(2,1)S(1)}, bf16[256,1024]{1,0:T(8,128)(2,1)S(1)}, u32[]{:S(2)}, u32[]{:S(2)}) collective-permute-start(bf16[256,1024]{1,0:T(8,128)(2,1)S(1)} %get-tuple-element.91), channel_id=1, source_target_pairs={{0,2},{1,3},{2,0},{3,1},{4,6},{5,7},{6,4},{7,5},{8,10},{9,11},{10,... | collective-permute-start | bytes 1572872 | tf_op jit(solution)/shard_map/ppermute | solution.py:334
  16.4 25.5 %collective-permute-start.7 = (bf16[256,1024]{1,0:T(8,128)(2,1)S(1)}, bf16[256,1024]{1,0:T(8,128)(2,1)S(1)}, u32[]{:S(2)}, u32[]{:S(2)}) collective-permute-start(bf16[256,1024]{1,0:T(8,128)(2,1)S(1)} %get-tuple-element.92), channel_id=1, source_target_pairs={{0,3},{1,2},{2,1},{3,0},{4,7},{5,6},{6,5},{7,4},{8,11},{9,10},{10,... | collective-permute-start | bytes 1572872 | tf_op jit(solution)/shard_map/ppermute | solution.py:334
  20.5 7.8 %collective-permute-start.4 = (f32[256,128]{1,0:T(8,128)S(1)}, f32[256,128]{1,0:T(8,128)S(1)}, u32[]{:S(2)}, u32[]{:S(2)}) collective-permute-start(f32[256,128]{1,0:T(8,128)S(1)} %fusion.refs_0_), channel_id=1, source_target_pairs={{0,12},{1,13},{2,14},{3,15},{4,8},{5,9},{6,10},{7,11},{8,4},{9,5},... | collective-permute-start | bytes 393224 | tf_op jit(solution)/shard_map/ppermute | solution.py:334
  24.7 9.8 %collective-permute-start.3 = (f32[256,128]{1,0:T(8,128)S(1)}, f32[256,128]{1,0:T(8,128)S(1)}, u32[]{:S(2)}, u32[]{:S(2)}) collective-permute-start(f32[256,128]{1,0:T(8,128)S(1)} %fusion.refs_0_), channel_id=1, source_target_pairs={{0,8},{1,9},{2,10},{3,11},{4,12},{5,13},{6,14},{7,15},{8,0},{9,1},... | collective-permute-start | bytes 393224 | tf_op jit(solution)/shard_map/ppermute | solution.py:334
  28.3 8.7 %collective-permute-start.2 = (f32[256,128]{1,0:T(8,128)S(1)}, f32[256,128]{1,0:T(8,128)S(1)}, u32[]{:S(2)}, u32[]{:S(2)}) collective-permute-start(f32[256,128]{1,0:T(8,128)S(1)} %fusion.refs_0_), channel_id=1, source_target_pairs={{0,4},{1,5},{2,6},{3,7},{4,0},{5,1},{6,2},{7,3},{8,12},{9,13},{10,... | collective-permute-start | bytes 393224 | tf_op jit(solution)/shard_map/ppermute | solution.py:334
  44.0 5.9 %collective-permute-start.9 = (f32[264,128]{1,0:T(8,128)S(1)}, f32[264,128]{1,0:T(8,128)S(1)}, u32[]{:S(2)}, u32[]{:S(2)}) collective-permute-start(f32[264,128]{1,0:T(8,128)S(1)} %shard_map.123.refs_0_), channel_id=1, source_target_pairs={{0,2},{1,3},{2,0},{3,1},{4,6},{5,7},{6,4},{7,5},{8,10},{9,11},{10,... | collective-permute-start | bytes 405512 | tf_op jit(solution)/shard_map/ppermute | solution.py:334
  50.9 9.1 %collective-permute-start.12 = (f32[264,128]{1,0:T(8,128)S(1)}, f32[264,128]{1,0:T(8,128)S(1)}, u32[]{:S(2)}, u32[]{:S(2)}) collective-permute-start(f32[264,128]{1,0:T(8,128)S(1)} %get-tuple-element.98.refs_0_), channel_id=1, source_target_pairs={{0,12},{1,13},{2,14},{3,15},{4,8},{5,9},{6,10},{7,11},{8,4},{9,5},... | collective-permute-start | bytes 405512 | tf_op jit(solution)/shard_map/ppermute | solution.py:334
  54.7 11.1 %collective-permute-start.11 = (f32[264,128]{1,0:T(8,128)S(1)}, f32[264,128]{1,0:T(8,128)S(1)}, u32[]{:S(2)}, u32[]{:S(2)}) collective-permute-start(f32[264,128]{1,0:T(8,128)S(1)} %get-tuple-element.98.refs_0_), channel_id=1, source_target_pairs={{0,8},{1,9},{2,10},{3,11},{4,12},{5,13},{6,14},{7,15},{8,0},{9,1},... | collective-permute-start | bytes 405512 | tf_op jit(solution)/shard_map/ppermute | solution.py:334
  54.7 11.1 %collective-permute-start.10 = (f32[264,128]{1,0:T(8,128)S(1)}, f32[264,128]{1,0:T(8,128)S(1)}, u32[]{:S(2)}, u32[]{:S(2)}) collective-permute-start(f32[264,128]{1,0:T(8,128)S(1)} %get-tuple-element.98.refs_0_), channel_id=1, source_target_pairs={{0,4},{1,5},{2,6},{3,7},{4,0},{5,1},{6,2},{7,3},{8,12},{9,13},{10,... | collective-permute-start | bytes 405512 | tf_op jit(solution)/shard_map/ppermute | solution.py:334
  55.3 3.4 %collective-permute-start.15 = (f32[32,256]{1,0:T(8,128)S(1)}, f32[32,256]{1,0:T(8,128)S(1)}, u32[]{:S(2)}, u32[]{:S(2)}) collective-permute-start(f32[32,256]{1,0:T(8,128)S(1)} %get-tuple-element.105), channel_id=1, source_target_pairs={{0,3},{1,2},{2,1},{3,0},{4,7},{5,6},{6,5},{7,4},{8,11},{9,10},{10,... | collective-permute-start | bytes 98312 | tf_op jit(solution)/shard_map/ppermute | solution.py:334
  55.4 4.0 %collective-permute-start.14 = (f32[32,256]{1,0:T(8,128)S(1)}, f32[32,256]{1,0:T(8,128)S(1)}, u32[]{:S(2)}, u32[]{:S(2)}) collective-permute-start(f32[32,256]{1,0:T(8,128)S(1)} %get-tuple-element.105), channel_id=1, source_target_pairs={{0,2},{1,3},{2,0},{3,1},{4,6},{5,7},{6,4},{7,5},{8,10},{9,11},{10,... | collective-permute-start | bytes 98312 | tf_op jit(solution)/shard_map/ppermute | solution.py:334
  68.2 4.4 %collective-permute-start.17 = (bf16[272,128]{1,0:T(8,128)(2,1)S(1)}, bf16[272,128]{1,0:T(8,128)(2,1)S(1)}, u32[]{:S(2)}, u32[]{:S(2)}) collective-permute-start(bf16[272,128]{1,0:T(8,128)(2,1)S(1)} %shard_map.126.refs_0_), channel_id=1, source_target_pairs={{0,2},{1,3},{2,0},{3,1},{4,6},{5,7},{6,4},{7,5},{8,10},{9,11},{10,... | collective-permute-start | bytes 208904 | tf_op jit(solution)/shard_map/ppermute | solution.py:334
  73.2 6.4 %collective-permute-start.20 = (bf16[264,128]{1,0:T(8,128)(2,1)S(1)}, bf16[264,128]{1,0:T(8,128)(2,1)S(1)}, u32[]{:S(2)}, u32[]{:S(2)}) collective-permute-start(bf16[264,128]{1,0:T(8,128)(2,1)S(1)} %get-tuple-element.113.refs_0_), channel_id=1, source_target_pairs={{0,12},{1,13},{2,14},{3,15},{4,8},{5,9},{6,10},{7,11},{8,4},{9,5},... | collective-permute-start | bytes 202760 | tf_op jit(solution)/shard_map/ppermute | solution.py:334
  75.7 5.6 %collective-permute-start.19 = (bf16[264,128]{1,0:T(8,128)(2,1)S(1)}, bf16[264,128]{1,0:T(8,128)(2,1)S(1)}, u32[]{:S(2)}, u32[]{:S(2)}) collective-permute-start(bf16[264,128]{1,0:T(8,128)(2,1)S(1)} %get-tuple-element.113.refs_0_), channel_id=1, source_target_pairs={{0,8},{1,9},{2,10},{3,11},{4,12},{5,13},{6,14},{7,15},{8,0},{9,1},... | collective-permute-start | bytes 202760 | tf_op jit(solution)/shard_map/ppermute | solution.py:334
  75.7 5.6 %collective-permute-start.18 = (bf16[264,128]{1,0:T(8,128)(2,1)S(1)}, bf16[264,128]{1,0:T(8,128)(2,1)S(1)}, u32[]{:S(2)}, u32[]{:S(2)}) collective-permute-start(bf16[264,128]{1,0:T(8,128)(2,1)S(1)} %get-tuple-element.113.refs_0_), channel_id=1, source_target_pairs={{0,4},{1,5},{2,6},{3,7},{4,0},{5,1},{6,2},{7,3},{8,12},{9,13},{10,... | collective-permute-start | bytes 202760 | tf_op jit(solution)/shard_map/ppermute | solution.py:334
  82.2 2.2 %collective-permute-start.21 = (f32[264,128]{1,0:T(8,128)S(1)}, f32[264,128]{1,0:T(8,128)S(1)}, u32[]{:S(2)}, u32[]{:S(2)}) collective-permute-start(f32[264,128]{1,0:T(8,128)S(1)} %get-tuple-element.120.refs_0_), channel_id=1, source_target_pairs={{0,1},{1,0},{2,3},{3,2},{4,5},{5,4},{6,7},{7,6},{8,9},{9,8},{10,11... | collective-permute-start | bytes 405512 | tf_op jit(solution)/shard_map/ppermute | solution.py:334
  82.2 15.8 %collective-permute-start.28 = (bf16[96,1024]{1,0:T(8,128)(2,1)S(1)}, bf16[96,1024]{1,0:T(8,128)(2,1)S(1)}, u32[]{:S(2)}, u32[]{:S(2)}) collective-permute-start(bf16[96,1024]{1,0:T(8,128)(2,1)S(1)} %constant_dynamic-update-slice_fusion.refs_17_), channel_id=1, source_target_pairs={{0,3},{1,2},{2,1},{3,0},{4,7},{5,6},{6,5},{7,4},{8,11},{9,10},{10,... | collective-permute-start | bytes 589832 | tf_op jit(solution)/shard_map/ppermute | solution.py:334
  83.9 16.5 %collective-permute-start.27 = (bf16[96,1024]{1,0:T(8,128)(2,1)S(1)}, bf16[96,1024]{1,0:T(8,128)(2,1)S(1)}, u32[]{:S(2)}, u32[]{:S(2)}) collective-permute-start(bf16[96,1024]{1,0:T(8,128)(2,1)S(1)} %constant_dynamic-update-slice_fusion.refs_17_), channel_id=1, source_target_pairs={{0,2},{1,3},{2,0},{3,1},{4,6},{5,7},{6,4},{7,5},{8,10},{9,11},{10,... | collective-permute-start | bytes 589832 | tf_op jit(solution)/shard_map/ppermute | solution.py:334
  84.4 16.0 %collective-permute-start.26 = (bf16[96,1024]{1,0:T(8,128)(2,1)S(1)}, bf16[96,1024]{1,0:T(8,128)(2,1)S(1)}, u32[]{:S(2)}, u32[]{:S(2)}) collective-permute-start(bf16[96,1024]{1,0:T(8,128)(2,1)S(1)} %constant_dynamic-update-slice_fusion.refs_17_), channel_id=1, source_target_pairs={{0,1},{1,0},{2,3},{3,2},{4,5},{5,4},{6,7},{7,6},{8,9},{9,8},{10,11... | collective-permute-start | bytes 589832 | tf_op jit(solution)/shard_map/ppermute | solution.py:334
  84.5 10.7 %collective-permute-start.22 = (bf16[272,128]{1,0:T(8,128)(2,1)S(1)}, bf16[272,128]{1,0:T(8,128)(2,1)S(1)}, u32[]{:S(2)}, u32[]{:S(2)}) collective-permute-start(bf16[272,128]{1,0:T(8,128)(2,1)S(1)} %shard_map.129.refs_0_), channel_id=1, source_target_pairs={{0,2},{1,3},{2,0},{3,1},{4,6},{5,7},{6,4},{7,5},{8,10},{9,11},{10,... | collective-permute-start | bytes 208904 | tf_op jit(solution)/shard_map/ppermute | solution.py:334
  95.8 6.3 %collective-permute-start.25 = (bf16[264,128]{1,0:T(8,128)(2,1)S(1)}, bf16[264,128]{1,0:T(8,128)(2,1)S(1)}, u32[]{:S(2)}, u32[]{:S(2)}) collective-permute-start(bf16[264,128]{1,0:T(8,128)(2,1)S(1)} %get-tuple-element.123.refs_0_), channel_id=1, source_target_pairs={{0,12},{1,13},{2,14},{3,15},{4,8},{5,9},{6,10},{7,11},{8,4},{9,5},... | collective-permute-start | bytes 202760 | tf_op jit(solution)/shard_map/ppermute | solution.py:334
  98.1 6.5 %collective-permute-start.24 = (bf16[264,128]{1,0:T(8,128)(2,1)S(1)}, bf16[264,128]{1,0:T(8,128)(2,1)S(1)}, u32[]{:S(2)}, u32[]{:S(2)}) collective-permute-start(bf16[264,128]{1,0:T(8,128)(2,1)S(1)} %get-tuple-element.123.refs_0_), channel_id=1, source_target_pairs={{0,8},{1,9},{2,10},{3,11},{4,12},{5,13},{6,14},{7,15},{8,0},{9,1},... | collective-permute-start | bytes 202760 | tf_op jit(solution)/shard_map/ppermute | solution.py:334
  98.1 6.5 %collective-permute-start.23 = (bf16[264,128]{1,0:T(8,128)(2,1)S(1)}, bf16[264,128]{1,0:T(8,128)(2,1)S(1)}, u32[]{:S(2)}, u32[]{:S(2)}) collective-permute-start(bf16[264,128]{1,0:T(8,128)(2,1)S(1)} %get-tuple-element.123.refs_0_), channel_id=1, source_target_pairs={{0,4},{1,5},{2,6},{3,7},{4,0},{5,1},{6,2},{7,3},{8,12},{9,13},{10,... | collective-permute-start | bytes 202760 | tf_op jit(solution)/shard_map/ppermute | solution.py:334
  107.4 4.4 %collective-permute-start.30 = (bf16[272,128]{1,0:T(8,128)(2,1)S(1)}, bf16[272,128]{1,0:T(8,128)(2,1)S(1)}, u32[]{:S(2)}, u32[]{:S(2)}) collective-permute-start(bf16[272,128]{1,0:T(8,128)(2,1)S(1)} %shard_map.132.refs_0_), channel_id=1, source_target_pairs={{0,2},{1,3},{2,0},{3,1},{4,6},{5,7},{6,4},{7,5},{8,10},{9,11},{10,... | collective-permute-start | bytes 208904 | tf_op jit(solution)/shard_map/ppermute | solution.py:334
  109.0 5.6 %collective-permute-start.36 = (bf16[32,1024]{1,0:T(8,128)(2,1)S(1)}, bf16[32,1024]{1,0:T(8,128)(2,1)S(1)}, u32[]{:S(2)}, u32[]{:S(2)}) collective-permute-start(bf16[32,1024]{1,0:T(8,128)(2,1)S(1)} %get-tuple-element.134.refs_3_.refs_21_), channel_id=1, source_target_pairs={{0,3},{1,2},{2,1},{3,0},{4,7},{5,6},{6,5},{7,4},{8,11},{9,10},{10,... | collective-permute-start | bytes 196616 | tf_op jit(solution)/shard_map/ppermute | solution.py:334
  109.0 7.6 %collective-permute-start.35 = (bf16[32,1024]{1,0:T(8,128)(2,1)S(1)}, bf16[32,1024]{1,0:T(8,128)(2,1)S(1)}, u32[]{:S(2)}, u32[]{:S(2)}) collective-permute-start(bf16[32,1024]{1,0:T(8,128)(2,1)S(1)} %get-tuple-element.134.refs_3_.refs_21_), channel_id=1, source_target_pairs={{0,2},{1,3},{2,0},{3,1},{4,6},{5,7},{6,4},{7,5},{8,10},{9,11},{10,... | collective-permute-start | bytes 196616 | tf_op jit(solution)/shard_map/ppermute | solution.py:334
  110.5 6.1 %collective-permute-start.34 = (bf16[32,1024]{1,0:T(8,128)(2,1)S(1)}, bf16[32,1024]{1,0:T(8,128)(2,1)S(1)}, u32[]{:S(2)}, u32[]{:S(2)}) collective-permute-start(bf16[32,1024]{1,0:T(8,128)(2,1)S(1)} %get-tuple-element.134.refs_3_.refs_21_), channel_id=1, source_target_pairs={{0,1},{1,0},{2,3},{3,2},{4,5},{5,4},{6,7},{7,6},{8,9},{9,8},{10,11... | collective-permute-start | bytes 196616 | tf_op jit(solution)/shard_map/ppermute | solution.py:334
  112.1 5.5 %collective-permute-start.33 = (f32[8,128]{1,0:T(8,128)S(1)}, f32[8,128]{1,0:T(8,128)S(1)}, u32[]{:S(2)}, u32[]{:S(2)}) collective-permute-start(f32[8,128]{1,0:T(8,128)S(1)} %get-tuple-element.136.refs_0_), channel_id=1, source_target_pairs={{0,12},{1,13},{2,14},{3,15},{4,8},{5,9},{6,10},{7,11},{8,4},{9,5},... | collective-permute-start | bytes 12296 | tf_op jit(solution)/shard_map/ppermute | solution.py:334
  114.6 4.5 %collective-permute-start.32 = (f32[8,128]{1,0:T(8,128)S(1)}, f32[8,128]{1,0:T(8,128)S(1)}, u32[]{:S(2)}, u32[]{:S(2)}) collective-permute-start(f32[8,128]{1,0:T(8,128)S(1)} %get-tuple-element.136.refs_0_), channel_id=1, source_target_pairs={{0,8},{1,9},{2,10},{3,11},{4,12},{5,13},{6,14},{7,15},{8,0},{9,1},... | collective-permute-start | bytes 12296 | tf_op jit(solution)/shard_map/ppermute | solution.py:334
  114.6 4.5 %collective-permute-start.31 = (f32[8,128]{1,0:T(8,128)S(1)}, f32[8,128]{1,0:T(8,128)S(1)}, u32[]{:S(2)}, u32[]{:S(2)}) collective-permute-start(f32[8,128]{1,0:T(8,128)S(1)} %get-tuple-element.136.refs_0_), channel_id=1, source_target_pairs={{0,4},{1,5},{2,6},{3,7},{4,0},{5,1},{6,2},{7,3},{8,12},{9,13},{10,... | collective-permute-start | bytes 12296 | tf_op jit(solution)/shard_map/ppermute | solution.py:334
  (16 other events, 84.4 us)

commit v5 on v4

--- a/solution.py
+++ b/solution.py
@@ -15,11 +15,11 @@
 TILE = 8
 QUAD = 4
 F32, BF16 = jnp.float32, jnp.bfloat16
-PEOPLE_KIND = (F32, BF16, BF16)
+PEOPLE_KIND = (BF16, BF16, BF16)
 IMAGE_KIND = (F32, BF16, BF16, BF16)
 VMEM = pl.BlockSpec(memory_space=pltpu.VMEM)
 SMEM = pl.BlockSpec(memory_space=pltpu.SMEM)
-ANY = pl.BlockSpec(memory_space=pl.ANY)
+HBM = pl.BlockSpec(memory_space=pltpu.HBM)
 PARAMS = pltpu.CompilerParams(vmem_limit_bytes=12 << 20)
 
 
@@ -106,9 +106,9 @@
     traits = residual.shape[0]
     quarter = width // QUAD
 
-    def kernel(block_ref, valid_ref, geno_ref, coef_ref, noise_ref, res_ref, people_ref, sigma_ref, prior_ref, *refs):
-        x_refs, refs = refs[:QUAD], refs[QUAD:]
-        noise_out, partial_ref, kept_ref, given_ref, cross_ref, var_ref, ridge_ref, mask_ref, old_ref, sems = refs
+    def kernel(block_ref, valid_ref, geno_ref, coef_ref, noise_ref, *refs):
+        wanted, x_refs, refs = refs[:4], refs[4 : 4 + QUAD], refs[4 + QUAD :]
+        noise_out, partial_ref, kept_ref, given_ref, cross_ref, var_ref, ridge_ref, mask_ref, old_ref, *landed, sems = refs
         me = lax.axis_index("ppl")
         own = place_in_quad()
         copies = []
@@ -124,7 +124,12 @@
             copies.append(pair)
         start = pl.multiple_of(own * quarter, LANES)
         last = pltpu.make_async_copy(noise_ref.at[:, pl.ds(start, quarter)], noise_out, sems.at[2 * QUAD])
-        last.start()
+        small = [pltpu.make_async_copy(a, b, sems.at[2 * QUAD + 1 + k]) for k, (a, b) in enumerate(zip(wanted, landed))]
+        for copy in (*small, last):
+            copy.start()
+        for copy in small:
+            copy.wait()
+        res_ref, people_ref, sigma_ref, prior_ref = landed
         noise_var = to_column(sigma_ref[...], traits)
         var_ref[...] = noise_var
         ridge_ref[...] = to_column(prior_ref[...], traits)
@@ -163,9 +168,13 @@
         kernel,
         compiler_params=PARAMS,
         out_shape=out_shape,
-        in_specs=[SMEM, SMEM, ANY, ANY, ANY] + [VMEM] * 4,
+        in_specs=[SMEM, SMEM] + [HBM] * 7,
         out_specs=[VMEM] * len(out_shape),
-        scratch_shapes=[pltpu.VMEM((QUAD, traits, quarter), F32), pltpu.SemaphoreType.DMA((2 * QUAD + 1,))],
+        scratch_shapes=[
+            pltpu.VMEM((QUAD, traits, quarter), F32),
+            *(pltpu.VMEM(array.shape, F32) for array in (residual, noise_people, sigma2_old, prior_prec)),
+            pltpu.SemaphoreType.DMA((2 * QUAD + 5,)),
+        ],
     )(block_index, valid_counts, genotypes, coef_all, noise_coef, residual, noise_people, sigma2_old, prior_prec)
 
 
@@ -237,7 +246,10 @@
     rounded = state[0].astype(BF16)
     rows = mask.shape[1] // QUAD
     energy = by_pairs([row_sum(part) for part in slots_of(state[0] * rounded.astype(F32), rows)])
-    total = by_pairs([dot(part, block) for part, block in zip(slots_of(rounded, rows), x)])
+    total, at = 0.0, 0
+    for block in x:
+        total += dot(rounded[:, at : at + block.shape[0]], block)
+        at += block.shape[0]
     return pack(total, [energy], kind), *state
 
 
@@ -257,7 +269,7 @@
     blocks = coef_all.shape[1] // width
     kept = ITERS - 1
     args = [*got, norm, length, noise_var, ridge, gamma, before, image, *steps, *betas, *early, *late]
-    split = [len(got), 7, kept, kept, QUAD, QUAD]
+    split = [len(got), 7, kept, kept, kept * QUAD, QUAD]
 
     def kernel(block_ref, valid_ref, *refs):
         groups, at = [], 0
@@ -289,7 +301,7 @@
         for slot in range(QUAD):
             value = scale[kept] * late[slot][...].astype(F32)
             for k in range(kept):
-                value += scale[k] * early[slot][k * traits : (k + 1) * traits].astype(F32)
+                value += scale[k] * early[k * QUAD + slot][...].astype(F32)
             scratch[slot] = value
             give(slot).start()
         res_ref[...] = before[:, :rows] - step * image[...]
@@ -308,7 +320,7 @@
         compiler_params=PARAMS,
         out_shape=[shape(coef_all.shape, F32), shape((traits, rows), F32), shape((1, traits), F32)],
         in_specs=[SMEM, SMEM] + [VMEM] * (len(args) + 1),
-        out_specs=[ANY, VMEM, VMEM],
+        out_specs=[HBM, VMEM, VMEM],
         scratch_shapes=[pltpu.VMEM((QUAD, traits, quarter), F32), pltpu.SemaphoreType.DMA((blocks + QUAD,))],
     )(block_index, valid_counts, *args, coef_all)
 
@@ -354,20 +366,24 @@
             else:
                 (x,) = fuse(add, *got)
 
-    made = prepare(
-        block_index, valid_counts, genotypes, coef_all, noise_coef, residual, noise_people, sigma2_old[None, :], prior_prec[None, :]
-    )
+    ahead = rows // 2
+    corner = (0, (place_in_quad() ^ 2) * (width // QUAD))
+    head = swap(lax.dynamic_slice(genotypes, corner, (ahead, width // QUAD)), 2)
+    columns = sigma2_old[None, :], prior_prec[None, :]
+    made = prepare(block_index, valid_counts, genotypes, coef_all, noise_coef, residual, noise_people, *columns)
     x_give, (noise_quarter, partial_res, kept, given, sent, noise_var, ridge, mask) = made[:QUAD], made[QUAD:]
     lines = kept.shape[0]
     back = swap(sent, 1)
     given = given + back[lines:]
+    x_give = [x_give[0], x_give[1], x_give[2][ahead:], x_give[3]]
     given, x_give = lax.optimization_barrier((given, x_give))
     far = swap(given, 2)
     kept = kept + back[:lines] + far
-    x = [x_give[0]] + [swap(x_give[slot], slot) for slot in (1, 2, 3)]
+    near, across, far_x = (swap(x_give[slot], slot) for slot in (1, 2, 3))
+    x = [x_give[0], near, head, across, far_x]
     got = over_z(kept, 0)
 
-    steps, betas, lows = [], [], []
+    steps, betas, early = [], [], []
     for number in range(ITERS):
         if number == 0:
             sent, search, low = fuse(first_search, *got, noise_quarter, noise_var, ridge, *x)
@@ -376,7 +392,6 @@
                 next_search, *got, search, direction, image, before, norm, length, noise_var, ridge, *x
             )
             steps.append(step)
-        lows.append(low)
         (sent,) = fuse(functools.partial(over_core, IMAGE_KIND[number], 3 if number else 2, traits, rows), sent, swap(sent, 1))
         back = swap(sent, 2)
         if number == ITERS - 1:
@@ -390,13 +405,11 @@
         if number:
             betas.append(beta)
         got = over_z(sent, 1)
+        spread = share(low) + (share(partial_res) if number == 0 else [])
+        got, spread = lax.optimization_barrier((got, spread))
         if number == 0:
-            before = share(partial_res)
-            got, before = lax.optimization_barrier((got, before))
-            before = jnp.concatenate(before, axis=1)
-        if number == ITERS - 2:
-            early = share(jnp.concatenate(lows, axis=0))
-            got, early = lax.optimization_barrier((got, early))
+            before = jnp.concatenate(spread[QUAD:], axis=1)
+        early += spread[:QUAD]
 
     late = share(low)
     got = over_z(sent, 4)

time: 122 us -> 116 us (0.951)
  waiting for transfers between devices: 55.6 us -> 41.9 us
  starting transfers between devices: 45.1 us -> 51.3 us
    ppermute x37 -> x44, waiting for transfers between devices: 55.6 us -> 41.9 us  [swap(): return lax.ppermute(x, 'ppl', [(i, i ^ distance) for i in range(count)])]
    ppermute x37 -> x44, starting transfers between devices: 45.1 us -> 51.3 us  [swap(): return lax.ppermute(x, 'ppl', [(i, i ^ distance) for i in range(count)])]
    unnamed x24 -> x22, local copies, waits for them, and re-layouts: 7.37 us -> 7.36 us
  transfers between devices with their start and end apart: 37 -> 44, of which waited for: 23 -> 18; matrix products, arithmetic and copies ran while one was open for 0% -> 1% of each run, Pallas kernels for 1% -> 2%
where the time goes in v5:
time: 116 us; the launch traced here: 115 us
  starting transfers between devices  51.3 us (44%)
  waiting for transfers between devices  41.9 us (36%)
  Pallas kernels  12.1 us (10%)
  local copies, waits for them, and re-layouts  8.34 us (7%)
  between operations  1.48 us (1%)
    ppermute x44, starting transfers between devices, swap(): return lax.ppermute(x, 'ppl', [(i, i ^ distance) for i in range(count)])  51.3 us
    ppermute x44, waiting for transfers between devices, swap(): return lax.ppermute(x, 'ppl', [(i, i ^ distance) for i in range(count)])  41.9 us
    unnamed x22, local copies, waits for them, and re-layouts  7.36 us
    pallas_call x12, Pallas kernels, fuse(): pl.pallas_call(kernel, out_shape=shapes, compiler_params=PARAMS, in_specs...  6.72 us
    pallas_call x1, Pallas kernels, prepare(): pl.pallas_call(kernel, compiler_params=PARAMS, out_shape=out_shape, in_sp...  2.98 us
    pallas_call x1, Pallas kernels, finish(): pl.pallas_call(kernel, compiler_params=PARAMS, out_shape=[shape(coef_all....  2.42 us
  transfers between devices with their start and end apart: 44, of which 18 were waited for; matrix products, arithmetic and copies ran while one was open for 1% of the time, Pallas kernels for 2%

profile of v5, /device:TPU:0, one launch (start us, length us, event | category | flops | bytes accessed | tf_op | source)
XLA Modules:
  0.0 115.2 jit_solution(16868019393846964211)
XLA Ops:
  2.5 1.6 %copy-done.2 = bf16[256,4096]{1,0:T(8,128)(2,1)S(1)} copy-done((bf16[256,4096]{1,0:T(8,128)(2,1)S(1)}, bf16[256,4096]{1,0:T(8,128)(2,1)}, u32[]{:S(2)}) %copy-start.2) | copy-done | bytes 2097176
  8.6 3.0 %shard_map.121 = (bf16[256,1024]{1,0:T(8,128)(2,1)S(1)}, bf16[256,1024]{1,0:T(8,128)(2,1)S(1)}, bf16[256,1024]{1,0:T(8,128)(2,1)S(1)}, bf16[256,1024]{1,0:T(8,12...) custom-call(s32[1]{0:T(128)S(6)} %copy.13.block_ref, ...), custom_call_target="tpu_custom_call" | custom-call | tf_op jit(solution)/shard_map/pallas_call | solution.py:167
  13.4 2.9 %collective-permute-start.1 = (f32[256,128]{1,0:T(8,128)S(1)}, f32[256,128]{1,0:T(8,128)S(1)}, u32[]{:S(2)}, u32[]{:S(2)}) collective-permute-start(f32[256,128]{1,0:T(8,128)S(1)} %slice_add_fusion), channel_id=1, source_target_pairs={{0,2},{1,3},{2,0},{3,1},{4,6},{5,7},{6,4},{7,5},{8,10},{9,11},{10,... | collective-permute-start | bytes 393224 | tf_op jit(solution)/shard_map/ppermute | solution.py:346
  17.5 2.0 %collective-permute-start.6 = (bf16[128,1024]{1,0:T(8,128)(2,1)S(1)}, bf16[128,1024]{1,0:T(8,128)(2,1)S(1)}, u32[]{:S(2)}, u32[]{:S(2)}) collective-permute-start(bf16[128,1024]{1,0:T(8,128)(2,1)S(1)} %constant_dynamic-slice_fusion), channel_id=1, source_target_pairs={{0,2},{1,3},{2,0},{3,1},{4,6},{5,7},{6,4},{7,5},{8,10},{9,11},{10,... | collective-permute-start | bytes 786440 | tf_op jit(solution)/shard_map/ppermute | solution.py:346
  20.7 4.2 %collective-permute-start.4 = (f32[256,128]{1,0:T(8,128)S(1)}, f32[256,128]{1,0:T(8,128)S(1)}, u32[]{:S(2)}, u32[]{:S(2)}) collective-permute-start(f32[256,128]{1,0:T(8,128)S(1)} %fusion.refs_0_), channel_id=1, source_target_pairs={{0,12},{1,13},{2,14},{3,15},{4,8},{5,9},{6,10},{7,11},{8,4},{9,5},... | collective-permute-start | bytes 393224 | tf_op jit(solution)/shard_map/ppermute | solution.py:346
  24.8 1.5 %collective-permute-start.7 = (bf16[128,1024]{1,0:T(8,128)(2,1)S(1)}, bf16[128,1024]{1,0:T(8,128)(2,1)S(1)}, u32[]{:S(2)}, u32[]{:S(2)}) collective-permute-start(bf16[128,1024]{1,0:T(8,128)(2,1)S(1)} %slice.11), channel_id=1, source_target_pairs={{0,2},{1,3},{2,0},{3,1},{4,6},{5,7},{6,4},{7,5},{8,10},{9,11},{10,... | collective-permute-start | bytes 786440 | tf_op jit(solution)/shard_map/ppermute | solution.py:346
  26.4 11.1 %collective-permute-done.6.refs_9_.refs_6_.refs_14_.refs_10_ = bf16[128,1024]{1,0:T(8,128)(2,1)S(1)} collective-permute-done((bf16[128,1024]{1,0:T(8,128)(2,1)S(1)}, bf16[128,1024]{1,0:T(8,128)(2,1)S(1)}, u32[]{:S(2)}, u32[]{:S(2)}) %collective-permute-start.6) | collective-permute-done | bytes 262176 | tf_op jit(solution)/shard_map/ppermute | solution.py:346
  37.5 3.1 %collective-permute-start.3 = (f32[256,128]{1,0:T(8,128)S(1)}, f32[256,128]{1,0:T(8,128)S(1)}, u32[]{:S(2)}, u32[]{:S(2)}) collective-permute-start(f32[256,128]{1,0:T(8,128)S(1)} %fusion.refs_0_), channel_id=1, source_target_pairs={{0,8},{1,9},{2,10},{3,11},{4,12},{5,13},{6,14},{7,15},{8,0},{9,1},... | collective-permute-start | bytes 393224 | tf_op jit(solution)/shard_map/ppermute | solution.py:346
  40.6 1.6 %collective-permute-start.2 = (f32[256,128]{1,0:T(8,128)S(1)}, f32[256,128]{1,0:T(8,128)S(1)}, u32[]{:S(2)}, u32[]{:S(2)}) collective-permute-start(f32[256,128]{1,0:T(8,128)S(1)} %fusion.refs_0_), channel_id=1, source_target_pairs={{0,4},{1,5},{2,6},{3,7},{4,0},{5,1},{6,2},{7,3},{8,12},{9,13},{10,... | collective-permute-start | bytes 393224 | tf_op jit(solution)/shard_map/ppermute | solution.py:346
  42.2 3.6 %collective-permute-done.3.refs_2_ = f32[256,128]{1,0:T(8,128)S(1)} collective-permute-done((f32[256,128]{1,0:T(8,128)S(1)}, f32[256,128]{1,0:T(8,128)S(1)}, u32[]{:S(2)}, u32[]{:S(2)}) %collective-permute-start.3) | collective-permute-done | bytes 131104 | tf_op jit(solution)/shard_map/ppermute | solution.py:346
  48.1 1.5 %collective-permute-start.10 = (f32[264,128]{1,0:T(8,128)S(1)}, f32[264,128]{1,0:T(8,128)S(1)}, u32[]{:S(2)}, u32[]{:S(2)}) collective-permute-start(f32[264,128]{1,0:T(8,128)S(1)} %shard_map.123.refs_0_), channel_id=1, source_target_pairs={{0,2},{1,3},{2,0},{3,1},{4,6},{5,7},{6,4},{7,5},{8,10},{9,11},{10,... | collective-permute-start | bytes 405512 | tf_op jit(solution)/shard_map/ppermute | solution.py:346
  49.7 1.7 %collective-permute-start.19 = (f32[32,256]{1,0:T(8,128)S(1)}, f32[32,256]{1,0:T(8,128)S(1)}, u32[]{:S(2)}, u32[]{:S(2)}) collective-permute-start(f32[32,256]{1,0:T(8,128)S(1)} %get-tuple-element.117), channel_id=1, source_target_pairs={{0,3},{1,2},{2,1},{3,0},{4,7},{5,6},{6,5},{7,4},{8,11},{9,10},{10,... | collective-permute-start | bytes 98312 | tf_op jit(solution)/shard_map/ppermute | solution.py:346
  52.0 2.7 %collective-permute-done.10.refs_1_ = f32[264,128]{1,0:T(8,128)S(1)} collective-permute-done((f32[264,128]{1,0:T(8,128)S(1)}, f32[264,128]{1,0:T(8,128)S(1)}, u32[]{:S(2)}, u32[]{:S(2)}) %collective-permute-start.10) | collective-permute-done | bytes 135200 | tf_op jit(solution)/shard_map/ppermute | solution.py:346
  55.6 3.0 %collective-permute-start.13 = (bf16[264,128]{1,0:T(8,128)(2,1)S(1)}, bf16[264,128]{1,0:T(8,128)(2,1)S(1)}, u32[]{:S(2)}, u32[]{:S(2)}) collective-permute-start(bf16[264,128]{1,0:T(8,128)(2,1)S(1)} %get-tuple-element.110.refs_0_), channel_id=1, source_target_pairs={{0,12},{1,13},{2,14},{3,15},{4,8},{5,9},{6,10},{7,11},{8,4},{9,5},... | collective-permute-start | bytes 202760 | tf_op jit(solution)/shard_map/ppermute | solution.py:346
  60.0 1.5 %collective-permute-start.15 = (bf16[32,1024]{1,0:T(8,128)(2,1)S(1)}, bf16[32,1024]{1,0:T(8,128)(2,1)S(1)}, u32[]{:S(2)}, u32[]{:S(2)}) collective-permute-start(bf16[32,1024]{1,0:T(8,128)(2,1)S(1)} %get-tuple-element.162.refs_3_.refs_17_), channel_id=1, source_target_pairs={{0,2},{1,3},{2,0},{3,1},{4,6},{5,7},{6,4},{7,5},{8,10},{9,11},{10,... | collective-permute-start | bytes 196616 | tf_op jit(solution)/shard_map/ppermute | solution.py:346
  61.5 2.8 %collective-permute-done.15.refs_19_ = bf16[32,1024]{1,0:T(8,128)(2,1)S(1)} collective-permute-done((bf16[32,1024]{1,0:T(8,128)(2,1)S(1)}, bf16[32,1024]{1,0:T(8,128)(2,1)S(1)}, u32[]{:S(2)}, u32[]{:S(2)}) %collective-permute-start.15) | collective-permute-done | bytes 65568 | tf_op jit(solution)/shard_map/ppermute | solution.py:346
  66.7 1.6 %collective-permute-start.21 = (bf16[272,128]{1,0:T(8,128)(2,1)S(1)}, bf16[272,128]{1,0:T(8,128)(2,1)S(1)}, u32[]{:S(2)}, u32[]{:S(2)}) collective-permute-start(bf16[272,128]{1,0:T(8,128)(2,1)S(1)} %shard_map.126.refs_0_), channel_id=1, source_target_pairs={{0,2},{1,3},{2,0},{3,1},{4,6},{5,7},{6,4},{7,5},{8,10},{9,11},{10,... | collective-permute-start | bytes 208904 | tf_op jit(solution)/shard_map/ppermute | solution.py:346
  68.3 2.8 %collective-permute-done.21.refs_1_ = bf16[272,128]{1,0:T(8,128)(2,1)S(1)} collective-permute-done((bf16[272,128]{1,0:T(8,128)(2,1)S(1)}, bf16[272,128]{1,0:T(8,128)(2,1)S(1)}, u32[]{:S(2)}, u32[]{:S(2)}) %collective-permute-start.21) | collective-permute-done | bytes 69664 | tf_op jit(solution)/shard_map/ppermute | solution.py:346
  71.7 3.1 %collective-permute-start.24 = (bf16[264,128]{1,0:T(8,128)(2,1)S(1)}, bf16[264,128]{1,0:T(8,128)(2,1)S(1)}, u32[]{:S(2)}, u32[]{:S(2)}) collective-permute-start(bf16[264,128]{1,0:T(8,128)(2,1)S(1)} %get-tuple-element.126.refs_0_), channel_id=1, source_target_pairs={{0,12},{1,13},{2,14},{3,15},{4,8},{5,9},{6,10},{7,11},{8,4},{9,5},... | collective-permute-start | bytes 202760 | tf_op jit(solution)/shard_map/ppermute | solution.py:346
  76.1 2.2 %collective-permute-start.26 = (bf16[32,1024]{1,0:T(8,128)(2,1)S(1)}, bf16[32,1024]{1,0:T(8,128)(2,1)S(1)}, u32[]{:S(2)}, u32[]{:S(2)}) collective-permute-start(bf16[32,1024]{1,0:T(8,128)(2,1)S(1)} %get-tuple-element.166.refs_3_.refs_21_), channel_id=1, source_target_pairs={{0,2},{1,3},{2,0},{3,1},{4,6},{5,7},{6,4},{7,5},{8,10},{9,11},{10,... | collective-permute-start | bytes 196616 | tf_op jit(solution)/shard_map/ppermute | solution.py:346
  78.3 2.2 %collective-permute-done.26.refs_23_ = bf16[32,1024]{1,0:T(8,128)(2,1)S(1)} collective-permute-done((bf16[32,1024]{1,0:T(8,128)(2,1)S(1)}, bf16[32,1024]{1,0:T(8,128)(2,1)S(1)}, u32[]{:S(2)}, u32[]{:S(2)}) %collective-permute-start.26) | collective-permute-done | bytes 65568 | tf_op jit(solution)/shard_map/ppermute | solution.py:346
  82.9 2.1 %collective-permute-start.29 = (bf16[272,128]{1,0:T(8,128)(2,1)S(1)}, bf16[272,128]{1,0:T(8,128)(2,1)S(1)}, u32[]{:S(2)}, u32[]{:S(2)}) collective-permute-start(bf16[272,128]{1,0:T(8,128)(2,1)S(1)} %shard_map.129.refs_0_), channel_id=1, source_target_pairs={{0,2},{1,3},{2,0},{3,1},{4,6},{5,7},{6,4},{7,5},{8,10},{9,11},{10,... | collective-permute-start | bytes 208904 | tf_op jit(solution)/shard_map/ppermute | solution.py:346
  85.0 2.5 %collective-permute-done.29.refs_1_ = bf16[272,128]{1,0:T(8,128)(2,1)S(1)} collective-permute-done((bf16[272,128]{1,0:T(8,128)(2,1)S(1)}, bf16[272,128]{1,0:T(8,128)(2,1)S(1)}, u32[]{:S(2)}, u32[]{:S(2)}) %collective-permute-start.29) | collective-permute-done | bytes 69664 | tf_op jit(solution)/shard_map/ppermute | solution.py:346
  88.1 3.1 %collective-permute-start.32 = (bf16[264,128]{1,0:T(8,128)(2,1)S(1)}, bf16[264,128]{1,0:T(8,128)(2,1)S(1)}, u32[]{:S(2)}, u32[]{:S(2)}) collective-permute-start(bf16[264,128]{1,0:T(8,128)(2,1)S(1)} %get-tuple-element.139.refs_0_), channel_id=1, source_target_pairs={{0,12},{1,13},{2,14},{3,15},{4,8},{5,9},{6,10},{7,11},{8,4},{9,5},... | collective-permute-start | bytes 202760 | tf_op jit(solution)/shard_map/ppermute | solution.py:346
  92.6 2.4 %collective-permute-start.34 = (bf16[32,1024]{1,0:T(8,128)(2,1)S(1)}, bf16[32,1024]{1,0:T(8,128)(2,1)S(1)}, u32[]{:S(2)}, u32[]{:S(2)}) collective-permute-start(bf16[32,1024]{1,0:T(8,128)(2,1)S(1)} %get-tuple-element.170.refs_3_.refs_25_), channel_id=1, source_target_pairs={{0,2},{1,3},{2,0},{3,1},{4,6},{5,7},{6,4},{7,5},{8,10},{9,11},{10,... | collective-permute-start | bytes 196616 | tf_op jit(solution)/shard_map/ppermute | solution.py:346
  95.0 2.2 %collective-permute-done.34.refs_27_ = bf16[32,1024]{1,0:T(8,128)(2,1)S(1)} collective-permute-done((bf16[32,1024]{1,0:T(8,128)(2,1)S(1)}, bf16[32,1024]{1,0:T(8,128)(2,1)S(1)}, u32[]{:S(2)}, u32[]{:S(2)}) %collective-permute-start.34) | collective-permute-done | bytes 65568 | tf_op jit(solution)/shard_map/ppermute | solution.py:346
  97.3 1.4 %shard_map.131 = (f32[264,128]{1,0:T(8,128)S(1)}, f32[32,1024]{1,0:T(8,128)}, bf16[32,1024]{1,0:T(8,128)(2,1)S(1)}, f32[32,1024]{1,0:T(8,128)S(1)}, f32[32,1]{1,0:T(8,128)S(1)}) custom-call(bf16[264,128]{1,0:T(8,128)(2,1)S(1)} %get-tuple-element.139.refs_0_, bf16[264,128]{1,0:T(8,128)(2,1)S(1)} %collective-permute-done.30.refs_1_, ...), custom_call_target="tpu_custom_call" | custom-call | tf_op jit(solution)/shard_map/pallas_call | solution.py:97
  100.2 2.1 %collective-permute-start.37 = (bf16[272,128]{1,0:T(8,128)(2,1)S(1)}, bf16[272,128]{1,0:T(8,128)(2,1)S(1)}, u32[]{:S(2)}, u32[]{:S(2)}) collective-permute-start(bf16[272,128]{1,0:T(8,128)(2,1)S(1)} %shard_map.132.refs_0_), channel_id=1, source_target_pairs={{0,2},{1,3},{2,0},{3,1},{4,6},{5,7},{6,4},{7,5},{8,10},{9,11},{10,... | collective-permute-start | bytes 208904 | tf_op jit(solution)/shard_map/ppermute | solution.py:346
  102.3 1.5 %collective-permute-start.42 = (bf16[32,1024]{1,0:T(8,128)(2,1)S(1)}, bf16[32,1024]{1,0:T(8,128)(2,1)S(1)}, u32[]{:S(2)}, u32[]{:S(2)}) collective-permute-start(bf16[32,1024]{1,0:T(8,128)(2,1)S(1)} %get-tuple-element.150.refs_3_.refs_29_), channel_id=1, source_target_pairs={{0,2},{1,3},{2,0},{3,1},{4,6},{5,7},{6,4},{7,5},{8,10},{9,11},{10,... | collective-permute-start | bytes 196616 | tf_op jit(solution)/shard_map/ppermute | solution.py:346
  105.1 3.1 %collective-permute-start.40 = (f32[8,128]{1,0:T(8,128)S(1)}, f32[8,128]{1,0:T(8,128)S(1)}, u32[]{:S(2)}, u32[]{:S(2)}) collective-permute-start(f32[8,128]{1,0:T(8,128)S(1)} %get-tuple-element.152.refs_0_), channel_id=1, source_target_pairs={{0,12},{1,13},{2,14},{3,15},{4,8},{5,9},{6,10},{7,11},{8,4},{9,5},... | collective-permute-start | bytes 12296 | tf_op jit(solution)/shard_map/ppermute | solution.py:346
  110.6 2.1 %collective-permute-done.39.refs_2_ = f32[8,128]{1,0:T(8,128)S(1)} collective-permute-done((f32[8,128]{1,0:T(8,128)S(1)}, f32[8,128]{1,0:T(8,128)S(1)}, u32[]{:S(2)}, u32[]{:S(2)}) %collective-permute-start.39) | collective-permute-done | bytes 4128 | tf_op jit(solution)/shard_map/ppermute | solution.py:346
  112.8 2.4 %shard_map.134 = (f32[32,8192]{1,0:T(8,128)}, f32[32,256]{1,0:T(8,128)}, f32[1,32]{1,0:T(1,128)}) custom-call(s32[1]{0:T(128)S(6)} %copy.13.block_ref, s32[16]{0:T(128)S(1)} %copy-done.7, f32[8,128]{1,0:T(8,128)S(1)} %get-tuple-element.152.refs_0_, f32[8,128]{1,0:T(8,128)S(1)} %collective-permute-done.38.refs_1_, ...), custom_call_target="tpu_custom_call" | custom-call | tf_op jit(solution)/shard_map/pallas_call | solution.py:318
  (97 shorter events, 29.0 us)
Async XLA Ops:
  13.4 7.3 %collective-permute-start.1 = (f32[256,128]{1,0:T(8,128)S(1)}, f32[256,128]{1,0:T(8,128)S(1)}, u32[]{:S(2)}, u32[]{:S(2)}) collective-permute-start(f32[256,128]{1,0:T(8,128)S(1)} %slice_add_fusion), channel_id=1, source_target_pairs={{0,2},{1,3},{2,0},{3,1},{4,6},{5,7},{6,4},{7,5},{8,10},{9,11},{10,... | collective-permute-start | bytes 393224 | tf_op jit(solution)/shard_map/ppermute | solution.py:346
  16.3 29.7 %collective-permute-start.5 = (bf16[256,1024]{1,0:T(8,128)(2,1)S(1)}, bf16[256,1024]{1,0:T(8,128)(2,1)S(1)}, u32[]{:S(2)}, u32[]{:S(2)}) collective-permute-start(bf16[256,1024]{1,0:T(8,128)(2,1)S(1)} %get-tuple-element.102), channel_id=1, source_target_pairs={{0,1},{1,0},{2,3},{3,2},{4,5},{5,4},{6,7},{7,6},{8,9},{9,8},{10,11... | collective-permute-start | bytes 1572872 | tf_op jit(solution)/shard_map/ppermute | solution.py:346
  16.3 29.7 %collective-permute-start.8 = (bf16[256,1024]{1,0:T(8,128)(2,1)S(1)}, bf16[256,1024]{1,0:T(8,128)(2,1)S(1)}, u32[]{:S(2)}, u32[]{:S(2)}) collective-permute-start(bf16[256,1024]{1,0:T(8,128)(2,1)S(1)} %get-tuple-element.104), channel_id=1, source_target_pairs={{0,3},{1,2},{2,1},{3,0},{4,7},{5,6},{6,5},{7,4},{8,11},{9,10},{10,... | collective-permute-start | bytes 1572872 | tf_op jit(solution)/shard_map/ppermute | solution.py:346
  17.5 20.0 %collective-permute-start.6 = (bf16[128,1024]{1,0:T(8,128)(2,1)S(1)}, bf16[128,1024]{1,0:T(8,128)(2,1)S(1)}, u32[]{:S(2)}, u32[]{:S(2)}) collective-permute-start(bf16[128,1024]{1,0:T(8,128)(2,1)S(1)} %constant_dynamic-slice_fusion), channel_id=1, source_target_pairs={{0,2},{1,3},{2,0},{3,1},{4,6},{5,7},{6,4},{7,5},{8,10},{9,11},{10,... | collective-permute-start | bytes 786440 | tf_op jit(solution)/shard_map/ppermute | solution.py:346
  20.7 19.9 %collective-permute-start.4 = (f32[256,128]{1,0:T(8,128)S(1)}, f32[256,128]{1,0:T(8,128)S(1)}, u32[]{:S(2)}, u32[]{:S(2)}) collective-permute-start(f32[256,128]{1,0:T(8,128)S(1)} %fusion.refs_0_), channel_id=1, source_target_pairs={{0,12},{1,13},{2,14},{3,15},{4,8},{5,9},{6,10},{7,11},{8,4},{9,5},... | collective-permute-start | bytes 393224 | tf_op jit(solution)/shard_map/ppermute | solution.py:346
  24.8 21.2 %collective-permute-start.7 = (bf16[128,1024]{1,0:T(8,128)(2,1)S(1)}, bf16[128,1024]{1,0:T(8,128)(2,1)S(1)}, u32[]{:S(2)}, u32[]{:S(2)}) collective-permute-start(bf16[128,1024]{1,0:T(8,128)(2,1)S(1)} %slice.11), channel_id=1, source_target_pairs={{0,2},{1,3},{2,0},{3,1},{4,6},{5,7},{6,4},{7,5},{8,10},{9,11},{10,... | collective-permute-start | bytes 786440 | tf_op jit(solution)/shard_map/ppermute | solution.py:346
  37.5 8.3 %collective-permute-start.3 = (f32[256,128]{1,0:T(8,128)S(1)}, f32[256,128]{1,0:T(8,128)S(1)}, u32[]{:S(2)}, u32[]{:S(2)}) collective-permute-start(f32[256,128]{1,0:T(8,128)S(1)} %fusion.refs_0_), channel_id=1, source_target_pairs={{0,8},{1,9},{2,10},{3,11},{4,12},{5,13},{6,14},{7,15},{8,0},{9,1},... | collective-permute-start | bytes 393224 | tf_op jit(solution)/shard_map/ppermute | solution.py:346
  40.6 5.4 %collective-permute-start.2 = (f32[256,128]{1,0:T(8,128)S(1)}, f32[256,128]{1,0:T(8,128)S(1)}, u32[]{:S(2)}, u32[]{:S(2)}) collective-permute-start(f32[256,128]{1,0:T(8,128)S(1)} %fusion.refs_0_), channel_id=1, source_target_pairs={{0,4},{1,5},{2,6},{3,7},{4,0},{5,1},{6,2},{7,3},{8,12},{9,13},{10,... | collective-permute-start | bytes 393224 | tf_op jit(solution)/shard_map/ppermute | solution.py:346
  48.1 6.5 %collective-permute-start.10 = (f32[264,128]{1,0:T(8,128)S(1)}, f32[264,128]{1,0:T(8,128)S(1)}, u32[]{:S(2)}, u32[]{:S(2)}) collective-permute-start(f32[264,128]{1,0:T(8,128)S(1)} %shard_map.123.refs_0_), channel_id=1, source_target_pairs={{0,2},{1,3},{2,0},{3,1},{4,6},{5,7},{6,4},{7,5},{8,10},{9,11},{10,... | collective-permute-start | bytes 405512 | tf_op jit(solution)/shard_map/ppermute | solution.py:346
  49.7 11.8 %collective-permute-start.16 = (bf16[32,1024]{1,0:T(8,128)(2,1)S(1)}, bf16[32,1024]{1,0:T(8,128)(2,1)S(1)}, u32[]{:S(2)}, u32[]{:S(2)}) collective-permute-start(bf16[32,1024]{1,0:T(8,128)(2,1)S(1)} %get-tuple-element.162.refs_3_.refs_17_), channel_id=1, source_target_pairs={{0,3},{1,2},{2,1},{3,0},{4,7},{5,6},{6,5},{7,4},{8,11},{9,10},{10,... | collective-permute-start | bytes 196616 | tf_op jit(solution)/shard_map/ppermute | solution.py:346
  49.7 9.0 %collective-permute-start.19 = (f32[32,256]{1,0:T(8,128)S(1)}, f32[32,256]{1,0:T(8,128)S(1)}, u32[]{:S(2)}, u32[]{:S(2)}) collective-permute-start(f32[32,256]{1,0:T(8,128)S(1)} %get-tuple-element.117), channel_id=1, source_target_pairs={{0,3},{1,2},{2,1},{3,0},{4,7},{5,6},{6,5},{7,4},{8,11},{9,10},{10,... | collective-permute-start | bytes 98312 | tf_op jit(solution)/shard_map/ppermute | solution.py:346
  51.4 7.3 %collective-permute-start.18 = (f32[32,256]{1,0:T(8,128)S(1)}, f32[32,256]{1,0:T(8,128)S(1)}, u32[]{:S(2)}, u32[]{:S(2)}) collective-permute-start(f32[32,256]{1,0:T(8,128)S(1)} %get-tuple-element.117), channel_id=1, source_target_pairs={{0,2},{1,3},{2,0},{3,1},{4,6},{5,7},{6,4},{7,5},{8,10},{9,11},{10,... | collective-permute-start | bytes 98312 | tf_op jit(solution)/shard_map/ppermute | solution.py:346
  52.0 8.0 %collective-permute-start.17 = (f32[32,256]{1,0:T(8,128)S(1)}, f32[32,256]{1,0:T(8,128)S(1)}, u32[]{:S(2)}, u32[]{:S(2)}) collective-permute-start(f32[32,256]{1,0:T(8,128)S(1)} %get-tuple-element.117), channel_id=1, source_target_pairs={{0,1},{1,0},{2,3},{3,2},{4,5},{5,4},{6,7},{7,6},{8,9},{9,8},{10,11... | collective-permute-start | bytes 98312 | tf_op jit(solution)/shard_map/ppermute | solution.py:346
  55.6 8.7 %collective-permute-start.13 = (bf16[264,128]{1,0:T(8,128)(2,1)S(1)}, bf16[264,128]{1,0:T(8,128)(2,1)S(1)}, u32[]{:S(2)}, u32[]{:S(2)}) collective-permute-start(bf16[264,128]{1,0:T(8,128)(2,1)S(1)} %get-tuple-element.110.refs_0_), channel_id=1, source_target_pairs={{0,12},{1,13},{2,14},{3,15},{4,8},{5,9},{6,10},{7,11},{8,4},{9,5},... | collective-permute-start | bytes 202760 | tf_op jit(solution)/shard_map/ppermute | solution.py:346
  58.7 5.6 %collective-permute-start.12 = (bf16[264,128]{1,0:T(8,128)(2,1)S(1)}, bf16[264,128]{1,0:T(8,128)(2,1)S(1)}, u32[]{:S(2)}, u32[]{:S(2)}) collective-permute-start(bf16[264,128]{1,0:T(8,128)(2,1)S(1)} %get-tuple-element.110.refs_0_), channel_id=1, source_target_pairs={{0,8},{1,9},{2,10},{3,11},{4,12},{5,13},{6,14},{7,15},{8,0},{9,1},... | collective-permute-start | bytes 202760 | tf_op jit(solution)/shard_map/ppermute | solution.py:346
  58.7 5.6 %collective-permute-start.11 = (bf16[264,128]{1,0:T(8,128)(2,1)S(1)}, bf16[264,128]{1,0:T(8,128)(2,1)S(1)}, u32[]{:S(2)}, u32[]{:S(2)}) collective-permute-start(bf16[264,128]{1,0:T(8,128)(2,1)S(1)} %get-tuple-element.110.refs_0_), channel_id=1, source_target_pairs={{0,4},{1,5},{2,6},{3,7},{4,0},{5,1},{6,2},{7,3},{8,12},{9,13},{10,... | collective-permute-start | bytes 202760 | tf_op jit(solution)/shard_map/ppermute | solution.py:346
  68.3 10.0 %collective-permute-start.27 = (bf16[32,1024]{1,0:T(8,128)(2,1)S(1)}, bf16[32,1024]{1,0:T(8,128)(2,1)S(1)}, u32[]{:S(2)}, u32[]{:S(2)}) collective-permute-start(bf16[32,1024]{1,0:T(8,128)(2,1)S(1)} %get-tuple-element.166.refs_3_.refs_21_), channel_id=1, source_target_pairs={{0,3},{1,2},{2,1},{3,0},{4,7},{5,6},{6,5},{7,4},{8,11},{9,10},{10,... | collective-permute-start | bytes 196616 | tf_op jit(solution)/shard_map/ppermute | solution.py:346
  71.7 8.8 %collective-permute-start.24 = (bf16[264,128]{1,0:T(8,128)(2,1)S(1)}, bf16[264,128]{1,0:T(8,128)(2,1)S(1)}, u32[]{:S(2)}, u32[]{:S(2)}) collective-permute-start(bf16[264,128]{1,0:T(8,128)(2,1)S(1)} %get-tuple-element.126.refs_0_), channel_id=1, source_target_pairs={{0,12},{1,13},{2,14},{3,15},{4,8},{5,9},{6,10},{7,11},{8,4},{9,5},... | collective-permute-start | bytes 202760 | tf_op jit(solution)/shard_map/ppermute | solution.py:346
  74.8 5.7 %collective-permute-start.23 = (bf16[264,128]{1,0:T(8,128)(2,1)S(1)}, bf16[264,128]{1,0:T(8,128)(2,1)S(1)}, u32[]{:S(2)}, u32[]{:S(2)}) collective-permute-start(bf16[264,128]{1,0:T(8,128)(2,1)S(1)} %get-tuple-element.126.refs_0_), channel_id=1, source_target_pairs={{0,8},{1,9},{2,10},{3,11},{4,12},{5,13},{6,14},{7,15},{8,0},{9,1},... | collective-permute-start | bytes 202760 | tf_op jit(solution)/shard_map/ppermute | solution.py:346
  74.8 5.7 %collective-permute-start.22 = (bf16[264,128]{1,0:T(8,128)(2,1)S(1)}, bf16[264,128]{1,0:T(8,128)(2,1)S(1)}, u32[]{:S(2)}, u32[]{:S(2)}) collective-permute-start(bf16[264,128]{1,0:T(8,128)(2,1)S(1)} %get-tuple-element.126.refs_0_), channel_id=1, source_target_pairs={{0,4},{1,5},{2,6},{3,7},{4,0},{5,1},{6,2},{7,3},{8,12},{9,13},{10,... | collective-permute-start | bytes 202760 | tf_op jit(solution)/shard_map/ppermute | solution.py:346
  82.9 4.6 %collective-permute-start.29 = (bf16[272,128]{1,0:T(8,128)(2,1)S(1)}, bf16[272,128]{1,0:T(8,128)(2,1)S(1)}, u32[]{:S(2)}, u32[]{:S(2)}) collective-permute-start(bf16[272,128]{1,0:T(8,128)(2,1)S(1)} %shard_map.129.refs_0_), channel_id=1, source_target_pairs={{0,2},{1,3},{2,0},{3,1},{4,6},{5,7},{6,4},{7,5},{8,10},{9,11},{10,... | collective-permute-start | bytes 208904 | tf_op jit(solution)/shard_map/ppermute | solution.py:346
  85.0 10.0 %collective-permute-start.35 = (bf16[32,1024]{1,0:T(8,128)(2,1)S(1)}, bf16[32,1024]{1,0:T(8,128)(2,1)S(1)}, u32[]{:S(2)}, u32[]{:S(2)}) collective-permute-start(bf16[32,1024]{1,0:T(8,128)(2,1)S(1)} %get-tuple-element.170.refs_3_.refs_25_), channel_id=1, source_target_pairs={{0,3},{1,2},{2,1},{3,0},{4,7},{5,6},{6,5},{7,4},{8,11},{9,10},{10,... | collective-permute-start | bytes 196616 | tf_op jit(solution)/shard_map/ppermute | solution.py:346
  88.1 9.1 %collective-permute-start.32 = (bf16[264,128]{1,0:T(8,128)(2,1)S(1)}, bf16[264,128]{1,0:T(8,128)(2,1)S(1)}, u32[]{:S(2)}, u32[]{:S(2)}) collective-permute-start(bf16[264,128]{1,0:T(8,128)(2,1)S(1)} %get-tuple-element.139.refs_0_), channel_id=1, source_target_pairs={{0,12},{1,13},{2,14},{3,15},{4,8},{5,9},{6,10},{7,11},{8,4},{9,5},... | collective-permute-start | bytes 202760 | tf_op jit(solution)/shard_map/ppermute | solution.py:346
  91.2 6.0 %collective-permute-start.31 = (bf16[264,128]{1,0:T(8,128)(2,1)S(1)}, bf16[264,128]{1,0:T(8,128)(2,1)S(1)}, u32[]{:S(2)}, u32[]{:S(2)}) collective-permute-start(bf16[264,128]{1,0:T(8,128)(2,1)S(1)} %get-tuple-element.139.refs_0_), channel_id=1, source_target_pairs={{0,8},{1,9},{2,10},{3,11},{4,12},{5,13},{6,14},{7,15},{8,0},{9,1},... | collective-permute-start | bytes 202760 | tf_op jit(solution)/shard_map/ppermute | solution.py:346
  91.2 6.0 %collective-permute-start.30 = (bf16[264,128]{1,0:T(8,128)(2,1)S(1)}, bf16[264,128]{1,0:T(8,128)(2,1)S(1)}, u32[]{:S(2)}, u32[]{:S(2)}) collective-permute-start(bf16[264,128]{1,0:T(8,128)(2,1)S(1)} %get-tuple-element.139.refs_0_), channel_id=1, source_target_pairs={{0,4},{1,5},{2,6},{3,7},{4,0},{5,1},{6,2},{7,3},{8,12},{9,13},{10,... | collective-permute-start | bytes 202760 | tf_op jit(solution)/shard_map/ppermute | solution.py:346
  92.6 4.7 %collective-permute-start.34 = (bf16[32,1024]{1,0:T(8,128)(2,1)S(1)}, bf16[32,1024]{1,0:T(8,128)(2,1)S(1)}, u32[]{:S(2)}, u32[]{:S(2)}) collective-permute-start(bf16[32,1024]{1,0:T(8,128)(2,1)S(1)} %get-tuple-element.170.refs_3_.refs_25_), channel_id=1, source_target_pairs={{0,2},{1,3},{2,0},{3,1},{4,6},{5,7},{6,4},{7,5},{8,10},{9,11},{10,... | collective-permute-start | bytes 196616 | tf_op jit(solution)/shard_map/ppermute | solution.py:346
  100.2 4.7 %collective-permute-start.37 = (bf16[272,128]{1,0:T(8,128)(2,1)S(1)}, bf16[272,128]{1,0:T(8,128)(2,1)S(1)}, u32[]{:S(2)}, u32[]{:S(2)}) collective-permute-start(bf16[272,128]{1,0:T(8,128)(2,1)S(1)} %shard_map.132.refs_0_), channel_id=1, source_target_pairs={{0,2},{1,3},{2,0},{3,1},{4,6},{5,7},{6,4},{7,5},{8,10},{9,11},{10,... | collective-permute-start | bytes 208904 | tf_op jit(solution)/shard_map/ppermute | solution.py:346
  102.2 6.0 %collective-permute-start.43 = (bf16[32,1024]{1,0:T(8,128)(2,1)S(1)}, bf16[32,1024]{1,0:T(8,128)(2,1)S(1)}, u32[]{:S(2)}, u32[]{:S(2)}) collective-permute-start(bf16[32,1024]{1,0:T(8,128)(2,1)S(1)} %get-tuple-element.150.refs_3_.refs_29_), channel_id=1, source_target_pairs={{0,3},{1,2},{2,1},{3,0},{4,7},{5,6},{6,5},{7,4},{8,11},{9,10},{10,... | collective-permute-start | bytes 196616 | tf_op jit(solution)/shard_map/ppermute | solution.py:346
  102.3 7.3 %collective-permute-start.42 = (bf16[32,1024]{1,0:T(8,128)(2,1)S(1)}, bf16[32,1024]{1,0:T(8,128)(2,1)S(1)}, u32[]{:S(2)}, u32[]{:S(2)}) collective-permute-start(bf16[32,1024]{1,0:T(8,128)(2,1)S(1)} %get-tuple-element.150.refs_3_.refs_29_), channel_id=1, source_target_pairs={{0,2},{1,3},{2,0},{3,1},{4,6},{5,7},{6,4},{7,5},{8,10},{9,11},{10,... | collective-permute-start | bytes 196616 | tf_op jit(solution)/shard_map/ppermute | solution.py:346
  103.7 5.8 %collective-permute-start.41 = (bf16[32,1024]{1,0:T(8,128)(2,1)S(1)}, bf16[32,1024]{1,0:T(8,128)(2,1)S(1)}, u32[]{:S(2)}, u32[]{:S(2)}) collective-permute-start(bf16[32,1024]{1,0:T(8,128)(2,1)S(1)} %get-tuple-element.150.refs_3_.refs_29_), channel_id=1, source_target_pairs={{0,1},{1,0},{2,3},{3,2},{4,5},{5,4},{6,7},{7,6},{8,9},{9,8},{10,11... | collective-permute-start | bytes 196616 | tf_op jit(solution)/shard_map/ppermute | solution.py:346
  105.1 5.5 %collective-permute-start.40 = (f32[8,128]{1,0:T(8,128)S(1)}, f32[8,128]{1,0:T(8,128)S(1)}, u32[]{:S(2)}, u32[]{:S(2)}) collective-permute-start(f32[8,128]{1,0:T(8,128)S(1)} %get-tuple-element.152.refs_0_), channel_id=1, source_target_pairs={{0,12},{1,13},{2,14},{3,15},{4,8},{5,9},{6,10},{7,11},{8,4},{9,5},... | collective-permute-start | bytes 12296 | tf_op jit(solution)/shard_map/ppermute | solution.py:346
  108.2 4.5 %collective-permute-start.39 = (f32[8,128]{1,0:T(8,128)S(1)}, f32[8,128]{1,0:T(8,128)S(1)}, u32[]{:S(2)}, u32[]{:S(2)}) collective-permute-start(f32[8,128]{1,0:T(8,128)S(1)} %get-tuple-element.152.refs_0_), channel_id=1, source_target_pairs={{0,8},{1,9},{2,10},{3,11},{4,12},{5,13},{6,14},{7,15},{8,0},{9,1},... | collective-permute-start | bytes 12296 | tf_op jit(solution)/shard_map/ppermute | solution.py:346
  (23 other events, 113.3 us)

commit v6 on v5

--- a/solution.py
+++ b/solution.py
@@ -102,34 +102,38 @@
 
 
 def prepare(block_index, valid_counts, genotypes, coef_all, noise_coef, residual, noise_people, sigma2_old, prior_prec):
+    operands = genotypes, coef_all, noise_coef, valid_counts, residual, noise_people, sigma2_old, prior_prec
     rows, width = genotypes.shape
     traits = residual.shape[0]
     quarter = width // QUAD
 
-    def kernel(block_ref, valid_ref, geno_ref, coef_ref, noise_ref, *refs):
-        wanted, x_refs, refs = refs[:4], refs[4 : 4 + QUAD], refs[4 + QUAD :]
-        noise_out, partial_ref, kept_ref, given_ref, cross_ref, var_ref, ridge_ref, mask_ref, old_ref, *landed, sems = refs
+    def kernel(block_ref, geno_ref, coef_ref, noise_ref, *refs):
+        wanted, x_refs, (noise_out, partial_ref, *refs) = refs[:5], refs[5 : 5 + QUAD], refs[5 + QUAD :]
+        kept_ref, given_ref, cross_ref, var_ref, ridge_ref, mask_ref, present_ref, old_ref, *landed, sems = refs
         me = lax.axis_index("ppl")
         own = place_in_quad()
+        small = [pltpu.make_async_copy(a, b, sems.at[2 * QUAD + 1 + k]) for k, (a, b) in enumerate(zip(wanted, landed))]
+        for copy in small:
+            copy.start()
+        valid_ref, res_ref, people_ref, sigma_ref, prior_ref = landed
         copies = []
         for slot in range(QUAD):
-            start = pl.multiple_of((own ^ slot) * quarter, LANES)
-            first = pl.multiple_of(block_ref[0] * width + start, LANES)
+            span = pl.ds(pl.multiple_of((own ^ slot) * quarter, LANES), quarter)
+            first = pl.multiple_of(block_ref[0] * width + (own ^ slot) * quarter, LANES)
             pair = (
-                pltpu.make_async_copy(coef_ref.at[:, pl.ds(first, quarter)], old_ref.at[slot], sems.at[2 * slot]),
-                pltpu.make_async_copy(geno_ref.at[:, pl.ds(start, quarter)], x_refs[slot], sems.at[2 * slot + 1]),
+                pltpu.make_async_copy(coef_ref.at[:, pl.ds(first, quarter)], old_ref.at[slot], sems.at[QUAD + slot]),
+                pltpu.make_async_copy(geno_ref.at[:, span], x_refs[slot], sems.at[slot]),
             )
             for copy in pair:
                 copy.start()
             copies.append(pair)
-        start = pl.multiple_of(own * quarter, LANES)
-        last = pltpu.make_async_copy(noise_ref.at[:, pl.ds(start, quarter)], noise_out, sems.at[2 * QUAD])
-        small = [pltpu.make_async_copy(a, b, sems.at[2 * QUAD + 1 + k]) for k, (a, b) in enumerate(zip(wanted, landed))]
-        for copy in (*small, last):
-            copy.start()
+        span = pl.ds(pl.multiple_of(own * quarter, LANES), quarter)
+        last = pltpu.make_async_copy(noise_ref.at[:, span], noise_out, sems.at[2 * QUAD])
+        last.start()
         for copy in small:
             copy.wait()
-        res_ref, people_ref, sigma_ref, prior_ref = landed
+        present = sum(valid_ref[k] for k in range(valid_counts.shape[0]))
+        present_ref[...] = jnp.full((1, traits), present, jnp.int32).astype(F32)
         noise_var = to_column(sigma_ref[...], traits)
         var_ref[...] = noise_var
         ridge_ref[...] = to_column(prior_ref[...], traits)
@@ -163,19 +167,21 @@
         shape((traits, 1), F32),
         shape((traits, 1), F32),
         shape((1, QUAD * rows), F32),
+        shape((1, traits), F32),
     ]
     return pl.pallas_call(
         kernel,
         compiler_params=PARAMS,
         out_shape=out_shape,
-        in_specs=[SMEM, SMEM] + [HBM] * 7,
+        in_specs=[SMEM] + [HBM] * 8,
         out_specs=[VMEM] * len(out_shape),
         scratch_shapes=[
             pltpu.VMEM((QUAD, traits, quarter), F32),
+            pltpu.SMEM(valid_counts.shape, jnp.int32),
             *(pltpu.VMEM(array.shape, F32) for array in (residual, noise_people, sigma2_old, prior_prec)),
-            pltpu.SemaphoreType.DMA((2 * QUAD + 5,)),
+            pltpu.SemaphoreType.DMA((2 * QUAD + 6,)),
         ],
-    )(block_index, valid_counts, genotypes, coef_all, noise_coef, residual, noise_people, sigma2_old, prior_prec)
+    )(block_index, *(pltpu.with_memory_space_constraint(array, pltpu.HBM) for array in operands))
 
 
 def image_part(search, direction, x):
@@ -194,14 +200,15 @@
     return image_part(total / noise_var + jnp.sqrt(ridge) * noise_coef, None, x)
 
 
-def next_search(got0, got1, got2, got3, search, direction, image, before, norm, length, noise_var, ridge, *x):
+def next_search(first, got0, got1, got2, got3, search, direction, image, norm, length, noise_var, ridge, *x):
+    fitted, x = (0.0, x) if first else (x[0], x[1:])
     traits, quarter = search.shape
     opened = [unpack(got, traits, quarter, 1) for got in (got0, got1, got2, got3)]
     total = by_pairs([wide for wide, _ in opened])
     energy = by_pairs([columns[0] for _, columns in opened])
     step = norm / (energy / noise_var + ridge * length)
     search = search - step * (total / noise_var + ridge * direction)
-    return *image_part(search, direction, x), before - step * image, step
+    return *image_part(search, direction, x), fitted + step * image, step
 
 
 def cross(packed, way, traits, rows):
@@ -253,16 +260,17 @@
     return pack(total, [energy], kind), *state
 
 
-def last_sums(sent, back, mask, low, direction, image, norm_old, length, before):
+def last_sums(sent, back, mask, low, direction, image, norm_old, length, fitted, *partial):
+    before = jnp.concatenate(partial, axis=1) - fitted
     image, _, norm, length, beta = new_image(3, sent, back, mask, low, direction, image, norm_old, length)
     rows = mask.shape[1] // QUAD
     products = (image * image.astype(BF16).astype(F32), before * before, before * image, image * image)
     sums = [to_row(by_pairs([row_sum(part) for part in slots_of(product, rows)])) for product in products]
     packed = jnp.concatenate(sums + [jnp.zeros((TILE - len(sums), LANES), F32)], axis=0)
-    return packed, image[:, :rows], norm, length, beta
-
-
-def finish(block_index, valid_counts, got, norm, length, noise_var, ridge, gamma, before, image, steps, betas, early, late, coef_all):
+    return packed, before[:, :rows], image[:, :rows], norm, length, beta
+
+
+def finish(block_index, present, got, norm, length, noise_var, ridge, gamma, before, image, steps, betas, early, late, coef_all):
     traits, quarter = late[0].shape
     rows = image.shape[1]
     width = QUAD * quarter
@@ -271,7 +279,7 @@
     args = [*got, norm, length, noise_var, ridge, gamma, before, image, *steps, *betas, *early, *late]
     split = [len(got), 7, kept, kept, kept * QUAD, QUAD]
 
-    def kernel(block_ref, valid_ref, *refs):
+    def kernel(block_ref, present_ref, *refs):
         groups, at = [], 0
         for size in split:
             groups.append(refs[at : at + size])
@@ -304,11 +312,10 @@
                 value += scale[k] * early[k * QUAD + slot][...].astype(F32)
             scratch[slot] = value
             give(slot).start()
-        res_ref[...] = before[:, :rows] - step * image[...]
+        res_ref[...] = before[...] - step * image[...]
         squares = squares - step * (2.0 * mixed - step * energy_full)
-        present = sum(valid_ref[k] for k in range(valid_counts.shape[0])).astype(F32)
         row = to_row(squares + PRIOR_DOF * PRIOR_SCALE)[:, :traits]
-        sigma_ref[...] = row / ((present + PRIOR_DOF) * gamma[...])
+        sigma_ref[...] = row / ((present_ref[...] + PRIOR_DOF) * gamma[...])
         for slot in range(QUAD):
             give(slot).wait()
         for index in range(blocks):
@@ -319,10 +326,10 @@
         kernel,
         compiler_params=PARAMS,
         out_shape=[shape(coef_all.shape, F32), shape((traits, rows), F32), shape((1, traits), F32)],
-        in_specs=[SMEM, SMEM] + [VMEM] * (len(args) + 1),
+        in_specs=[SMEM] + [VMEM] * (len(args) + 2),
         out_specs=[HBM, VMEM, VMEM],
         scratch_shapes=[pltpu.VMEM((QUAD, traits, quarter), F32), pltpu.SemaphoreType.DMA((blocks + QUAD,))],
-    )(block_index, valid_counts, *args, coef_all)
+    )(block_index, present, *args, coef_all)
 
 
 def per_device(
@@ -371,7 +378,7 @@
     head = swap(lax.dynamic_slice(genotypes, corner, (ahead, width // QUAD)), 2)
     columns = sigma2_old[None, :], prior_prec[None, :]
     made = prepare(block_index, valid_counts, genotypes, coef_all, noise_coef, residual, noise_people, *columns)
-    x_give, (noise_quarter, partial_res, kept, given, sent, noise_var, ridge, mask) = made[:QUAD], made[QUAD:]
+    x_give, (noise_quarter, partial_res, kept, given, sent, noise_var, ridge, mask, present) = made[:QUAD], made[QUAD:]
     lines = kept.shape[0]
     back = swap(sent, 1)
     given = given + back[lines:]
@@ -382,20 +389,24 @@
     near, across, far_x = (swap(x_give[slot], slot) for slot in (1, 2, 3))
     x = [x_give[0], near, head, across, far_x]
     got = over_z(kept, 0)
+    partial = share(partial_res)
 
     steps, betas, early = [], [], []
     for number in range(ITERS):
         if number == 0:
             sent, search, low = fuse(first_search, *got, noise_quarter, noise_var, ridge, *x)
         else:
-            sent, search, low, before, step = fuse(
-                next_search, *got, search, direction, image, before, norm, length, noise_var, ridge, *x
+            held = () if number == 1 else (fitted,)
+            sent, search, low, fitted, step = fuse(
+                functools.partial(next_search, number == 1), *got, search, direction, image, norm, length, noise_var, ridge, *held, *x
             )
             steps.append(step)
         (sent,) = fuse(functools.partial(over_core, IMAGE_KIND[number], 3 if number else 2, traits, rows), sent, swap(sent, 1))
         back = swap(sent, 2)
         if number == ITERS - 1:
-            sent, image, norm, length, beta = fuse(last_sums, sent, back, mask, low, direction, image, norm, length, before)
+            sent, before, image, norm, length, beta = fuse(
+                last_sums, sent, back, mask, low, direction, image, norm, length, fitted, *partial
+            )
             betas.append(beta)
             break
         state = (direction, image, norm, length) if number else ()
@@ -405,17 +416,13 @@
         if number:
             betas.append(beta)
         got = over_z(sent, 1)
-        spread = share(low) + (share(partial_res) if number == 0 else [])
-        got, spread = lax.optimization_barrier((got, spread))
-        if number == 0:
-            before = jnp.concatenate(spread[QUAD:], axis=1)
-        early += spread[:QUAD]
+        early += share(low)
 
     late = share(low)
     got = over_z(sent, 4)
     coef_new, residual_new, sigma2_new = finish(
         block_index,
-        valid_counts,
+        present,
         got,
         norm,
         length,

time: 116 us -> 123 us (1.060)
  waiting for transfers between devices: 41.9 us -> 59.3 us
  local copies, waits for them, and re-layouts: 8.34 us -> 1 us
  starting transfers between devices: 51.3 us -> 49 us
    ppermute x44, waiting for transfers between devices: 41.9 us -> 59.3 us  [swap(): return lax.ppermute(x, 'ppl', [(i, i ^ distance) for i in range(count)])]
    unnamed x22 -> x4, local copies, waits for them, and re-layouts: 7.36 us -> 0.02 us
    ppermute x44, starting transfers between devices: 51.3 us -> 49 us  [swap(): return lax.ppermute(x, 'ppl', [(i, i ^ distance) for i in range(count)])]
  transfers between devices with their start and end apart: 44 -> 44, of which waited for: 18 -> 23; matrix products, arithmetic and copies ran while one was open for 1% -> 1% of each run, Pallas kernels for 2% -> 0%
where the time goes in v6:
time: 123 us
  waiting for transfers between devices  59.3 us (48%)
  starting transfers between devices  49 us (40%)
  Pallas kernels  11.7 us (10%)
  between operations  1.42 us (1%)
    ppermute x44, waiting for transfers between devices, swap(): return lax.ppermute(x, 'ppl', [(i, i ^ distance) for i in range(count)])  59.3 us
    ppermute x44, starting transfers between devices, swap(): return lax.ppermute(x, 'ppl', [(i, i ^ distance) for i in range(count)])  49 us
    pallas_call x12, Pallas kernels, fuse(): pl.pallas_call(kernel, out_shape=shapes, compiler_params=PARAMS, in_specs...  6.71 us
    pallas_call x1, Pallas kernels, prepare(): pl.pallas_call(kernel, compiler_params=PARAMS, out_shape=out_shape, in_sp...  3.21 us
  transfers between devices with their start and end apart: 44, of which 23 were waited for; matrix products, arithmetic and copies ran while one was open for 1% of the time, Pallas kernels for 0%

profile of v6, /device:TPU:0, one launch (start us, length us, event | category | flops | bytes accessed | tf_op | source)
XLA Modules:
  0.0 122.5 jit_solution(8984269720592514223)
XLA Ops:
  1.3 3.2 %shard_map.121 = (bf16[256,1024]{1,0:T(8,128)(2,1)S(1)}, bf16[256,1024]{1,0:T(8,128)(2,1)S(1)}, bf16[256,1024]{1,0:T(8,128)(2,1)S(1)}, bf16[256,1024]{1,0:T(8,12...) custom-call(s32[1]{0:T(128)S(6)} %copy.13.block_ref, ...), custom_call_target="tpu_custom_call" | custom-call | tf_op jit(solution)/shard_map/pallas_call | solution.py:172
  6.2 2.9 %collective-permute-start.1 = (f32[256,128]{1,0:T(8,128)S(1)}, f32[256,128]{1,0:T(8,128)S(1)}, u32[]{:S(2)}, u32[]{:S(2)}) collective-permute-start(f32[256,128]{1,0:T(8,128)S(1)} %slice_add_fusion), channel_id=1, source_target_pairs={{0,2},{1,3},{2,0},{3,1},{4,6},{5,7},{6,4},{7,5},{8,10},{9,11},{10,... | collective-permute-start | bytes 393224 | tf_op jit(solution)/shard_map/ppermute | solution.py:353
  10.4 2.0 %collective-permute-start.6 = (bf16[128,1024]{1,0:T(8,128)(2,1)S(1)}, bf16[128,1024]{1,0:T(8,128)(2,1)S(1)}, u32[]{:S(2)}, u32[]{:S(2)}) collective-permute-start(bf16[128,1024]{1,0:T(8,128)(2,1)S(1)} %constant_dynamic-slice_fusion), channel_id=1, source_target_pairs={{0,2},{1,3},{2,0},{3,1},{4,6},{5,7},{6,4},{7,5},{8,10},{9,11},{10,... | collective-permute-start | bytes 786440 | tf_op jit(solution)/shard_map/ppermute | solution.py:353
  13.6 2.1 %collective-permute-start.2 = (f32[256,128]{1,0:T(8,128)S(1)}, f32[256,128]{1,0:T(8,128)S(1)}, u32[]{:S(2)}, u32[]{:S(2)}) collective-permute-start(f32[256,128]{1,0:T(8,128)S(1)} %fusion.refs_0_), channel_id=1, source_target_pairs={{0,4},{1,5},{2,6},{3,7},{4,0},{5,1},{6,2},{7,3},{8,12},{9,13},{10,... | collective-permute-start | bytes 393224 | tf_op jit(solution)/shard_map/ppermute | solution.py:353
  15.7 1.5 %collective-permute-start.7 = (bf16[128,1024]{1,0:T(8,128)(2,1)S(1)}, bf16[128,1024]{1,0:T(8,128)(2,1)S(1)}, u32[]{:S(2)}, u32[]{:S(2)}) collective-permute-start(bf16[128,1024]{1,0:T(8,128)(2,1)S(1)} %slice.11), channel_id=1, source_target_pairs={{0,2},{1,3},{2,0},{3,1},{4,6},{5,7},{6,4},{7,5},{8,10},{9,11},{10,... | collective-permute-start | bytes 786440 | tf_op jit(solution)/shard_map/ppermute | solution.py:353
  17.2 13.2 %collective-permute-done.6.refs_9_.refs_6_.refs_13_.refs_10_.refs_14_ = bf16[128,1024]{1,0:T(8,128)(2,1)S(1)} collective-permute-done((bf16[128,1024]{1,0:T(8,128)(2,1)S(1)}, bf16[128,1024]{1,0:T(8,128)(2,1)S(1)}, u32[]{:S(2)}, u32[]{:S(2)}) %collective-permute-start.6) | collective-permute-done | bytes 262176 | tf_op jit(solution)/shard_map/ppermute | solution.py:353
  30.4 3.1 %collective-permute-start.3 = (f32[256,128]{1,0:T(8,128)S(1)}, f32[256,128]{1,0:T(8,128)S(1)}, u32[]{:S(2)}, u32[]{:S(2)}) collective-permute-start(f32[256,128]{1,0:T(8,128)S(1)} %fusion.refs_0_), channel_id=1, source_target_pairs={{0,8},{1,9},{2,10},{3,11},{4,12},{5,13},{6,14},{7,15},{8,0},{9,1},... | collective-permute-start | bytes 393224 | tf_op jit(solution)/shard_map/ppermute | solution.py:353
  34.8 7.5 %collective-permute-done.3.refs_2_ = f32[256,128]{1,0:T(8,128)S(1)} collective-permute-done((f32[256,128]{1,0:T(8,128)S(1)}, f32[256,128]{1,0:T(8,128)S(1)}, u32[]{:S(2)}, u32[]{:S(2)}) %collective-permute-start.3) | collective-permute-done | bytes 131104 | tf_op jit(solution)/shard_map/ppermute | solution.py:353
  44.5 1.6 %collective-permute-start.10 = (f32[264,128]{1,0:T(8,128)S(1)}, f32[264,128]{1,0:T(8,128)S(1)}, u32[]{:S(2)}, u32[]{:S(2)}) collective-permute-start(f32[264,128]{1,0:T(8,128)S(1)} %shard_map.123.refs_0_), channel_id=1, source_target_pairs={{0,2},{1,3},{2,0},{3,1},{4,6},{5,7},{6,4},{7,5},{8,10},{9,11},{10,... | collective-permute-start | bytes 405512 | tf_op jit(solution)/shard_map/ppermute | solution.py:353
  46.1 4.1 %collective-permute-done.10.refs_1_ = f32[264,128]{1,0:T(8,128)S(1)} collective-permute-done((f32[264,128]{1,0:T(8,128)S(1)}, f32[264,128]{1,0:T(8,128)S(1)}, u32[]{:S(2)}, u32[]{:S(2)}) %collective-permute-start.10) | collective-permute-done | bytes 135200 | tf_op jit(solution)/shard_map/ppermute | solution.py:353
  51.2 2.4 %collective-permute-start.11 = (bf16[264,128]{1,0:T(8,128)(2,1)S(1)}, bf16[264,128]{1,0:T(8,128)(2,1)S(1)}, u32[]{:S(2)}, u32[]{:S(2)}) collective-permute-start(bf16[264,128]{1,0:T(8,128)(2,1)S(1)} %get-tuple-element.83.refs_0_), channel_id=1, source_target_pairs={{0,4},{1,5},{2,6},{3,7},{4,0},{5,1},{6,2},{7,3},{8,12},{9,13},{10,... | collective-permute-start | bytes 202760 | tf_op jit(solution)/shard_map/ppermute | solution.py:353
  53.5 1.9 %collective-permute-start.12 = (bf16[264,128]{1,0:T(8,128)(2,1)S(1)}, bf16[264,128]{1,0:T(8,128)(2,1)S(1)}, u32[]{:S(2)}, u32[]{:S(2)}) collective-permute-start(bf16[264,128]{1,0:T(8,128)(2,1)S(1)} %get-tuple-element.83.refs_0_), channel_id=1, source_target_pairs={{0,8},{1,9},{2,10},{3,11},{4,12},{5,13},{6,14},{7,15},{8,0},{9,1},... | collective-permute-start | bytes 202760 | tf_op jit(solution)/shard_map/ppermute | solution.py:353
  55.5 1.5 %collective-permute-start.13 = (bf16[264,128]{1,0:T(8,128)(2,1)S(1)}, bf16[264,128]{1,0:T(8,128)(2,1)S(1)}, u32[]{:S(2)}, u32[]{:S(2)}) collective-permute-start(bf16[264,128]{1,0:T(8,128)(2,1)S(1)} %get-tuple-element.83.refs_0_), channel_id=1, source_target_pairs={{0,12},{1,13},{2,14},{3,15},{4,8},{5,9},{6,10},{7,11},{8,4},{9,5},... | collective-permute-start | bytes 202760 | tf_op jit(solution)/shard_map/ppermute | solution.py:353
  56.9 4.9 %collective-permute-done.12.refs_2_ = bf16[264,128]{1,0:T(8,128)(2,1)S(1)} collective-permute-done((bf16[264,128]{1,0:T(8,128)(2,1)S(1)}, bf16[264,128]{1,0:T(8,128)(2,1)S(1)}, u32[]{:S(2)}, u32[]{:S(2)}) %collective-permute-start.12) | collective-permute-done | bytes 67616 | tf_op jit(solution)/shard_map/ppermute | solution.py:353
  64.2 1.6 %collective-permute-start.15 = (bf16[272,128]{1,0:T(8,128)(2,1)S(1)}, bf16[272,128]{1,0:T(8,128)(2,1)S(1)}, u32[]{:S(2)}, u32[]{:S(2)}) collective-permute-start(bf16[272,128]{1,0:T(8,128)(2,1)S(1)} %shard_map.126.refs_0_), channel_id=1, source_target_pairs={{0,2},{1,3},{2,0},{3,1},{4,6},{5,7},{6,4},{7,5},{8,10},{9,11},{10,... | collective-permute-start | bytes 208904 | tf_op jit(solution)/shard_map/ppermute | solution.py:353
  65.8 2.8 %collective-permute-done.15.refs_1_ = bf16[272,128]{1,0:T(8,128)(2,1)S(1)} collective-permute-done((bf16[272,128]{1,0:T(8,128)(2,1)S(1)}, bf16[272,128]{1,0:T(8,128)(2,1)S(1)}, u32[]{:S(2)}, u32[]{:S(2)}) %collective-permute-start.15) | collective-permute-done | bytes 69664 | tf_op jit(solution)/shard_map/ppermute | solution.py:353
  70.5 1.5 %collective-permute-start.17 = (bf16[264,128]{1,0:T(8,128)(2,1)S(1)}, bf16[264,128]{1,0:T(8,128)(2,1)S(1)}, u32[]{:S(2)}, u32[]{:S(2)}) collective-permute-start(bf16[264,128]{1,0:T(8,128)(2,1)S(1)} %get-tuple-element.91.refs_0_), channel_id=1, source_target_pairs={{0,8},{1,9},{2,10},{3,11},{4,12},{5,13},{6,14},{7,15},{8,0},{9,1},... | collective-permute-start | bytes 202760 | tf_op jit(solution)/shard_map/ppermute | solution.py:353
  72.0 1.6 %collective-permute-start.18 = (bf16[264,128]{1,0:T(8,128)(2,1)S(1)}, bf16[264,128]{1,0:T(8,128)(2,1)S(1)}, u32[]{:S(2)}, u32[]{:S(2)}) collective-permute-start(bf16[264,128]{1,0:T(8,128)(2,1)S(1)} %get-tuple-element.91.refs_0_), channel_id=1, source_target_pairs={{0,12},{1,13},{2,14},{3,15},{4,8},{5,9},{6,10},{7,11},{8,4},{9,5},... | collective-permute-start | bytes 202760 | tf_op jit(solution)/shard_map/ppermute | solution.py:353
  74.1 2.9 %collective-permute-done.17.refs_2_ = bf16[264,128]{1,0:T(8,128)(2,1)S(1)} collective-permute-done((bf16[264,128]{1,0:T(8,128)(2,1)S(1)}, bf16[264,128]{1,0:T(8,128)(2,1)S(1)}, u32[]{:S(2)}, u32[]{:S(2)}) %collective-permute-start.17) | collective-permute-done | bytes 67616 | tf_op jit(solution)/shard_map/ppermute | solution.py:353
  80.6 1.6 %collective-permute-start.20 = (bf16[272,128]{1,0:T(8,128)(2,1)S(1)}, bf16[272,128]{1,0:T(8,128)(2,1)S(1)}, u32[]{:S(2)}, u32[]{:S(2)}) collective-permute-start(bf16[272,128]{1,0:T(8,128)(2,1)S(1)} %shard_map.129.refs_0_), channel_id=1, source_target_pairs={{0,2},{1,3},{2,0},{3,1},{4,6},{5,7},{6,4},{7,5},{8,10},{9,11},{10,... | collective-permute-start | bytes 208904 | tf_op jit(solution)/shard_map/ppermute | solution.py:353
  82.1 2.8 %collective-permute-done.20.refs_1_ = bf16[272,128]{1,0:T(8,128)(2,1)S(1)} collective-permute-done((bf16[272,128]{1,0:T(8,128)(2,1)S(1)}, bf16[272,128]{1,0:T(8,128)(2,1)S(1)}, u32[]{:S(2)}, u32[]{:S(2)}) %collective-permute-start.20) | collective-permute-done | bytes 69664 | tf_op jit(solution)/shard_map/ppermute | solution.py:353
  86.5 1.7 %collective-permute-start.22 = (bf16[264,128]{1,0:T(8,128)(2,1)S(1)}, bf16[264,128]{1,0:T(8,128)(2,1)S(1)}, u32[]{:S(2)}, u32[]{:S(2)}) collective-permute-start(bf16[264,128]{1,0:T(8,128)(2,1)S(1)} %get-tuple-element.100.refs_0_), channel_id=1, source_target_pairs={{0,8},{1,9},{2,10},{3,11},{4,12},{5,13},{6,14},{7,15},{8,0},{9,1},... | collective-permute-start | bytes 202760 | tf_op jit(solution)/shard_map/ppermute | solution.py:353
  88.2 1.8 %collective-permute-start.23 = (bf16[264,128]{1,0:T(8,128)(2,1)S(1)}, bf16[264,128]{1,0:T(8,128)(2,1)S(1)}, u32[]{:S(2)}, u32[]{:S(2)}) collective-permute-start(bf16[264,128]{1,0:T(8,128)(2,1)S(1)} %get-tuple-element.100.refs_0_), channel_id=1, source_target_pairs={{0,12},{1,13},{2,14},{3,15},{4,8},{5,9},{6,10},{7,11},{8,4},{9,5},... | collective-permute-start | bytes 202760 | tf_op jit(solution)/shard_map/ppermute | solution.py:353
  90.1 3.0 %collective-permute-done.22.refs_2_ = bf16[264,128]{1,0:T(8,128)(2,1)S(1)} collective-permute-done((bf16[264,128]{1,0:T(8,128)(2,1)S(1)}, bf16[264,128]{1,0:T(8,128)(2,1)S(1)}, u32[]{:S(2)}, u32[]{:S(2)}) %collective-permute-start.22) | collective-permute-done | bytes 67616 | tf_op jit(solution)/shard_map/ppermute | solution.py:353
  96.3 1.5 %collective-permute-start.33 = (bf16[32,1024]{1,0:T(8,128)(2,1)S(1)}, bf16[32,1024]{1,0:T(8,128)(2,1)S(1)}, u32[]{:S(2)}, u32[]{:S(2)}) collective-permute-start(bf16[32,1024]{1,0:T(8,128)(2,1)S(1)} %get-tuple-element.82.refs_3_.refs_17_), channel_id=1, source_target_pairs={{0,2},{1,3},{2,0},{3,1},{4,6},{5,7},{6,4},{7,5},{8,10},{9,11},{10,... | collective-permute-start | bytes 196616 | tf_op jit(solution)/shard_map/ppermute | solution.py:353
  98.2 1.5 %collective-permute-start.27 = (f32[32,256]{1,0:T(8,128)S(1)}, f32[32,256]{1,0:T(8,128)S(1)}, u32[]{:S(2)}, u32[]{:S(2)}) collective-permute-start(f32[32,256]{1,0:T(8,128)S(1)} %get-tuple-element.110.refs_9_), channel_id=1, source_target_pairs={{0,2},{1,3},{2,0},{3,1},{4,6},{5,7},{6,4},{7,5},{8,10},{9,11},{10,... | collective-permute-start | bytes 98312 | tf_op jit(solution)/shard_map/ppermute | solution.py:353
  99.9 3.2 %collective-permute-done.27.refs_11_ = f32[32,256]{1,0:T(8,128)S(1)} collective-permute-done((f32[32,256]{1,0:T(8,128)S(1)}, f32[32,256]{1,0:T(8,128)S(1)}, u32[]{:S(2)}, u32[]{:S(2)}) %collective-permute-start.27) | collective-permute-done | bytes 32800 | tf_op jit(solution)/shard_map/ppermute | solution.py:353
  108.5 1.6 %collective-permute-done.37.refs_24_ = bf16[32,1024]{1,0:T(8,128)(2,1)S(1)} collective-permute-done((bf16[32,1024]{1,0:T(8,128)(2,1)S(1)}, bf16[32,1024]{1,0:T(8,128)(2,1)S(1)}, u32[]{:S(2)}, u32[]{:S(2)}) %collective-permute-start.37) | collective-permute-done | bytes 65568 | tf_op jit(solution)/shard_map/ppermute | solution.py:353
  113.7 1.6 %collective-permute-start.30 = (f32[8,128]{1,0:T(8,128)S(1)}, f32[8,128]{1,0:T(8,128)S(1)}, u32[]{:S(2)}, u32[]{:S(2)}) collective-permute-start(f32[8,128]{1,0:T(8,128)S(1)} %get-tuple-element.111.refs_0_), channel_id=1, source_target_pairs={{0,8},{1,9},{2,10},{3,11},{4,12},{5,13},{6,14},{7,15},{8,0},{9,1},... | collective-permute-start | bytes 12296 | tf_op jit(solution)/shard_map/ppermute | solution.py:353
  115.3 2.0 %collective-permute-start.31 = (f32[8,128]{1,0:T(8,128)S(1)}, f32[8,128]{1,0:T(8,128)S(1)}, u32[]{:S(2)}, u32[]{:S(2)}) collective-permute-start(f32[8,128]{1,0:T(8,128)S(1)} %get-tuple-element.111.refs_0_), channel_id=1, source_target_pairs={{0,12},{1,13},{2,14},{3,15},{4,8},{5,9},{6,10},{7,11},{8,4},{9,5},... | collective-permute-start | bytes 12296 | tf_op jit(solution)/shard_map/ppermute | solution.py:353
  118.2 2.5 %collective-permute-done.31.refs_3_ = f32[8,128]{1,0:T(8,128)S(1)} collective-permute-done((f32[8,128]{1,0:T(8,128)S(1)}, f32[8,128]{1,0:T(8,128)S(1)}, u32[]{:S(2)}, u32[]{:S(2)}) %collective-permute-start.31) | collective-permute-done | bytes 4128 | tf_op jit(solution)/shard_map/ppermute | solution.py:353
  120.7 1.8 %shard_map.134 = (f32[32,8192]{1,0:T(8,128)}, f32[32,256]{1,0:T(8,128)}, f32[1,32]{1,0:T(1,128)}) custom-call(s32[1]{0:T(128)S(6)} %copy.13.block_ref, f32[1,32]{1,0:T(1,128)S(1)} %get-tuple-element.64.present_ref, f32[8,128]{1,0:T(8,128)S(1)} %get-tuple-element.111.refs_0_, f32[8,128]{1,0:T(8,128)S(1)} %collective-permute-done.29.refs_1_, ...), custom_call_target="tpu_custom_call" | custom-call | tf_op jit(solution)/shard_map/pallas_call | solution.py:325
  (78 shorter events, 32.0 us)
Async XLA Ops:
  6.2 7.3 %collective-permute-start.1 = (f32[256,128]{1,0:T(8,128)S(1)}, f32[256,128]{1,0:T(8,128)S(1)}, u32[]{:S(2)}, u32[]{:S(2)}) collective-permute-start(f32[256,128]{1,0:T(8,128)S(1)} %slice_add_fusion), channel_id=1, source_target_pairs={{0,2},{1,3},{2,0},{3,1},{4,6},{5,7},{6,4},{7,5},{8,10},{9,11},{10,... | collective-permute-start | bytes 393224 | tf_op jit(solution)/shard_map/ppermute | solution.py:353
  9.2 33.2 %collective-permute-start.5 = (bf16[256,1024]{1,0:T(8,128)(2,1)S(1)}, bf16[256,1024]{1,0:T(8,128)(2,1)S(1)}, u32[]{:S(2)}, u32[]{:S(2)}) collective-permute-start(bf16[256,1024]{1,0:T(8,128)(2,1)S(1)} %get-tuple-element.77), channel_id=1, source_target_pairs={{0,1},{1,0},{2,3},{3,2},{4,5},{5,4},{6,7},{7,6},{8,9},{9,8},{10,11... | collective-permute-start | bytes 1572872 | tf_op jit(solution)/shard_map/ppermute | solution.py:353
  9.2 33.2 %collective-permute-start.8 = (bf16[256,1024]{1,0:T(8,128)(2,1)S(1)}, bf16[256,1024]{1,0:T(8,128)(2,1)S(1)}, u32[]{:S(2)}, u32[]{:S(2)}) collective-permute-start(bf16[256,1024]{1,0:T(8,128)(2,1)S(1)} %get-tuple-element.79), channel_id=1, source_target_pairs={{0,3},{1,2},{2,1},{3,0},{4,7},{5,6},{6,5},{7,4},{8,11},{9,10},{10,... | collective-permute-start | bytes 1572872 | tf_op jit(solution)/shard_map/ppermute | solution.py:353
  10.4 20.0 %collective-permute-start.6 = (bf16[128,1024]{1,0:T(8,128)(2,1)S(1)}, bf16[128,1024]{1,0:T(8,128)(2,1)S(1)}, u32[]{:S(2)}, u32[]{:S(2)}) collective-permute-start(bf16[128,1024]{1,0:T(8,128)(2,1)S(1)} %constant_dynamic-slice_fusion), channel_id=1, source_target_pairs={{0,2},{1,3},{2,0},{3,1},{4,6},{5,7},{6,4},{7,5},{8,10},{9,11},{10,... | collective-permute-start | bytes 786440 | tf_op jit(solution)/shard_map/ppermute | solution.py:353
  13.6 19.9 %collective-permute-start.2 = (f32[256,128]{1,0:T(8,128)S(1)}, f32[256,128]{1,0:T(8,128)S(1)}, u32[]{:S(2)}, u32[]{:S(2)}) collective-permute-start(f32[256,128]{1,0:T(8,128)S(1)} %fusion.refs_0_), channel_id=1, source_target_pairs={{0,4},{1,5},{2,6},{3,7},{4,0},{5,1},{6,2},{7,3},{8,12},{9,13},{10,... | collective-permute-start | bytes 393224 | tf_op jit(solution)/shard_map/ppermute | solution.py:353
  15.7 26.7 %collective-permute-start.7 = (bf16[128,1024]{1,0:T(8,128)(2,1)S(1)}, bf16[128,1024]{1,0:T(8,128)(2,1)S(1)}, u32[]{:S(2)}, u32[]{:S(2)}) collective-permute-start(bf16[128,1024]{1,0:T(8,128)(2,1)S(1)} %slice.11), channel_id=1, source_target_pairs={{0,2},{1,3},{2,0},{3,1},{4,6},{5,7},{6,4},{7,5},{8,10},{9,11},{10,... | collective-permute-start | bytes 786440 | tf_op jit(solution)/shard_map/ppermute | solution.py:353
  30.4 12.0 %collective-permute-start.3 = (f32[256,128]{1,0:T(8,128)S(1)}, f32[256,128]{1,0:T(8,128)S(1)}, u32[]{:S(2)}, u32[]{:S(2)}) collective-permute-start(f32[256,128]{1,0:T(8,128)S(1)} %fusion.refs_0_), channel_id=1, source_target_pairs={{0,8},{1,9},{2,10},{3,11},{4,12},{5,13},{6,14},{7,15},{8,0},{9,1},... | collective-permute-start | bytes 393224 | tf_op jit(solution)/shard_map/ppermute | solution.py:353
  33.5 8.9 %collective-permute-start.4 = (f32[256,128]{1,0:T(8,128)S(1)}, f32[256,128]{1,0:T(8,128)S(1)}, u32[]{:S(2)}, u32[]{:S(2)}) collective-permute-start(f32[256,128]{1,0:T(8,128)S(1)} %fusion.refs_0_), channel_id=1, source_target_pairs={{0,12},{1,13},{2,14},{3,15},{4,8},{5,9},{6,10},{7,11},{8,4},{9,5},... | collective-permute-start | bytes 393224 | tf_op jit(solution)/shard_map/ppermute | solution.py:353
  44.5 5.7 %collective-permute-start.10 = (f32[264,128]{1,0:T(8,128)S(1)}, f32[264,128]{1,0:T(8,128)S(1)}, u32[]{:S(2)}, u32[]{:S(2)}) collective-permute-start(f32[264,128]{1,0:T(8,128)S(1)} %shard_map.123.refs_0_), channel_id=1, source_target_pairs={{0,2},{1,3},{2,0},{3,1},{4,6},{5,7},{6,4},{7,5},{8,10},{9,11},{10,... | collective-permute-start | bytes 405512 | tf_op jit(solution)/shard_map/ppermute | solution.py:353
  51.2 5.8 %collective-permute-start.11 = (bf16[264,128]{1,0:T(8,128)(2,1)S(1)}, bf16[264,128]{1,0:T(8,128)(2,1)S(1)}, u32[]{:S(2)}, u32[]{:S(2)}) collective-permute-start(bf16[264,128]{1,0:T(8,128)(2,1)S(1)} %get-tuple-element.83.refs_0_), channel_id=1, source_target_pairs={{0,4},{1,5},{2,6},{3,7},{4,0},{5,1},{6,2},{7,3},{8,12},{9,13},{10,... | collective-permute-start | bytes 202760 | tf_op jit(solution)/shard_map/ppermute | solution.py:353
  53.5 8.3 %collective-permute-start.12 = (bf16[264,128]{1,0:T(8,128)(2,1)S(1)}, bf16[264,128]{1,0:T(8,128)(2,1)S(1)}, u32[]{:S(2)}, u32[]{:S(2)}) collective-permute-start(bf16[264,128]{1,0:T(8,128)(2,1)S(1)} %get-tuple-element.83.refs_0_), channel_id=1, source_target_pairs={{0,8},{1,9},{2,10},{3,11},{4,12},{5,13},{6,14},{7,15},{8,0},{9,1},... | collective-permute-start | bytes 202760 | tf_op jit(solution)/shard_map/ppermute | solution.py:353
  55.5 6.4 %collective-permute-start.13 = (bf16[264,128]{1,0:T(8,128)(2,1)S(1)}, bf16[264,128]{1,0:T(8,128)(2,1)S(1)}, u32[]{:S(2)}, u32[]{:S(2)}) collective-permute-start(bf16[264,128]{1,0:T(8,128)(2,1)S(1)} %get-tuple-element.83.refs_0_), channel_id=1, source_target_pairs={{0,12},{1,13},{2,14},{3,15},{4,8},{5,9},{6,10},{7,11},{8,4},{9,5},... | collective-permute-start | bytes 202760 | tf_op jit(solution)/shard_map/ppermute | solution.py:353
  69.2 5.0 %collective-permute-start.16 = (bf16[264,128]{1,0:T(8,128)(2,1)S(1)}, bf16[264,128]{1,0:T(8,128)(2,1)S(1)}, u32[]{:S(2)}, u32[]{:S(2)}) collective-permute-start(bf16[264,128]{1,0:T(8,128)(2,1)S(1)} %get-tuple-element.91.refs_0_), channel_id=1, source_target_pairs={{0,4},{1,5},{2,6},{3,7},{4,0},{5,1},{6,2},{7,3},{8,12},{9,13},{10,... | collective-permute-start | bytes 202760 | tf_op jit(solution)/shard_map/ppermute | solution.py:353
  70.5 6.6 %collective-permute-start.17 = (bf16[264,128]{1,0:T(8,128)(2,1)S(1)}, bf16[264,128]{1,0:T(8,128)(2,1)S(1)}, u32[]{:S(2)}, u32[]{:S(2)}) collective-permute-start(bf16[264,128]{1,0:T(8,128)(2,1)S(1)} %get-tuple-element.91.refs_0_), channel_id=1, source_target_pairs={{0,8},{1,9},{2,10},{3,11},{4,12},{5,13},{6,14},{7,15},{8,0},{9,1},... | collective-permute-start | bytes 202760 | tf_op jit(solution)/shard_map/ppermute | solution.py:353
  72.0 6.2 %collective-permute-start.18 = (bf16[264,128]{1,0:T(8,128)(2,1)S(1)}, bf16[264,128]{1,0:T(8,128)(2,1)S(1)}, u32[]{:S(2)}, u32[]{:S(2)}) collective-permute-start(bf16[264,128]{1,0:T(8,128)(2,1)S(1)} %get-tuple-element.91.refs_0_), channel_id=1, source_target_pairs={{0,12},{1,13},{2,14},{3,15},{4,8},{5,9},{6,10},{7,11},{8,4},{9,5},... | collective-permute-start | bytes 202760 | tf_op jit(solution)/shard_map/ppermute | solution.py:353
  85.6 4.6 %collective-permute-start.21 = (bf16[264,128]{1,0:T(8,128)(2,1)S(1)}, bf16[264,128]{1,0:T(8,128)(2,1)S(1)}, u32[]{:S(2)}, u32[]{:S(2)}) collective-permute-start(bf16[264,128]{1,0:T(8,128)(2,1)S(1)} %get-tuple-element.100.refs_0_), channel_id=1, source_target_pairs={{0,4},{1,5},{2,6},{3,7},{4,0},{5,1},{6,2},{7,3},{8,12},{9,13},{10,... | collective-permute-start | bytes 202760 | tf_op jit(solution)/shard_map/ppermute | solution.py:353
  86.5 6.6 %collective-permute-start.22 = (bf16[264,128]{1,0:T(8,128)(2,1)S(1)}, bf16[264,128]{1,0:T(8,128)(2,1)S(1)}, u32[]{:S(2)}, u32[]{:S(2)}) collective-permute-start(bf16[264,128]{1,0:T(8,128)(2,1)S(1)} %get-tuple-element.100.refs_0_), channel_id=1, source_target_pairs={{0,8},{1,9},{2,10},{3,11},{4,12},{5,13},{6,14},{7,15},{8,0},{9,1},... | collective-permute-start | bytes 202760 | tf_op jit(solution)/shard_map/ppermute | solution.py:353
  88.2 6.2 %collective-permute-start.23 = (bf16[264,128]{1,0:T(8,128)(2,1)S(1)}, bf16[264,128]{1,0:T(8,128)(2,1)S(1)}, u32[]{:S(2)}, u32[]{:S(2)}) collective-permute-start(bf16[264,128]{1,0:T(8,128)(2,1)S(1)} %get-tuple-element.100.refs_0_), channel_id=1, source_target_pairs={{0,12},{1,13},{2,14},{3,15},{4,8},{5,9},{6,10},{7,11},{8,4},{9,5},... | collective-permute-start | bytes 202760 | tf_op jit(solution)/shard_map/ppermute | solution.py:353
  96.3 8.5 %collective-permute-start.32 = (bf16[32,1024]{1,0:T(8,128)(2,1)S(1)}, bf16[32,1024]{1,0:T(8,128)(2,1)S(1)}, u32[]{:S(2)}, u32[]{:S(2)}) collective-permute-start(bf16[32,1024]{1,0:T(8,128)(2,1)S(1)} %get-tuple-element.82.refs_3_.refs_17_), channel_id=1, source_target_pairs={{0,1},{1,0},{2,3},{3,2},{4,5},{5,4},{6,7},{7,6},{8,9},{9,8},{10,11... | collective-permute-start | bytes 196616 | tf_op jit(solution)/shard_map/ppermute | solution.py:353
  96.3 9.1 %collective-permute-start.33 = (bf16[32,1024]{1,0:T(8,128)(2,1)S(1)}, bf16[32,1024]{1,0:T(8,128)(2,1)S(1)}, u32[]{:S(2)}, u32[]{:S(2)}) collective-permute-start(bf16[32,1024]{1,0:T(8,128)(2,1)S(1)} %get-tuple-element.82.refs_3_.refs_17_), channel_id=1, source_target_pairs={{0,2},{1,3},{2,0},{3,1},{4,6},{5,7},{6,4},{7,5},{8,10},{9,11},{10,... | collective-permute-start | bytes 196616 | tf_op jit(solution)/shard_map/ppermute | solution.py:353
  97.8 8.6 %collective-permute-start.34 = (bf16[32,1024]{1,0:T(8,128)(2,1)S(1)}, bf16[32,1024]{1,0:T(8,128)(2,1)S(1)}, u32[]{:S(2)}, u32[]{:S(2)}) collective-permute-start(bf16[32,1024]{1,0:T(8,128)(2,1)S(1)} %get-tuple-element.82.refs_3_.refs_17_), channel_id=1, source_target_pairs={{0,3},{1,2},{2,1},{3,0},{4,7},{5,6},{6,5},{7,4},{8,11},{9,10},{10,... | collective-permute-start | bytes 196616 | tf_op jit(solution)/shard_map/ppermute | solution.py:353
  98.2 5.0 %collective-permute-start.27 = (f32[32,256]{1,0:T(8,128)S(1)}, f32[32,256]{1,0:T(8,128)S(1)}, u32[]{:S(2)}, u32[]{:S(2)}) collective-permute-start(f32[32,256]{1,0:T(8,128)S(1)} %get-tuple-element.110.refs_9_), channel_id=1, source_target_pairs={{0,2},{1,3},{2,0},{3,1},{4,6},{5,7},{6,4},{7,5},{8,10},{9,11},{10,... | collective-permute-start | bytes 98312 | tf_op jit(solution)/shard_map/ppermute | solution.py:353
  104.8 7.7 %collective-permute-start.25 = (bf16[272,128]{1,0:T(8,128)(2,1)S(1)}, bf16[272,128]{1,0:T(8,128)(2,1)S(1)}, u32[]{:S(2)}, u32[]{:S(2)}) collective-permute-start(bf16[272,128]{1,0:T(8,128)(2,1)S(1)} %shard_map.132.refs_0_), channel_id=1, source_target_pairs={{0,2},{1,3},{2,0},{3,1},{4,6},{5,7},{6,4},{7,5},{8,10},{9,11},{10,... | collective-permute-start | bytes 208904 | tf_op jit(solution)/shard_map/ppermute | solution.py:353
  105.4 4.8 %collective-permute-start.37 = (bf16[32,1024]{1,0:T(8,128)(2,1)S(1)}, bf16[32,1024]{1,0:T(8,128)(2,1)S(1)}, u32[]{:S(2)}, u32[]{:S(2)}) collective-permute-start(bf16[32,1024]{1,0:T(8,128)(2,1)S(1)} %get-tuple-element.90.refs_3_.refs_21_), channel_id=1, source_target_pairs={{0,3},{1,2},{2,1},{3,0},{4,7},{5,6},{6,5},{7,4},{8,11},{9,10},{10,... | collective-permute-start | bytes 196616 | tf_op jit(solution)/shard_map/ppermute | solution.py:353
  106.4 4.7 %collective-permute-start.38 = (bf16[32,1024]{1,0:T(8,128)(2,1)S(1)}, bf16[32,1024]{1,0:T(8,128)(2,1)S(1)}, u32[]{:S(2)}, u32[]{:S(2)}) collective-permute-start(bf16[32,1024]{1,0:T(8,128)(2,1)S(1)} %get-tuple-element.99.refs_3_.refs_25_), channel_id=1, source_target_pairs={{0,1},{1,0},{2,3},{3,2},{4,5},{5,4},{6,7},{7,6},{8,9},{9,8},{10,11... | collective-permute-start | bytes 196616 | tf_op jit(solution)/shard_map/ppermute | solution.py:353
  106.9 5.9 %collective-permute-start.39 = (bf16[32,1024]{1,0:T(8,128)(2,1)S(1)}, bf16[32,1024]{1,0:T(8,128)(2,1)S(1)}, u32[]{:S(2)}, u32[]{:S(2)}) collective-permute-start(bf16[32,1024]{1,0:T(8,128)(2,1)S(1)} %get-tuple-element.99.refs_3_.refs_25_), channel_id=1, source_target_pairs={{0,2},{1,3},{2,0},{3,1},{4,6},{5,7},{6,4},{7,5},{8,10},{9,11},{10,... | collective-permute-start | bytes 196616 | tf_op jit(solution)/shard_map/ppermute | solution.py:353
  107.7 6.0 %collective-permute-start.40 = (bf16[32,1024]{1,0:T(8,128)(2,1)S(1)}, bf16[32,1024]{1,0:T(8,128)(2,1)S(1)}, u32[]{:S(2)}, u32[]{:S(2)}) collective-permute-start(bf16[32,1024]{1,0:T(8,128)(2,1)S(1)} %get-tuple-element.99.refs_3_.refs_25_), channel_id=1, source_target_pairs={{0,3},{1,2},{2,1},{3,0},{4,7},{5,6},{6,5},{7,4},{8,11},{9,10},{10,... | collective-permute-start | bytes 196616 | tf_op jit(solution)/shard_map/ppermute | solution.py:353
  110.2 5.1 %collective-permute-start.41 = (bf16[32,1024]{1,0:T(8,128)(2,1)S(1)}, bf16[32,1024]{1,0:T(8,128)(2,1)S(1)}, u32[]{:S(2)}, u32[]{:S(2)}) collective-permute-start(bf16[32,1024]{1,0:T(8,128)(2,1)S(1)} %get-tuple-element.108.refs_3_.refs_29_), channel_id=1, source_target_pairs={{0,1},{1,0},{2,3},{3,2},{4,5},{5,4},{6,7},{7,6},{8,9},{9,8},{10,11... | collective-permute-start | bytes 196616 | tf_op jit(solution)/shard_map/ppermute | solution.py:353
  111.1 6.2 %collective-permute-start.42 = (bf16[32,1024]{1,0:T(8,128)(2,1)S(1)}, bf16[32,1024]{1,0:T(8,128)(2,1)S(1)}, u32[]{:S(2)}, u32[]{:S(2)}) collective-permute-start(bf16[32,1024]{1,0:T(8,128)(2,1)S(1)} %get-tuple-element.108.refs_3_.refs_29_), channel_id=1, source_target_pairs={{0,2},{1,3},{2,0},{3,1},{4,6},{5,7},{6,4},{7,5},{8,10},{9,11},{10,... | collective-permute-start | bytes 196616 | tf_op jit(solution)/shard_map/ppermute | solution.py:353
  112.5 4.8 %collective-permute-start.43 = (bf16[32,1024]{1,0:T(8,128)(2,1)S(1)}, bf16[32,1024]{1,0:T(8,128)(2,1)S(1)}, u32[]{:S(2)}, u32[]{:S(2)}) collective-permute-start(bf16[32,1024]{1,0:T(8,128)(2,1)S(1)} %get-tuple-element.108.refs_3_.refs_29_), channel_id=1, source_target_pairs={{0,3},{1,2},{2,1},{3,0},{4,7},{5,6},{6,5},{7,4},{8,11},{9,10},{10,... | collective-permute-start | bytes 196616 | tf_op jit(solution)/shard_map/ppermute | solution.py:353
  113.7 4.5 %collective-permute-start.30 = (f32[8,128]{1,0:T(8,128)S(1)}, f32[8,128]{1,0:T(8,128)S(1)}, u32[]{:S(2)}, u32[]{:S(2)}) collective-permute-start(f32[8,128]{1,0:T(8,128)S(1)} %get-tuple-element.111.refs_0_), channel_id=1, source_target_pairs={{0,8},{1,9},{2,10},{3,11},{4,12},{5,13},{6,14},{7,15},{8,0},{9,1},... | collective-permute-start | bytes 12296 | tf_op jit(solution)/shard_map/ppermute | solution.py:353
  115.3 5.4 %collective-permute-start.31 = (f32[8,128]{1,0:T(8,128)S(1)}, f32[8,128]{1,0:T(8,128)S(1)}, u32[]{:S(2)}, u32[]{:S(2)}) collective-permute-start(f32[8,128]{1,0:T(8,128)S(1)} %get-tuple-element.111.refs_0_), channel_id=1, source_target_pairs={{0,12},{1,13},{2,14},{3,15},{4,8},{5,9},{6,10},{7,11},{8,4},{9,5},... | collective-permute-start | bytes 12296 | tf_op jit(solution)/shard_map/ppermute | solution.py:353
  (14 other events, 107.4 us)

commit v7 on v6

--- a/solution.py
+++ b/solution.py
@@ -194,21 +194,66 @@
     return pack(image, sums, F32), search, low
 
 
-def first_search(got0, got1, got2, got3, noise_coef, noise_var, ridge, *x):
+def halves(kept, back, far):
+    total = kept + back[: kept.shape[0]] + far
+    high = total.astype(BF16)
+    return high, (total - high.astype(F32)).astype(BF16)
+
+
+def first_search(got0, got1, got2, got3, noise_coef, noise_var, ridge):
     traits, quarter = noise_coef.shape
-    total, _ = unpack((got0 + got1) + (got2 + got3), traits, quarter)
-    return image_part(total / noise_var + jnp.sqrt(ridge) * noise_coef, None, x)
-
-
-def next_search(first, got0, got1, got2, got3, search, direction, image, norm, length, noise_var, ridge, *x):
-    fitted, x = (0.0, x) if first else (x[0], x[1:])
+    total = by_pairs([unpack(got, traits, quarter)[0] for got in (got0, got1, got2, got3)])
+    search = total / noise_var + jnp.sqrt(ridge) * noise_coef
+    return pack(search, [row_sum(search * search)], BF16), search
+
+
+def first_image(mask, *rest):
+    opened, x = rest[:QUAD], rest[QUAD:]
+    rows, quarter = x[0].shape
+    lines = (opened[0].shape[0] - TILE) * LANES
+    traits = lines // quarter
+    opened = [unpack(piece, traits, quarter, 1) for piece in opened]
+    norm = by_pairs([columns[0] for _, columns in opened])
+    length = by_pairs([row_sum(wide * wide) for wide, _ in opened])
+    lows = [wide.astype(BF16) for wide, _ in opened]
+    image = mask[:, :rows] * by_pairs([dot_t(low, block) for low, block in zip(lows, x)])
+    rounded = image.astype(BF16)
+    energy = row_sum(image * rounded.astype(F32))
+    parts = [dot(rounded, block) for block in x]
+    sent = jnp.concatenate([pack(parts[1], (), F32), pack(parts[3], [energy], F32)], axis=0)
+    return pack(parts[0], [energy], F32), pack(parts[2], (), F32), sent, image, norm, length, *lows
+
+
+def over_core_first(kept, given, back):
+    lines = given.shape[0]
+    energy = kept[lines:] + back[2 * lines :]
+    both = (kept[:lines] + back[:lines], given + back[lines : 2 * lines])
+    return tuple(jnp.concatenate([part, energy], axis=0) for part in both)
+
+
+def over_quad_first(traits, kept, far):
+    wide, columns = unpack(kept + far, traits, (kept.shape[0] - TILE) * LANES // traits, 1)
+    return (pack(wide, columns, PEOPLE_KIND[0]),)
+
+
+def next_search(number, got0, got1, got2, got3, search, direction, norm, length, noise_var, ridge, *rest):
     traits, quarter = search.shape
+    if number == 1:
+        rest_of, x = rest[:QUAD], rest[QUAD:]
+        search = search + by_pairs([unpack(got, traits, quarter)[0] for got in rest_of]) / noise_var
     opened = [unpack(got, traits, quarter, 1) for got in (got0, got1, got2, got3)]
     total = by_pairs([wide for wide, _ in opened])
     energy = by_pairs([columns[0] for _, columns in opened])
     step = norm / (energy / noise_var + ridge * length)
     search = search - step * (total / noise_var + ridge * direction)
-    return *image_part(search, direction, x), fitted + step * image, step
+    fitted = ()
+    if number == 2:
+        image, image_old, step_old, *x = rest
+        fitted = (step_old * image_old + step * image,)
+    if number > 2:
+        image, fitted, *x = rest
+        fitted = (fitted + step * image,)
+    return *image_part(search, direction, x), step, *fitted
 
 
 def cross(packed, way, traits, rows):
@@ -234,8 +279,6 @@
     fresh = mask * (wide + far)
     norm, low_low = columns[:2]
     wide = low.astype(F32)
-    if direction is None:
-        return fresh, wide, norm, low_low, jnp.zeros_like(norm)
     beta = norm / norm_old
     length = low_low + beta * (2.0 * columns[2] + beta * length)
     return fresh + beta * image, wide + beta * direction, norm, length, beta
@@ -245,11 +288,14 @@
     return [wide[:, slot * rows : (slot + 1) * rows] for slot in range(QUAD)]
 
 
-def people_part(kind, first, sent, back, mask, low, *rest):
-    if first:
-        state, x = new_image(2, sent, back, mask, low, None, None, None, None), rest
+def people_part(number, sent, back, mask, low, direction, norm_old, length, *rest):
+    kept = ()
+    if number == 1:
+        image, x = jnp.concatenate(rest[:QUAD], axis=1), rest[QUAD:]
+        kept = (image,)
     else:
-        state, x = new_image(3, sent, back, mask, low, *rest[:4]), rest[4:]
+        image, *x = rest
+    state = new_image(3, sent, back, mask, low, direction, image, norm_old, length)
     rounded = state[0].astype(BF16)
     rows = mask.shape[1] // QUAD
     energy = by_pairs([row_sum(part) for part in slots_of(state[0] * rounded.astype(F32), rows)])
@@ -257,7 +303,7 @@
     for block in x:
         total += dot(rounded[:, at : at + block.shape[0]], block)
         at += block.shape[0]
-    return pack(total, [energy], kind), *state
+    return pack(total, [energy], PEOPLE_KIND[number]), *state, *kept
 
 
 def last_sums(sent, back, mask, low, direction, image, norm_old, length, fitted, *partial):
@@ -373,35 +419,41 @@
             else:
                 (x,) = fuse(add, *got)
 
-    ahead = rows // 2
-    corner = (0, (place_in_quad() ^ 2) * (width // QUAD))
-    head = swap(lax.dynamic_slice(genotypes, corner, (ahead, width // QUAD)), 2)
     columns = sigma2_old[None, :], prior_prec[None, :]
     made = prepare(block_index, valid_counts, genotypes, coef_all, noise_coef, residual, noise_people, *columns)
-    x_give, (noise_quarter, partial_res, kept, given, sent, noise_var, ridge, mask, present) = made[:QUAD], made[QUAD:]
+    x_give, made = made[:QUAD], made[QUAD:]
+    noise_quarter, partial_res, kept, given, sent, noise_var, ridge, mask, present = made
     lines = kept.shape[0]
+    near = swap(x_give[1], 1)
     back = swap(sent, 1)
     given = given + back[lines:]
-    x_give = [x_give[0], x_give[1], x_give[2][ahead:], x_give[3]]
-    given, x_give = lax.optimization_barrier((given, x_give))
     far = swap(given, 2)
-    kept = kept + back[:lines] + far
-    near, across, far_x = (swap(x_give[slot], slot) for slot in (1, 2, 3))
-    x = [x_give[0], near, head, across, far_x]
-    got = over_z(kept, 0)
-    partial = share(partial_res)
-
-    steps, betas, early = [], [], []
-    for number in range(ITERS):
-        if number == 0:
-            sent, search, low = fuse(first_search, *got, noise_quarter, noise_var, ridge, *x)
-        else:
-            held = () if number == 1 else (fitted,)
-            sent, search, low, fitted, step = fuse(
-                functools.partial(next_search, number == 1), *got, search, direction, image, norm, length, noise_var, ridge, *held, *x
-            )
-            steps.append(step)
-        (sent,) = fuse(functools.partial(over_core, IMAGE_KIND[number], 3 if number else 2, traits, rows), sent, swap(sent, 1))
+    first_cut, second_cut = rows * 3 // 4, rows * 3 // 8
+    pieces = [swap(x_give[2][:first_cut], 2)]
+    high, low_part = fuse(halves, kept, back, far)
+    got = over_z(high, 0)
+    sent, search = fuse(first_search, *got, noise_quarter, noise_var, ridge)
+    spread = share(sent)
+    pieces += [swap(x_give[2][first_cut:], 2), swap(x_give[3][:second_cut], 3)]
+    rest_of = over_z(low_part, 0)
+    kept, given, sent, image, norm, length, *early = fuse(first_image, mask, *spread, *x_give)
+    direction = early[0].astype(F32)
+    kept, given = fuse(over_core_first, kept, given, swap(sent, 1))
+    (sent,) = fuse(functools.partial(over_quad_first, traits), kept, swap(given, 2))
+    got = over_z(sent, 1)
+    pieces.append(swap(x_give[3][second_cut:], 3))
+    pictures = share(image)
+    x = [x_give[0], near, *pieces]
+
+    steps, betas = [], []
+    for number in range(1, ITERS):
+        held = {1: rest_of, 2: (image, *image_old, *steps) if number == 2 else ()}.get(number) or (image, fitted)
+        sent, search, low, step, *fitted = fuse(
+            functools.partial(next_search, number), *got, search, direction, norm, length, noise_var, ridge, *held, *x
+        )
+        fitted = fitted[0] if fitted else None
+        steps.append(step)
+        (sent,) = fuse(functools.partial(over_core, IMAGE_KIND[number], 3, traits, rows), sent, swap(sent, 1))
         back = swap(sent, 2)
         if number == ITERS - 1:
             sent, before, image, norm, length, beta = fuse(
@@ -409,14 +461,14 @@
             )
             betas.append(beta)
             break
-        state = (direction, image, norm, length) if number else ()
-        sent, image, direction, norm, length, beta = fuse(
-            functools.partial(people_part, PEOPLE_KIND[number], number == 0), sent, back, mask, low, *state, *x
+        sent, image, direction, norm, length, beta, *image_old = fuse(
+            functools.partial(people_part, number), sent, back, mask, low, direction, norm, length, *(pictures if number == 1 else (image,)), *x
         )
-        if number:
-            betas.append(beta)
+        betas.append(beta)
         got = over_z(sent, 1)
         early += share(low)
+        if number == 1:
+            partial = share(partial_res)
 
     late = share(low)
     got = over_z(sent, 4)

time: 123 us -> 130 us (1.057)
  waiting for transfers between devices: 59.3 us -> 68.9 us
    ppermute x44 -> x51, waiting for transfers between devices: 59.3 us -> 68.9 us  [swap(): return lax.ppermute(x, 'ppl', [(i, i ^ distance) for i in range(count)])]
    ppermute x44 -> x51, starting transfers between devices: 49 us -> 48.2 us  [swap(): return lax.ppermute(x, 'ppl', [(i, i ^ distance) for i in range(count)])]
    pallas_call x12 -> x14, Pallas kernels: 6.71 us -> 6.56 us  [fuse(): pl.pallas_call(kernel, out_shape=shapes, compiler_params=PARAMS, in_specs...]
  transfers between devices with their start and end apart: 44 -> 51, of which waited for: 23 -> 23; matrix products, arithmetic and copies ran while one was open for 1% -> 0% of each run, Pallas kernels for 0% -> 0%
where the time goes in v7:
time: 130 us
  waiting for transfers between devices  68.9 us (53%)
  starting transfers between devices  48.2 us (37%)
  Pallas kernels  11.6 us (9%)
  between operations  1.46 us (1%)
    ppermute x51, waiting for transfers between devices, swap(): return lax.ppermute(x, 'ppl', [(i, i ^ distance) for i in range(count)])  68.9 us
    ppermute x51, starting transfers between devices, swap(): return lax.ppermute(x, 'ppl', [(i, i ^ distance) for i in range(count)])  48.2 us
    pallas_call x14, Pallas kernels, fuse(): pl.pallas_call(kernel, out_shape=shapes, compiler_params=PARAMS, in_specs...  6.56 us
    pallas_call x1, Pallas kernels, prepare(): pl.pallas_call(kernel, compiler_params=PARAMS, out_shape=out_shape, in_sp...  3.21 us
  transfers between devices with their start and end apart: 51, of which 23 were waited for; matrix products, arithmetic and copies ran while one was open for 0% of the time, Pallas kernels for 0%

profile of v7, /device:TPU:0, one launch (start us, length us, event | category | flops | bytes accessed | tf_op | source)
XLA Modules:
  0.0 130.3 jit_solution(14875915720904289149)
XLA Ops:
  1.3 3.2 %shard_map.121 = (bf16[256,1024]{1,0:T(8,128)(2,1)S(1)}, bf16[256,1024]{1,0:T(8,128)(2,1)S(1)}, bf16[256,1024]{1,0:T(8,128)(2,1)S(1)}, bf16[256,1024]{1,0:T(8,12...) custom-call(s32[1]{0:T(128)S(6)} %copy.13.block_ref, ...), custom_call_target="tpu_custom_call" | custom-call | tf_op jit(solution)/shard_map/pallas_call | solution.py:172
  6.2 2.9 %collective-permute-start.1 = (f32[256,128]{1,0:T(8,128)S(1)}, f32[256,128]{1,0:T(8,128)S(1)}, u32[]{:S(2)}, u32[]{:S(2)}) collective-permute-start(f32[256,128]{1,0:T(8,128)S(1)} %slice_add_fusion), channel_id=1, source_target_pairs={{0,2},{1,3},{2,0},{3,1},{4,6},{5,7},{6,4},{7,5},{8,10},{9,11},{10,... | collective-permute-start | bytes 393224 | tf_op jit(solution)/shard_map/ppermute | solution.py:399
  9.2 3.8 %collective-permute-done.1.refs_2_ = f32[256,128]{1,0:T(8,128)S(1)} collective-permute-done((f32[256,128]{1,0:T(8,128)S(1)}, f32[256,128]{1,0:T(8,128)S(1)}, u32[]{:S(2)}, u32[]{:S(2)}) %collective-permute-start.1) | collective-permute-done | bytes 131104 | tf_op jit(solution)/shard_map/ppermute | solution.py:399
  13.0 1.9 %collective-permute-start.2 = (bf16[256,128]{1,0:T(8,128)(2,1)S(1)}, bf16[256,128]{1,0:T(8,128)(2,1)S(1)}, u32[]{:S(2)}, u32[]{:S(2)}) collective-permute-start(bf16[256,128]{1,0:T(8,128)(2,1)S(1)} %get-tuple-element.72.refs_0_), channel_id=1, source_target_pairs={{0,4},{1,5},{2,6},{3,7},{4,0},{5,1},{6,2},{7,3},{8,12},{9,13},{10,... | collective-permute-start | bytes 196616 | tf_op jit(solution)/shard_map/ppermute | solution.py:399
  14.9 2.6 %collective-permute-start.3 = (bf16[256,128]{1,0:T(8,128)(2,1)S(1)}, bf16[256,128]{1,0:T(8,128)(2,1)S(1)}, u32[]{:S(2)}, u32[]{:S(2)}) collective-permute-start(bf16[256,128]{1,0:T(8,128)(2,1)S(1)} %get-tuple-element.72.refs_0_), channel_id=1, source_target_pairs={{0,8},{1,9},{2,10},{3,11},{4,12},{5,13},{6,14},{7,15},{8,0},{9,1},... | collective-permute-start | bytes 196616 | tf_op jit(solution)/shard_map/ppermute | solution.py:399
  17.5 4.1 %collective-permute-done.3.refs_2_ = bf16[256,128]{1,0:T(8,128)(2,1)S(1)} collective-permute-done((bf16[256,128]{1,0:T(8,128)(2,1)S(1)}, bf16[256,128]{1,0:T(8,128)(2,1)S(1)}, u32[]{:S(2)}, u32[]{:S(2)}) %collective-permute-start.3) | collective-permute-done | bytes 65568 | tf_op jit(solution)/shard_map/ppermute | solution.py:399
  21.6 1.9 %collective-permute-done.4.refs_3_ = bf16[256,128]{1,0:T(8,128)(2,1)S(1)} collective-permute-done((bf16[256,128]{1,0:T(8,128)(2,1)S(1)}, bf16[256,128]{1,0:T(8,128)(2,1)S(1)}, u32[]{:S(2)}, u32[]{:S(2)}) %collective-permute-start.4) | collective-permute-done | bytes 65568 | tf_op jit(solution)/shard_map/ppermute | solution.py:399
  23.8 1.6 %collective-permute-start.6 = (bf16[264,128]{1,0:T(8,128)(2,1)S(1)}, bf16[264,128]{1,0:T(8,128)(2,1)S(1)}, u32[]{:S(2)}, u32[]{:S(2)}) collective-permute-start(bf16[264,128]{1,0:T(8,128)(2,1)S(1)} %get-tuple-element.76.refs_1_), channel_id=1, source_target_pairs={{0,2},{1,3},{2,0},{3,1},{4,6},{5,7},{6,4},{7,5},{8,10},{9,11},{10,... | collective-permute-start | bytes 202760 | tf_op jit(solution)/shard_map/ppermute | solution.py:399
  25.6 2.7 %collective-permute-done.6.refs_3_ = bf16[264,128]{1,0:T(8,128)(2,1)S(1)} collective-permute-done((bf16[264,128]{1,0:T(8,128)(2,1)S(1)}, bf16[264,128]{1,0:T(8,128)(2,1)S(1)}, u32[]{:S(2)}, u32[]{:S(2)}) %collective-permute-start.6) | collective-permute-done | bytes 67616 | tf_op jit(solution)/shard_map/ppermute | solution.py:399
  29.5 1.6 %shard_map.124 = (f32[264,128]{1,0:T(8,128)S(1)}, f32[256,128]{1,0:T(8,128)S(1)}, f32[520,128]{1,0:T(8,128)S(1)}, f32[32,256]{1,0:T(8,128)S(1)}, f32[32,1]{1,0:T...) custom-call(f32[1,1024]{1,0:T(1,128)S(1)} %get-tuple-element.68.refs, ...), custom_call_target="tpu_custom_call" | custom-call | tf_op jit(solution)/shard_map/pallas_call | solution.py:97
  31.6 1.3 %collective-permute-start.17 = (bf16[192,1024]{1,0:T(8,128)(2,1)S(1)}, bf16[192,1024]{1,0:T(8,128)(2,1)S(1)}, u32[]{:S(2)}, u32[]{:S(2)}) collective-permute-start(bf16[192,1024]{1,0:T(8,128)(2,1)S(1)} %slice.16), channel_id=1, source_target_pairs={{0,2},{1,3},{2,0},{3,1},{4,6},{5,7},{6,4},{7,5},{8,10},{9,11},{10,... | collective-permute-start | bytes 1179656 | tf_op jit(solution)/shard_map/ppermute | solution.py:399
  35.8 10.7 %collective-permute-done.18.refs_17_.refs_14_.refs_16_.refs_11_.refs_15_ = bf16[64,1024]{1,0:T(8,128)(2,1)S(1)} collective-permute-done((bf16[64,1024]{1,0:T(8,128)(2,1)S(1)}, bf16[64,1024]{1,0:T(8,128)(2,1)S(1)}, u32[]{:S(2)}, u32[]{:S(2)}) %collective-permute-start.18) | collective-permute-done | bytes 131104 | tf_op jit(solution)/shard_map/ppermute | solution.py:399
  47.8 8.8 %collective-permute-done.19.refs_18_.refs_15_.refs_17_.refs_12_.refs_16_ = bf16[96,1024]{1,0:T(8,128)(2,1)S(1)} collective-permute-done((bf16[96,1024]{1,0:T(8,128)(2,1)S(1)}, bf16[96,1024]{1,0:T(8,128)(2,1)S(1)}, u32[]{:S(2)}, u32[]{:S(2)}) %collective-permute-start.19) | collective-permute-done | bytes 196640 | tf_op jit(solution)/shard_map/ppermute | solution.py:399
  56.5 3.3 %collective-permute-done.9.refs_1_ = f32[264,128]{1,0:T(8,128)S(1)} collective-permute-done((f32[264,128]{1,0:T(8,128)S(1)}, f32[264,128]{1,0:T(8,128)S(1)}, u32[]{:S(2)}, u32[]{:S(2)}) %collective-permute-start.9) | collective-permute-done | bytes 135200 | tf_op jit(solution)/shard_map/ppermute | solution.py:399
  63.0 2.4 %collective-permute-start.12 = (bf16[264,128]{1,0:T(8,128)(2,1)S(1)}, bf16[264,128]{1,0:T(8,128)(2,1)S(1)}, u32[]{:S(2)}, u32[]{:S(2)}) collective-permute-start(bf16[264,128]{1,0:T(8,128)(2,1)S(1)} %shard_map.126.refs_0_), channel_id=1, source_target_pairs={{0,12},{1,13},{2,14},{3,15},{4,8},{5,9},{6,10},{7,11},{8,4},{9,5},... | collective-permute-start | bytes 202760 | tf_op jit(solution)/shard_map/ppermute | solution.py:399
  66.8 6.0 %collective-permute-done.15.refs_13_ = bf16[256,128]{1,0:T(8,128)(2,1)S(1)} collective-permute-done((bf16[256,128]{1,0:T(8,128)(2,1)S(1)}, bf16[256,128]{1,0:T(8,128)(2,1)S(1)}, u32[]{:S(2)}, u32[]{:S(2)}) %collective-permute-start.15) | collective-permute-done | bytes 65568 | tf_op jit(solution)/shard_map/ppermute | solution.py:399
  73.8 1.3 %collective-permute-done.21.refs_1_ = f32[264,128]{1,0:T(8,128)S(1)} collective-permute-done((f32[264,128]{1,0:T(8,128)S(1)}, f32[264,128]{1,0:T(8,128)S(1)}, u32[]{:S(2)}, u32[]{:S(2)}) %collective-permute-start.21) | collective-permute-done | bytes 135200 | tf_op jit(solution)/shard_map/ppermute | solution.py:399
  78.5 2.2 %collective-permute-done.24.refs_9_ = f32[32,256]{1,0:T(8,128)S(1)} collective-permute-done((f32[32,256]{1,0:T(8,128)S(1)}, f32[32,256]{1,0:T(8,128)S(1)}, u32[]{:S(2)}, u32[]{:S(2)}) %collective-permute-start.24) | collective-permute-done | bytes 32800 | tf_op jit(solution)/shard_map/ppermute | solution.py:399
  81.6 1.5 %collective-permute-start.26 = (bf16[264,128]{1,0:T(8,128)(2,1)S(1)}, bf16[264,128]{1,0:T(8,128)(2,1)S(1)}, u32[]{:S(2)}, u32[]{:S(2)}) collective-permute-start(bf16[264,128]{1,0:T(8,128)(2,1)S(1)} %get-tuple-element.94.refs_0_), channel_id=1, source_target_pairs={{0,4},{1,5},{2,6},{3,7},{4,0},{5,1},{6,2},{7,3},{8,12},{9,13},{10,... | collective-permute-start | bytes 202760 | tf_op jit(solution)/shard_map/ppermute | solution.py:399
  83.6 2.5 %collective-permute-start.28 = (bf16[264,128]{1,0:T(8,128)(2,1)S(1)}, bf16[264,128]{1,0:T(8,128)(2,1)S(1)}, u32[]{:S(2)}, u32[]{:S(2)}) collective-permute-start(bf16[264,128]{1,0:T(8,128)(2,1)S(1)} %get-tuple-element.94.refs_0_), channel_id=1, source_target_pairs={{0,12},{1,13},{2,14},{3,15},{4,8},{5,9},{6,10},{7,11},{8,4},{9,5},... | collective-permute-start | bytes 202760 | tf_op jit(solution)/shard_map/ppermute | solution.py:399
  86.1 5.3 %collective-permute-done.27.refs_2_ = bf16[264,128]{1,0:T(8,128)(2,1)S(1)} collective-permute-done((bf16[264,128]{1,0:T(8,128)(2,1)S(1)}, bf16[264,128]{1,0:T(8,128)(2,1)S(1)}, u32[]{:S(2)}, u32[]{:S(2)}) %collective-permute-start.27) | collective-permute-done | bytes 67616 | tf_op jit(solution)/shard_map/ppermute | solution.py:399
  92.3 1.3 %collective-permute-done.29.refs_1_ = f32[264,128]{1,0:T(8,128)S(1)} collective-permute-done((f32[264,128]{1,0:T(8,128)S(1)}, f32[264,128]{1,0:T(8,128)S(1)}, u32[]{:S(2)}, u32[]{:S(2)}) %collective-permute-start.29) | collective-permute-done | bytes 135200 | tf_op jit(solution)/shard_map/ppermute | solution.py:399
  95.0 3.2 %collective-permute-done.30.refs_1_ = bf16[272,128]{1,0:T(8,128)(2,1)S(1)} collective-permute-done((bf16[272,128]{1,0:T(8,128)(2,1)S(1)}, bf16[272,128]{1,0:T(8,128)(2,1)S(1)}, u32[]{:S(2)}, u32[]{:S(2)}) %collective-permute-start.30) | collective-permute-done | bytes 69664 | tf_op jit(solution)/shard_map/ppermute | solution.py:399
  98.8 1.5 %collective-permute-start.31 = (bf16[264,128]{1,0:T(8,128)(2,1)S(1)}, bf16[264,128]{1,0:T(8,128)(2,1)S(1)}, u32[]{:S(2)}, u32[]{:S(2)}) collective-permute-start(bf16[264,128]{1,0:T(8,128)(2,1)S(1)} %get-tuple-element.104.refs_0_), channel_id=1, source_target_pairs={{0,4},{1,5},{2,6},{3,7},{4,0},{5,1},{6,2},{7,3},{8,12},{9,13},{10,... | collective-permute-start | bytes 202760 | tf_op jit(solution)/shard_map/ppermute | solution.py:399
  101.3 2.0 %collective-permute-start.33 = (bf16[264,128]{1,0:T(8,128)(2,1)S(1)}, bf16[264,128]{1,0:T(8,128)(2,1)S(1)}, u32[]{:S(2)}, u32[]{:S(2)}) collective-permute-start(bf16[264,128]{1,0:T(8,128)(2,1)S(1)} %get-tuple-element.104.refs_0_), channel_id=1, source_target_pairs={{0,12},{1,13},{2,14},{3,15},{4,8},{5,9},{6,10},{7,11},{8,4},{9,5},... | collective-permute-start | bytes 202760 | tf_op jit(solution)/shard_map/ppermute | solution.py:399
  103.2 4.3 %collective-permute-done.32.refs_2_ = bf16[264,128]{1,0:T(8,128)(2,1)S(1)} collective-permute-done((bf16[264,128]{1,0:T(8,128)(2,1)S(1)}, bf16[264,128]{1,0:T(8,128)(2,1)S(1)}, u32[]{:S(2)}, u32[]{:S(2)}) %collective-permute-start.32) | collective-permute-done | bytes 67616 | tf_op jit(solution)/shard_map/ppermute | solution.py:399
  116.2 1.7 %collective-permute-done.44.refs_24_ = bf16[32,1024]{1,0:T(8,128)(2,1)S(1)} collective-permute-done((bf16[32,1024]{1,0:T(8,128)(2,1)S(1)}, bf16[32,1024]{1,0:T(8,128)(2,1)S(1)}, u32[]{:S(2)}, u32[]{:S(2)}) %collective-permute-start.44) | collective-permute-done | bytes 65568 | tf_op jit(solution)/shard_map/ppermute | solution.py:399
  120.5 1.3 %collective-permute-start.39 = (f32[8,128]{1,0:T(8,128)S(1)}, f32[8,128]{1,0:T(8,128)S(1)}, u32[]{:S(2)}, u32[]{:S(2)}) collective-permute-start(f32[8,128]{1,0:T(8,128)S(1)} %get-tuple-element.115.refs_0_), channel_id=1, source_target_pairs={{0,4},{1,5},{2,6},{3,7},{4,0},{5,1},{6,2},{7,3},{8,12},{9,13},{10,... | collective-permute-start | bytes 12296 | tf_op jit(solution)/shard_map/ppermute | solution.py:399
  123.0 1.9 %collective-permute-start.41 = (f32[8,128]{1,0:T(8,128)S(1)}, f32[8,128]{1,0:T(8,128)S(1)}, u32[]{:S(2)}, u32[]{:S(2)}) collective-permute-start(f32[8,128]{1,0:T(8,128)S(1)} %get-tuple-element.115.refs_0_), channel_id=1, source_target_pairs={{0,12},{1,13},{2,14},{3,15},{4,8},{5,9},{6,10},{7,11},{8,4},{9,5},... | collective-permute-start | bytes 12296 | tf_op jit(solution)/shard_map/ppermute | solution.py:399
  125.0 1.4 %collective-permute-done.40.refs_2_ = f32[8,128]{1,0:T(8,128)S(1)} collective-permute-done((f32[8,128]{1,0:T(8,128)S(1)}, f32[8,128]{1,0:T(8,128)S(1)}, u32[]{:S(2)}, u32[]{:S(2)}) %collective-permute-start.40) | collective-permute-done | bytes 4128 | tf_op jit(solution)/shard_map/ppermute | solution.py:399
  126.3 2.1 %collective-permute-done.41.refs_3_ = f32[8,128]{1,0:T(8,128)S(1)} collective-permute-done((f32[8,128]{1,0:T(8,128)S(1)}, f32[8,128]{1,0:T(8,128)S(1)}, u32[]{:S(2)}, u32[]{:S(2)}) %collective-permute-start.41) | collective-permute-done | bytes 4128 | tf_op jit(solution)/shard_map/ppermute | solution.py:399
  128.4 1.8 %shard_map.136 = (f32[32,8192]{1,0:T(8,128)}, f32[32,256]{1,0:T(8,128)}, f32[1,32]{1,0:T(1,128)}) custom-call(s32[1]{0:T(128)S(6)} %copy.13.block_ref, f32[1,32]{1,0:T(1,128)S(1)} %get-tuple-element.67.present_ref, f32[8,128]{1,0:T(8,128)S(1)} %get-tuple-element.115.refs_0_, f32[8,128]{1,0:T(8,128)S(1)} %collective-permute-done.39.refs_1_, ...), custom_call_target="tpu_custom_call" | custom-call | tf_op jit(solution)/shard_map/pallas_call | solution.py:371
  (96 shorter events, 34.6 us)
Async XLA Ops:
  6.2 6.7 %collective-permute-start.1 = (f32[256,128]{1,0:T(8,128)S(1)}, f32[256,128]{1,0:T(8,128)S(1)}, u32[]{:S(2)}, u32[]{:S(2)}) collective-permute-start(f32[256,128]{1,0:T(8,128)S(1)} %slice_add_fusion), channel_id=1, source_target_pairs={{0,2},{1,3},{2,0},{3,1},{4,6},{5,7},{6,4},{7,5},{8,10},{9,11},{10,... | collective-permute-start | bytes 393224 | tf_op jit(solution)/shard_map/ppermute | solution.py:399
  14.9 6.7 %collective-permute-start.3 = (bf16[256,128]{1,0:T(8,128)(2,1)S(1)}, bf16[256,128]{1,0:T(8,128)(2,1)S(1)}, u32[]{:S(2)}, u32[]{:S(2)}) collective-permute-start(bf16[256,128]{1,0:T(8,128)(2,1)S(1)} %get-tuple-element.72.refs_0_), channel_id=1, source_target_pairs={{0,8},{1,9},{2,10},{3,11},{4,12},{5,13},{6,14},{7,15},{8,0},{9,1},... | collective-permute-start | bytes 196616 | tf_op jit(solution)/shard_map/ppermute | solution.py:399
  17.5 6.1 %collective-permute-start.4 = (bf16[256,128]{1,0:T(8,128)(2,1)S(1)}, bf16[256,128]{1,0:T(8,128)(2,1)S(1)}, u32[]{:S(2)}, u32[]{:S(2)}) collective-permute-start(bf16[256,128]{1,0:T(8,128)(2,1)S(1)} %get-tuple-element.72.refs_0_), channel_id=1, source_target_pairs={{0,12},{1,13},{2,14},{3,15},{4,8},{5,9},{6,10},{7,11},{8,4},{9,5},... | collective-permute-start | bytes 196616 | tf_op jit(solution)/shard_map/ppermute | solution.py:399
  23.8 4.5 %collective-permute-start.6 = (bf16[264,128]{1,0:T(8,128)(2,1)S(1)}, bf16[264,128]{1,0:T(8,128)(2,1)S(1)}, u32[]{:S(2)}, u32[]{:S(2)}) collective-permute-start(bf16[264,128]{1,0:T(8,128)(2,1)S(1)} %get-tuple-element.76.refs_1_), channel_id=1, source_target_pairs={{0,2},{1,3},{2,0},{3,1},{4,6},{5,7},{6,4},{7,5},{8,10},{9,11},{10,... | collective-permute-start | bytes 202760 | tf_op jit(solution)/shard_map/ppermute | solution.py:399
  31.2 41.6 %collective-permute-start.16 = (bf16[256,1024]{1,0:T(8,128)(2,1)S(1)}, bf16[256,1024]{1,0:T(8,128)(2,1)S(1)}, u32[]{:S(2)}, u32[]{:S(2)}) collective-permute-start(bf16[256,1024]{1,0:T(8,128)(2,1)S(1)} %get-tuple-element.78.refs_6_), channel_id=1, source_target_pairs={{0,1},{1,0},{2,3},{3,2},{4,5},{5,4},{6,7},{7,6},{8,9},{9,8},{10,11... | collective-permute-start | bytes 1572872 | tf_op jit(solution)/shard_map/ppermute | solution.py:399
  31.6 30.2 %collective-permute-start.17 = (bf16[192,1024]{1,0:T(8,128)(2,1)S(1)}, bf16[192,1024]{1,0:T(8,128)(2,1)S(1)}, u32[]{:S(2)}, u32[]{:S(2)}) collective-permute-start(bf16[192,1024]{1,0:T(8,128)(2,1)S(1)} %slice.16), channel_id=1, source_target_pairs={{0,2},{1,3},{2,0},{3,1},{4,6},{5,7},{6,4},{7,5},{8,10},{9,11},{10,... | collective-permute-start | bytes 1179656 | tf_op jit(solution)/shard_map/ppermute | solution.py:399
  33.0 13.5 %collective-permute-start.18 = (bf16[64,1024]{1,0:T(8,128)(2,1)S(1)}, bf16[64,1024]{1,0:T(8,128)(2,1)S(1)}, u32[]{:S(2)}, u32[]{:S(2)}) collective-permute-start(bf16[64,1024]{1,0:T(8,128)(2,1)S(1)} %slice.17), channel_id=1, source_target_pairs={{0,2},{1,3},{2,0},{3,1},{4,6},{5,7},{6,4},{7,5},{8,10},{9,11},{10,... | collective-permute-start | bytes 393224 | tf_op jit(solution)/shard_map/ppermute | solution.py:399
  33.8 27.1 %collective-permute-start.20 = (bf16[160,1024]{1,0:T(8,128)(2,1)S(1)}, bf16[160,1024]{1,0:T(8,128)(2,1)S(1)}, u32[]{:S(2)}, u32[]{:S(2)}) collective-permute-start(bf16[160,1024]{1,0:T(8,128)(2,1)S(1)} %slice.19), channel_id=1, source_target_pairs={{0,3},{1,2},{2,1},{3,0},{4,7},{5,6},{6,5},{7,4},{8,11},{9,10},{10,... | collective-permute-start | bytes 983048 | tf_op jit(solution)/shard_map/ppermute | solution.py:399
  34.6 21.9 %collective-permute-start.19 = (bf16[96,1024]{1,0:T(8,128)(2,1)S(1)}, bf16[96,1024]{1,0:T(8,128)(2,1)S(1)}, u32[]{:S(2)}, u32[]{:S(2)}) collective-permute-start(bf16[96,1024]{1,0:T(8,128)(2,1)S(1)} %slice.18), channel_id=1, source_target_pairs={{0,3},{1,2},{2,1},{3,0},{4,7},{5,6},{6,5},{7,4},{8,11},{9,10},{10,... | collective-permute-start | bytes 589832 | tf_op jit(solution)/shard_map/ppermute | solution.py:399
  46.5 13.3 %collective-permute-start.9 = (f32[264,128]{1,0:T(8,128)S(1)}, f32[264,128]{1,0:T(8,128)S(1)}, u32[]{:S(2)}, u32[]{:S(2)}) collective-permute-start(f32[264,128]{1,0:T(8,128)S(1)} %get-tuple-element.85), channel_id=1, source_target_pairs={{0,2},{1,3},{2,0},{3,1},{4,6},{5,7},{6,4},{7,5},{8,10},{9,11},{10,... | collective-permute-start | bytes 405512 | tf_op jit(solution)/shard_map/ppermute | solution.py:399
  56.5 6.5 %collective-permute-start.13 = (bf16[256,128]{1,0:T(8,128)(2,1)S(1)}, bf16[256,128]{1,0:T(8,128)(2,1)S(1)}, u32[]{:S(2)}, u32[]{:S(2)}) collective-permute-start(bf16[256,128]{1,0:T(8,128)(2,1)S(1)} %get-tuple-element.90.refs_10_), channel_id=1, source_target_pairs={{0,4},{1,5},{2,6},{3,7},{4,0},{5,1},{6,2},{7,3},{8,12},{9,13},{10,... | collective-permute-start | bytes 196616 | tf_op jit(solution)/shard_map/ppermute | solution.py:399
  59.8 6.9 %collective-permute-start.14 = (bf16[256,128]{1,0:T(8,128)(2,1)S(1)}, bf16[256,128]{1,0:T(8,128)(2,1)S(1)}, u32[]{:S(2)}, u32[]{:S(2)}) collective-permute-start(bf16[256,128]{1,0:T(8,128)(2,1)S(1)} %get-tuple-element.90.refs_10_), channel_id=1, source_target_pairs={{0,8},{1,9},{2,10},{3,11},{4,12},{5,13},{6,14},{7,15},{8,0},{9,1},... | collective-permute-start | bytes 196616 | tf_op jit(solution)/shard_map/ppermute | solution.py:399
  61.0 11.9 %collective-permute-start.10 = (bf16[264,128]{1,0:T(8,128)(2,1)S(1)}, bf16[264,128]{1,0:T(8,128)(2,1)S(1)}, u32[]{:S(2)}, u32[]{:S(2)}) collective-permute-start(bf16[264,128]{1,0:T(8,128)(2,1)S(1)} %shard_map.126.refs_0_), channel_id=1, source_target_pairs={{0,4},{1,5},{2,6},{3,7},{4,0},{5,1},{6,2},{7,3},{8,12},{9,13},{10,... | collective-permute-start | bytes 202760 | tf_op jit(solution)/shard_map/ppermute | solution.py:399
  61.8 11.1 %collective-permute-start.11 = (bf16[264,128]{1,0:T(8,128)(2,1)S(1)}, bf16[264,128]{1,0:T(8,128)(2,1)S(1)}, u32[]{:S(2)}, u32[]{:S(2)}) collective-permute-start(bf16[264,128]{1,0:T(8,128)(2,1)S(1)} %shard_map.126.refs_0_), channel_id=1, source_target_pairs={{0,8},{1,9},{2,10},{3,11},{4,12},{5,13},{6,14},{7,15},{8,0},{9,1},... | collective-permute-start | bytes 202760 | tf_op jit(solution)/shard_map/ppermute | solution.py:399
  63.0 9.8 %collective-permute-start.12 = (bf16[264,128]{1,0:T(8,128)(2,1)S(1)}, bf16[264,128]{1,0:T(8,128)(2,1)S(1)}, u32[]{:S(2)}, u32[]{:S(2)}) collective-permute-start(bf16[264,128]{1,0:T(8,128)(2,1)S(1)} %shard_map.126.refs_0_), channel_id=1, source_target_pairs={{0,12},{1,13},{2,14},{3,15},{4,8},{5,9},{6,10},{7,11},{8,4},{9,5},... | collective-permute-start | bytes 202760 | tf_op jit(solution)/shard_map/ppermute | solution.py:399
  66.7 6.2 %collective-permute-start.15 = (bf16[256,128]{1,0:T(8,128)(2,1)S(1)}, bf16[256,128]{1,0:T(8,128)(2,1)S(1)}, u32[]{:S(2)}, u32[]{:S(2)}) collective-permute-start(bf16[256,128]{1,0:T(8,128)(2,1)S(1)} %get-tuple-element.90.refs_10_), channel_id=1, source_target_pairs={{0,12},{1,13},{2,14},{3,15},{4,8},{5,9},{6,10},{7,11},{8,4},{9,5},... | collective-permute-start | bytes 196616 | tf_op jit(solution)/shard_map/ppermute | solution.py:399
  75.3 5.7 %collective-permute-start.22 = (bf16[272,128]{1,0:T(8,128)(2,1)S(1)}, bf16[272,128]{1,0:T(8,128)(2,1)S(1)}, u32[]{:S(2)}, u32[]{:S(2)}) collective-permute-start(bf16[272,128]{1,0:T(8,128)(2,1)S(1)} %shard_map.128.refs_0_), channel_id=1, source_target_pairs={{0,2},{1,3},{2,0},{3,1},{4,6},{5,7},{6,4},{7,5},{8,10},{9,11},{10,... | collective-permute-start | bytes 208904 | tf_op jit(solution)/shard_map/ppermute | solution.py:399
  83.1 8.2 %collective-permute-start.27 = (bf16[264,128]{1,0:T(8,128)(2,1)S(1)}, bf16[264,128]{1,0:T(8,128)(2,1)S(1)}, u32[]{:S(2)}, u32[]{:S(2)}) collective-permute-start(bf16[264,128]{1,0:T(8,128)(2,1)S(1)} %get-tuple-element.94.refs_0_), channel_id=1, source_target_pairs={{0,8},{1,9},{2,10},{3,11},{4,12},{5,13},{6,14},{7,15},{8,0},{9,1},... | collective-permute-start | bytes 202760 | tf_op jit(solution)/shard_map/ppermute | solution.py:399
  83.6 7.7 %collective-permute-start.28 = (bf16[264,128]{1,0:T(8,128)(2,1)S(1)}, bf16[264,128]{1,0:T(8,128)(2,1)S(1)}, u32[]{:S(2)}, u32[]{:S(2)}) collective-permute-start(bf16[264,128]{1,0:T(8,128)(2,1)S(1)} %get-tuple-element.94.refs_0_), channel_id=1, source_target_pairs={{0,12},{1,13},{2,14},{3,15},{4,8},{5,9},{6,10},{7,11},{8,4},{9,5},... | collective-permute-start | bytes 202760 | tf_op jit(solution)/shard_map/ppermute | solution.py:399
  100.3 7.3 %collective-permute-start.32 = (bf16[264,128]{1,0:T(8,128)(2,1)S(1)}, bf16[264,128]{1,0:T(8,128)(2,1)S(1)}, u32[]{:S(2)}, u32[]{:S(2)}) collective-permute-start(bf16[264,128]{1,0:T(8,128)(2,1)S(1)} %get-tuple-element.104.refs_0_), channel_id=1, source_target_pairs={{0,8},{1,9},{2,10},{3,11},{4,12},{5,13},{6,14},{7,15},{8,0},{9,1},... | collective-permute-start | bytes 202760 | tf_op jit(solution)/shard_map/ppermute | solution.py:399
  101.3 6.3 %collective-permute-start.33 = (bf16[264,128]{1,0:T(8,128)(2,1)S(1)}, bf16[264,128]{1,0:T(8,128)(2,1)S(1)}, u32[]{:S(2)}, u32[]{:S(2)}) collective-permute-start(bf16[264,128]{1,0:T(8,128)(2,1)S(1)} %get-tuple-element.104.refs_0_), channel_id=1, source_target_pairs={{0,12},{1,13},{2,14},{3,15},{4,8},{5,9},{6,10},{7,11},{8,4},{9,5},... | collective-permute-start | bytes 202760 | tf_op jit(solution)/shard_map/ppermute | solution.py:399
  111.2 4.9 %collective-permute-start.43 = (bf16[32,1024]{1,0:T(8,128)(2,1)S(1)}, bf16[32,1024]{1,0:T(8,128)(2,1)S(1)}, u32[]{:S(2)}, u32[]{:S(2)}) collective-permute-start(bf16[32,1024]{1,0:T(8,128)(2,1)S(1)} %get-tuple-element.92.refs_3_.refs_21_), channel_id=1, source_target_pairs={{0,2},{1,3},{2,0},{3,1},{4,6},{5,7},{6,4},{7,5},{8,10},{9,11},{10,... | collective-permute-start | bytes 196616 | tf_op jit(solution)/shard_map/ppermute | solution.py:399
  112.5 7.1 %collective-permute-start.35 = (bf16[272,128]{1,0:T(8,128)(2,1)S(1)}, bf16[272,128]{1,0:T(8,128)(2,1)S(1)}, u32[]{:S(2)}, u32[]{:S(2)}) collective-permute-start(bf16[272,128]{1,0:T(8,128)(2,1)S(1)} %shard_map.134.refs_0_), channel_id=1, source_target_pairs={{0,2},{1,3},{2,0},{3,1},{4,6},{5,7},{6,4},{7,5},{8,10},{9,11},{10,... | collective-permute-start | bytes 208904 | tf_op jit(solution)/shard_map/ppermute | solution.py:399
  113.9 4.9 %collective-permute-start.45 = (bf16[32,1024]{1,0:T(8,128)(2,1)S(1)}, bf16[32,1024]{1,0:T(8,128)(2,1)S(1)}, u32[]{:S(2)}, u32[]{:S(2)}) collective-permute-start(bf16[32,1024]{1,0:T(8,128)(2,1)S(1)} %get-tuple-element.103.refs_3_.refs_25_), channel_id=1, source_target_pairs={{0,1},{1,0},{2,3},{3,2},{4,5},{5,4},{6,7},{7,6},{8,9},{9,8},{10,11... | collective-permute-start | bytes 196616 | tf_op jit(solution)/shard_map/ppermute | solution.py:399
  114.7 5.7 %collective-permute-start.46 = (bf16[32,1024]{1,0:T(8,128)(2,1)S(1)}, bf16[32,1024]{1,0:T(8,128)(2,1)S(1)}, u32[]{:S(2)}, u32[]{:S(2)}) collective-permute-start(bf16[32,1024]{1,0:T(8,128)(2,1)S(1)} %get-tuple-element.103.refs_3_.refs_25_), channel_id=1, source_target_pairs={{0,2},{1,3},{2,0},{3,1},{4,6},{5,7},{6,4},{7,5},{8,10},{9,11},{10,... | collective-permute-start | bytes 196616 | tf_op jit(solution)/shard_map/ppermute | solution.py:399
  116.1 5.7 %collective-permute-start.47 = (bf16[32,1024]{1,0:T(8,128)(2,1)S(1)}, bf16[32,1024]{1,0:T(8,128)(2,1)S(1)}, u32[]{:S(2)}, u32[]{:S(2)}) collective-permute-start(bf16[32,1024]{1,0:T(8,128)(2,1)S(1)} %get-tuple-element.103.refs_3_.refs_25_), channel_id=1, source_target_pairs={{0,3},{1,2},{2,1},{3,0},{4,7},{5,6},{6,5},{7,4},{8,11},{9,10},{10,... | collective-permute-start | bytes 196616 | tf_op jit(solution)/shard_map/ppermute | solution.py:399
  117.9 5.2 %collective-permute-start.48 = (bf16[32,1024]{1,0:T(8,128)(2,1)S(1)}, bf16[32,1024]{1,0:T(8,128)(2,1)S(1)}, u32[]{:S(2)}, u32[]{:S(2)}) collective-permute-start(bf16[32,1024]{1,0:T(8,128)(2,1)S(1)} %get-tuple-element.112.refs_3_.refs_29_), channel_id=1, source_target_pairs={{0,1},{1,0},{2,3},{3,2},{4,5},{5,4},{6,7},{7,6},{8,9},{9,8},{10,11... | collective-permute-start | bytes 196616 | tf_op jit(solution)/shard_map/ppermute | solution.py:399
  118.8 6.2 %collective-permute-start.49 = (bf16[32,1024]{1,0:T(8,128)(2,1)S(1)}, bf16[32,1024]{1,0:T(8,128)(2,1)S(1)}, u32[]{:S(2)}, u32[]{:S(2)}) collective-permute-start(bf16[32,1024]{1,0:T(8,128)(2,1)S(1)} %get-tuple-element.112.refs_3_.refs_29_), channel_id=1, source_target_pairs={{0,2},{1,3},{2,0},{3,1},{4,6},{5,7},{6,4},{7,5},{8,10},{9,11},{10,... | collective-permute-start | bytes 196616 | tf_op jit(solution)/shard_map/ppermute | solution.py:399
  119.6 5.4 %collective-permute-start.50 = (bf16[32,1024]{1,0:T(8,128)(2,1)S(1)}, bf16[32,1024]{1,0:T(8,128)(2,1)S(1)}, u32[]{:S(2)}, u32[]{:S(2)}) collective-permute-start(bf16[32,1024]{1,0:T(8,128)(2,1)S(1)} %get-tuple-element.112.refs_3_.refs_29_), channel_id=1, source_target_pairs={{0,3},{1,2},{2,1},{3,0},{4,7},{5,6},{6,5},{7,4},{8,11},{9,10},{10,... | collective-permute-start | bytes 196616 | tf_op jit(solution)/shard_map/ppermute | solution.py:399
  120.5 4.5 %collective-permute-start.39 = (f32[8,128]{1,0:T(8,128)S(1)}, f32[8,128]{1,0:T(8,128)S(1)}, u32[]{:S(2)}, u32[]{:S(2)}) collective-permute-start(f32[8,128]{1,0:T(8,128)S(1)} %get-tuple-element.115.refs_0_), channel_id=1, source_target_pairs={{0,4},{1,5},{2,6},{3,7},{4,0},{5,1},{6,2},{7,3},{8,12},{9,13},{10,... | collective-permute-start | bytes 12296 | tf_op jit(solution)/shard_map/ppermute | solution.py:399
  121.8 4.5 %collective-permute-start.40 = (f32[8,128]{1,0:T(8,128)S(1)}, f32[8,128]{1,0:T(8,128)S(1)}, u32[]{:S(2)}, u32[]{:S(2)}) collective-permute-start(f32[8,128]{1,0:T(8,128)S(1)} %get-tuple-element.115.refs_0_), channel_id=1, source_target_pairs={{0,8},{1,9},{2,10},{3,11},{4,12},{5,13},{6,14},{7,15},{8,0},{9,1},... | collective-permute-start | bytes 12296 | tf_op jit(solution)/shard_map/ppermute | solution.py:399
  123.0 5.4 %collective-permute-start.41 = (f32[8,128]{1,0:T(8,128)S(1)}, f32[8,128]{1,0:T(8,128)S(1)}, u32[]{:S(2)}, u32[]{:S(2)}) collective-permute-start(f32[8,128]{1,0:T(8,128)S(1)} %get-tuple-element.115.refs_0_), channel_id=1, source_target_pairs={{0,12},{1,13},{2,14},{3,15},{4,8},{5,9},{6,10},{7,11},{8,4},{9,5},... | collective-permute-start | bytes 12296 | tf_op jit(solution)/shard_map/ppermute | solution.py:399
  (21 other events, 124.0 us)
